TPU v7x, 512 devices: a whole 4x8x8 slice. The times are simulated.
512 devices in a mesh: img: 2 (over core), row: 8 (over z_lo, x), col: 32 (over z_hi, y).
Axes of the slice: x: 4, y: 8, z: 8 (z_hi: 4, z_lo: 2; z = z_hi * 2 + z_lo), core: 2. Of those that a mesh axis runs over, the one named last changes fastest.
Arguments:
- images: bfloat16 [8, 128, 512], P('img', 'row', 'col'), may hold values from -4 to 4
- filters: bfloat16 [64, 9, 9], replicated, may hold values from -0.625 to 0.625
- hidden_bias: float32 [64], replicated, may hold values from -3 to -1
- visible_unit_bias: float32 [], replicated, may hold values from -0.5 to 0.5
- unit_noise: bfloat16 [8, 128, 32768], P('img', 'row', 'col'), may hold values from 0.019897461 to 0.9765625
Outputs:
- recon: bfloat16 [8, 128, 512], P('img', 'row', 'col')
- grad_filters: float32 [64, 9, 9], replicated
- grad_hidden: float32 [64], replicated
- grad_visible: float32 [], replicated
All inputs are finite; a program needn't handle non-finite values.
Results may differ from a plain program's by a relative error of at most 0.0075.
Values may be sent and summed in bfloat16 or wider, within the bound.
No kernel may reach another device: no remote copies, remote signals or barrier semaphores. Data moves between devices by JAX's collectives and lax.ppermute only.
A program may use at most 64 MiB of HBM per device.

v0:
```python
import jax
import jax.numpy as jnp
from jax import lax
from jax.sharding import Mesh
from jax.sharding import PartitionSpec as P

BLOCK = 4
ROW = ("row_0", "row_1")
COL = ("col_0", "col_1")
IMG_ROW_COL = ("img", "row_0", "row_1", "col_0", "col_1")


relaxation_coldness = 0.5


def extended(cells, sides, width):
    for axis, dim in sides:
        count = lax.axis_size(axis)
        ends = count - 1
        head = lax.slice_in_dim(cells, 0, width, axis=dim)
        tail = lax.slice_in_dim(cells, cells.shape[dim] - width, cells.shape[dim], axis=dim)
        cells = jnp.concatenate(
            [
                lax.ppermute(tail, axis, [(i, (i + 1) % count) for i in range(ends)]),
                cells,
                lax.ppermute(head, axis, [((i + 1) % count, i) for i in range(ends)]),
            ],
            axis=dim,
        )
    return cells


def over_axes(x, axes):
    for axis in axes:
        x = lax.psum(x, axis)
    return x


def group_peak_odds(binary_hidden_outcome):
    axis_ordering = binary_hidden_outcome.shape
    lifted_power = jnp.exp(binary_hidden_outcome).reshape(
        axis_ordering[0], axis_ordering[1], axis_ordering[2] // 2, 2, axis_ordering[3] // 2, 2
    )
    denominator = 1.0 + jnp.sum(lifted_power, axis=(3, 5), keepdims=True)
    return (lifted_power / denominator).reshape(axis_ordering)


def smoothed_draw(binary_hidden_outcome, flat_random_numbers):
    random_jitter_draw = -jnp.log(-jnp.log(flat_random_numbers.astype(jnp.float32)))
    return group_peak_odds(
        (binary_hidden_outcome + random_jitter_draw) / relaxation_coldness
    ).astype(jnp.bfloat16)


def cross_correlate(source, kernels, margin):
    return lax.conv_general_dilated(
        source,
        kernels,
        (1, 1),
        ((margin, margin), (margin, margin)),
        dimension_numbers=("NCHW", "OIHW", "NCHW"),
        preferred_element_type=jnp.float32,
    )


def filter_terms(source, hidden_map):
    return lax.conv_general_dilated(
        source,
        hidden_map,
        (1, 1),
        ((0, 0), (0, 0)),
        dimension_numbers=("NCHW", "IOHW", "NCHW"),
        preferred_element_type=jnp.float32,
    )[0]


def body(images, filters, hidden_bias, visible_unit_bias, unit_noise):
    images_here, tile_rows, tile_cols = images.shape
    channels = filters.shape[0]
    margin = filters.shape[1] // 2
    kernels = filters[:, None]
    flipped = filters[None, :, ::-1, ::-1]
    bias_map = hidden_bias[None, :, None, None]
    turns = images_here // BLOCK
    image_blocks = images.reshape(turns, BLOCK, tile_rows, tile_cols)
    perturbation_tile_sequence = unit_noise.reshape(turns, BLOCK, tile_rows, tile_cols, channels)

    def one_block(totals, inputs):
        visible, local_noise = inputs
        flat_random_numbers = local_noise.transpose(0, 3, 1, 2)
        visible_wide = extended(visible, ((ROW, 1), (COL, 2)), margin)
        positive = cross_correlate(visible_wide[:, None], kernels, 0) + bias_map
        pos_prob = group_peak_odds(positive)
        sample = smoothed_draw(positive, flat_random_numbers)
        sample_wide = extended(sample, ((ROW, 2), (COL, 3)), margin)
        recon_terms = cross_correlate(sample_wide, flipped, 0)[:, 0]
        recon = (recon_terms + visible_unit_bias).astype(jnp.bfloat16)
        recon_wide = extended(recon, ((ROW, 1), (COL, 2)), margin)
        model_phase_statistics = cross_correlate(recon_wide[:, None], kernels, 0) + bias_map
        neg_prob = group_peak_odds(model_phase_statistics)
        filter_sum = filter_terms(visible_wide[None], pos_prob.astype(jnp.bfloat16)) - filter_terms(
            recon_wide[None], neg_prob.astype(jnp.bfloat16)
        )
        hidden_sum = jnp.sum(pos_prob - neg_prob, axis=(0, 2, 3))
        visible_sum = jnp.sum(visible.astype(jnp.float32) - recon.astype(jnp.float32))
        return ((totals[0] + filter_sum, totals[1] + hidden_sum, totals[2] + visible_sum), recon)

    start = (
        jnp.zeros(filters.shape, jnp.float32),
        jnp.zeros(hidden_bias.shape, jnp.float32),
        jnp.zeros((), jnp.float32),
    )
    totals, recon_blocks = lax.scan(one_block, start, (image_blocks, perturbation_tile_sequence))
    filter_all, hidden_all, observed_layer_entire = (
        over_axes(totals[0], IMG_ROW_COL),
        over_axes(totals[1], IMG_ROW_COL),
        over_axes(totals[2], IMG_ROW_COL),
    )
    scale = 1.0 / float(
        images_here
        * tile_rows
        * tile_cols
        * lax.axis_size("img")
        * lax.axis_size(ROW)
        * lax.axis_size(COL)
    )
    recon = recon_blocks.reshape(images_here, tile_rows, tile_cols)
    return (recon, filter_all * scale, hidden_all * scale, observed_layer_entire * scale)


def solution(mesh):
    split = Mesh(
        mesh.devices.reshape(mesh.shape["img"], 2, 4, 4, 8),
        ("img", "row_0", "row_1", "col_0", "col_1"),
    )
    placed = (P("img", ROW, COL), P(), P(), P(), P("img", ROW, COL))
    return jax.shard_map(
        body,
        mesh=split,
        in_specs=placed,
        out_specs=(P("img", ROW, COL), P(), P(), P()),
        check_vma=False,
    )
```

profile of v0, /device:TPU:64, one launch (start us, length us, event | category | flops | bytes accessed | tf_op | source)
XLA Modules:
  0.0 273.3 jit_solution(13001224801078418485)
XLA Ops:
  0.6 0.7 fusion.19
  1.4 3.4 %collective-permute-start = (bf16[4,4,16]{2,1,0:T(4,128)(2,1)S(1)}, bf16[4,4,16]{2,1,0:T(4,128)(2,1)S(1)}, u32[]{:S(2)}, u32[]{:S(2)}) collective-permute-start(bf16[4,4,16]{2,1,0:T(4,128)(2,1)S(1)} %get-tuple-element.72), channel_id=1, source_target_pairs={{0,32},{32,64},{64,96},{96,128},{128,160},{160,192},{192,224},{1,3... | collective-permute-start | bytes 1544 | tf_op jit(solution)/shard_map/while/body/eval_jaxpr/ppermute | solution.py:24
  4.8 4.6 %collective-permute-start.1 = (bf16[4,4,16]{2,1,0:T(4,128)(2,1)S(1)}, bf16[4,4,16]{2,1,0:T(4,128)(2,1)S(1)}, u32[]{:S(2)}, u32[]{:S(2)}) collective-permute-start(bf16[4,4,16]{2,1,0:T(4,128)(2,1)S(1)} %get-tuple-element.73), channel_id=1, source_target_pairs={{32,0},{64,32},{96,64},{128,96},{160,128},{192,160},{224,192},{33,... | collective-permute-start | bytes 1544 | tf_op jit(solution)/shard_map/while/body/eval_jaxpr/ppermute | solution.py:26
  9.3 0.0 collective-permute-done
  9.3 1.3 collective-permute-done.1
  10.6 0.7 pad_maximum_fusion.5
  11.4 0.1 fusion.17
  11.4 3.5 %collective-permute-start.2 = (bf16[4,24,4]{2,1,0:T(8,128)(2,1)S(1)}, bf16[4,24,4]{2,1,0:T(8,128)(2,1)S(1)}, u32[]{:S(2)}, u32[]{:S(2)}) collective-permute-start(bf16[4,24,4]{2,1,0:T(8,128)(2,1)S(1)} %get-tuple-element.68), channel_id=1, source_target_pairs={{0,1},{1,2},{2,3},{3,4},{4,5},{5,6},{6,7},{7,8},{8,9},{9,10},{10,1... | collective-permute-start | bytes 2312 | tf_op jit(solution)/shard_map/while/body/eval_jaxpr/ppermute | solution.py:24
  14.9 0.0 copy-start
  14.9 1.3 collective-permute-start.3
  16.2 1.0 log_negate_fusion
  17.2 0.0 copy-start.2
  17.2 0.0 copy-start.3
  17.2 0.1 reshape.61
  17.4 0.0 collective-permute-done.2
  17.4 3.3 %collective-permute-done.3 = bf16[4,24,4]{2,1,0:T(8,128)(2,1)S(1)} collective-permute-done((bf16[4,24,4]{2,1,0:T(8,128)(2,1)S(1)}, bf16[4,24,4]{2,1,0:T(8,128)(2,1)S(1)}, u32[]{:S(2)}, u32[]{:S(2)}) %collective-permute-start.3) | collective-permute-done | bytes 800 | tf_op jit(solution)/shard_map/while/body/eval_jaxpr/ppermute | solution.py:26
  20.6 0.1 pad_maximum_fusion.6
  20.8 0.3 copy.55
  21.0 0.0 copy-done.2
  21.0 4.5 %fusion.14 = (f32[4,64,16,16]{1,0,3,2:T(4,128)S(1)}, f32[4,64,16,16]{1,0,3,2:T(4,128)S(1)}, f32[4,64,16,16]{1,0,3,2:T(4,128)S(1)}) fusion(f32[4,16,16,64]{3,2,1,0:T(8,128)S(1)} %reshape.61, f32[64]{0:T(128)S(1)} %copy-done.3, bf16[4,1,24,24]{0,1,3,2:T(2,128)(2,1)S(1)} %copy.55, bf16[64,1,9,9]{0,3,2,1:T(8,128)(2,1)S(1)} %bitcast.41), kind=kOutput, calls=%fused_computation.37 | convolution fusion | flops 10813440 | bytes 1063808 | tf_op jit(solution)/shard_map/while/body/eval_jaxpr/conv_general_dilated | solution.py:56
  25.5 0.1 reduce_sum.50
  25.7 0.1 div.50
  25.8 0.1 divide_convert_fusion
  26.0 3.0 %collective-permute-start.4 = (bf16[4,64,4,16]{1,0,3,2:T(4,128)(2,1)S(1)}, bf16[4,64,4,16]{1,0,3,2:T(4,128)(2,1)S(1)}, u32[]{:S(2)}, u32[]{:S(2)}) collective-permute-start(bf16[4,64,4,16]{1,0,3,2:T(4,128)(2,1)S(1)} %get-tuple-element.64), channel_id=1, source_target_pairs={{0,32},{32,64},{64,96},{96,128},{128,160},{160,192},{192,224},{1,3... | collective-permute-start | bytes 98312 | tf_op jit(solution)/shard_map/while/body/eval_jaxpr/ppermute | solution.py:24
  29.1 5.2 %collective-permute-start.5 = (bf16[4,64,4,16]{1,0,3,2:T(4,128)(2,1)S(1)}, bf16[4,64,4,16]{1,0,3,2:T(4,128)(2,1)S(1)}, u32[]{:S(2)}, u32[]{:S(2)}) collective-permute-start(bf16[4,64,4,16]{1,0,3,2:T(4,128)(2,1)S(1)} %get-tuple-element.65), channel_id=1, source_target_pairs={{32,0},{64,32},{96,64},{128,96},{160,128},{192,160},{224,192},{33,... | collective-permute-start | bytes 98312 | tf_op jit(solution)/shard_map/while/body/eval_jaxpr/ppermute | solution.py:26
  34.2 0.3 collective-permute-done.4
  34.5 1.6 collective-permute-done.5
  36.1 0.2 pad_maximum_fusion.4
  36.3 3.5 %collective-permute-start.6 = (bf16[4,64,24,4]{1,0,3,2:T(4,128)(2,1)S(1)}, bf16[4,64,24,4]{1,0,3,2:T(4,128)(2,1)S(1)}, u32[]{:S(2)}, u32[]{:S(2)}) collective-permute-start(bf16[4,64,24,4]{1,0,3,2:T(4,128)(2,1)S(1)} %get-tuple-element.62), channel_id=1, source_target_pairs={{0,1},{1,2},{2,3},{3,4},{4,5},{5,6},{6,7},{7,8},{8,9},{9,10},{10,1... | collective-permute-start | bytes 147464 | tf_op jit(solution)/shard_map/while/body/eval_jaxpr/ppermute | solution.py:24
  39.8 1.5 collective-permute-start.7
  42.0 0.0 collective-permute-done.6
  42.0 4.7 %collective-permute-done.7 = bf16[4,64,24,4]{1,0,3,2:T(4,128)(2,1)S(1)} collective-permute-done((bf16[4,64,24,4]{1,0,3,2:T(4,128)(2,1)S(1)}, bf16[4,64,24,4]{1,0,3,2:T(4,128)(2,1)S(1)}, u32[]{:S(2)}, u32[]{:S(2)}) %collective-permute-start.7) | collective-permute-done | bytes 49184 | tf_op jit(solution)/shard_map/while/body/eval_jaxpr/ppermute | solution.py:26
  46.6 94.6 %fusion.1 = f32[4,1,16,16]{0,1,3,2:T(1,128)S(1)} fusion(bf16[4,64,24,4]{1,0,3,2:T(4,128)(2,1)S(1)} %collective-permute-done.7, bf16[4,64,4,16]{1,0,3,2:T(4,128)(2,1)S(1)} %collective-permute-done.5, bf16[4,64,16,16]{1,0,3,2:T(4,128)(2,1)S(1)} %divide_convert_fusion, bf16[4,64,4,16]{1,0,3,2:T(4,128)(2,1)S(1)} %collective-permute-done.4, ...), kind=kOutput, calls=%fused_computation.5 | convolution fusion | flops 12091392 | bytes 309376 | tf_op jit(solution)/shard_map/while/body/eval_jaxpr/conv_general_dilated | solution.py:56
  141.2 0.2 copy.59
  141.4 0.6 subtract_reduce_fusion.1
  142.1 2.2 collective-permute-start.8
  144.3 6.1 %collective-permute-start.9 = (bf16[4,4,16]{2,1,0:T(4,128)(2,1)S(1)}, bf16[4,4,16]{2,1,0:T(4,128)(2,1)S(1)}, u32[]{:S(2)}, u32[]{:S(2)}) collective-permute-start(bf16[4,4,16]{2,1,0:T(4,128)(2,1)S(1)} %get-tuple-element.71), channel_id=1, source_target_pairs={{32,0},{64,32},{96,64},{128,96},{160,128},{192,160},{224,192},{33,... | collective-permute-start | bytes 1544 | tf_op jit(solution)/shard_map/while/body/eval_jaxpr/ppermute | solution.py:26
  150.4 0.1 reduce_sum.51
  150.5 0.0 collective-permute-done.8
  150.6 1.1 collective-permute-done.9
  151.7 0.1 fusion.16
  151.8 5.1 %collective-permute-start.10 = (bf16[4,24,4]{2,1,0:T(8,128)(2,1)S(1)}, bf16[4,24,4]{2,1,0:T(8,128)(2,1)S(1)}, u32[]{:S(2)}, u32[]{:S(2)}) collective-permute-start(bf16[4,24,4]{2,1,0:T(8,128)(2,1)S(1)} %get-tuple-element.66), channel_id=1, source_target_pairs={{0,1},{1,2},{2,3},{3,4},{4,5},{5,6},{6,7},{7,8},{8,9},{9,10},{10,1... | collective-permute-start | bytes 2312 | tf_op jit(solution)/shard_map/while/body/eval_jaxpr/ppermute | solution.py:24
  156.9 1.5 collective-permute-start.11
  158.4 0.3 copy.60
  158.7 0.0 collective-permute-done.10
  158.7 3.9 %collective-permute-done.11 = bf16[4,24,4]{2,1,0:T(8,128)(2,1)S(1)} collective-permute-done((bf16[4,24,4]{2,1,0:T(8,128)(2,1)S(1)}, bf16[4,24,4]{2,1,0:T(8,128)(2,1)S(1)}, u32[]{:S(2)}, u32[]{:S(2)}) %collective-permute-start.11) | collective-permute-done | bytes 800 | tf_op jit(solution)/shard_map/while/body/eval_jaxpr/ppermute | solution.py:26
  162.6 0.0 copy-done.1
  162.6 0.1 pad_maximum_fusion.8
  162.7 0.3 copy.61
  163.0 4.2 %fusion = f32[4,64,16,16]{1,0,3,2:T(4,128)S(1)} fusion(bf16[4,1,24,24]{0,1,3,2:T(2,128)(2,1)S(1)} %copy.61, f32[64]{0:T(128)S(1)} %copy-done.3, bf16[64,1,9,9]{0,3,2,1:T(8,128)(2,1)S(1)} %bitcast.42), kind=kOutput, calls=%fused_computation.1 | convolution fusion | flops 10682368 | bytes 277376 | tf_op jit(solution)/shard_map/while/body/eval_jaxpr/conv_general_dilated | solution.py:56
  167.2 0.1 reduce_sum.52
  167.4 0.3 copy.63
  167.6 0.1 div.56
  167.7 2.3 fusion.4
  170.0 0.1 div.53
  170.1 0.5 subtract_reduce_fusion
  170.6 2.3 convolution_subtract_fusion
  172.9 4.7 %all-reduce.4 = (f32[64,9,9]{0,2,1:T(8,128)S(1)}, f32[64]{0:T(128)S(1)}, f32[]{:T(128)}) all-reduce(f32[64,9,9]{0,2,1:T(8,128)S(1)} %bitcast.36, f32[64]{0:T(128)S(1)} %get-tuple-element.58, f32[]{:T(128)} %get-tuple-element.56), channel_id=1, replica_groups=mesh['img'=2,'row_0'=2,'row_1'=4,'col_0'=4,'col_1'=8] {'img'}, use_global_device_ids=true, to_apply=%region_3.4 | all-reduce | flops 5249 | bytes 41992 | tf_op jit(solution)/shard_map/psum | solution.py:35
  177.6 8.7 %all-reduce.3 = (f32[64,9,9]{0,2,1:T(8,128)S(1)}, f32[64]{0:T(128)S(1)}, f32[]{:T(128)}) all-reduce(f32[64,9,9]{0,2,1:T(8,128)S(1)} %get-tuple-element.53, f32[64]{0:T(128)S(1)} %get-tuple-element.54, f32[]{:T(128)} %get-tuple-element.55), channel_id=1, replica_groups=mesh['img'=2,'row_0'=2,'row_1'=4,'col_0'=4,'col_1'=8] {'row_0'}, use_global_device_ids=true, to_apply=%region_4.5 | all-reduce | flops 5249 | bytes 41992 | tf_op jit(solution)/shard_map/psum | solution.py:35
  186.3 20.8 %all-reduce.2 = (f32[64,9,9]{0,2,1:T(8,128)S(1)}, f32[64]{0:T(128)S(1)}, f32[]{:T(128)}) all-reduce(f32[64,9,9]{0,2,1:T(8,128)S(1)} %get-tuple-element.50, f32[64]{0:T(128)S(1)} %get-tuple-element.51, f32[]{:T(128)} %get-tuple-element.52), channel_id=1, replica_groups=mesh['img'=2,'row_0'=2,'row_1'=4,'col_0'=4,'col_1'=8] {'row_1'}, use_global_device_ids=true, to_apply=%region_5.6 | all-reduce | flops 5249 | bytes 41992 | tf_op jit(solution)/shard_map/psum | solution.py:35
  207.1 28.1 %all-reduce.1 = (f32[64,9,9]{0,2,1:T(8,128)S(1)}, f32[64]{0:T(128)S(1)}, f32[]{:T(128)}) all-reduce(f32[64,9,9]{0,2,1:T(8,128)S(1)} %get-tuple-element.47, f32[64]{0:T(128)S(1)} %get-tuple-element.48, f32[]{:T(128)} %get-tuple-element.49), channel_id=1, replica_groups=mesh['img'=2,'row_0'=2,'row_1'=4,'col_0'=4,'col_1'=8] {'col_0'}, use_global_device_ids=true, to_apply=%region_6.7 | all-reduce | flops 5249 | bytes 41992 | tf_op jit(solution)/shard_map/psum | solution.py:35
  235.2 35.0 %all-reduce = (f32[64,9,9]{0,2,1:T(8,128)S(1)}, f32[64]{0:T(128)S(1)}, f32[]{:T(128)}) all-reduce(f32[64,9,9]{0,2,1:T(8,128)S(1)} %get-tuple-element.44, f32[64]{0:T(128)S(1)} %get-tuple-element.45, f32[]{:T(128)} %get-tuple-element.46), channel_id=1, replica_groups=mesh['img'=2,'row_0'=2,'row_1'=4,'col_0'=4,'col_1'=8] {'col_1'}, use_global_device_ids=true, to_apply=%region_7.8 | all-reduce | flops 5249 | bytes 41992 | tf_op jit(solution)/shard_map/psum | solution.py:35
  270.2 0.6 broadcast_multiply_fusion
  270.8 0.5 broadcast_multiply_fusion.1
  (11 shorter events, 0.2 us)
Async XLA Ops:
  1.4 8.0 %collective-permute-start = (bf16[4,4,16]{2,1,0:T(4,128)(2,1)S(1)}, bf16[4,4,16]{2,1,0:T(4,128)(2,1)S(1)}, u32[]{:S(2)}, u32[]{:S(2)}) collective-permute-start(bf16[4,4,16]{2,1,0:T(4,128)(2,1)S(1)} %get-tuple-element.72), channel_id=1, source_target_pairs={{0,32},{32,64},{64,96},{96,128},{128,160},{160,192},{192,224},{1,3... | collective-permute-start | bytes 1544 | tf_op jit(solution)/shard_map/while/body/eval_jaxpr/ppermute | solution.py:24
  4.8 5.9 %collective-permute-start.1 = (bf16[4,4,16]{2,1,0:T(4,128)(2,1)S(1)}, bf16[4,4,16]{2,1,0:T(4,128)(2,1)S(1)}, u32[]{:S(2)}, u32[]{:S(2)}) collective-permute-start(bf16[4,4,16]{2,1,0:T(4,128)(2,1)S(1)} %get-tuple-element.73), channel_id=1, source_target_pairs={{32,0},{64,32},{96,64},{128,96},{160,128},{192,160},{224,192},{33,... | collective-permute-start | bytes 1544 | tf_op jit(solution)/shard_map/while/body/eval_jaxpr/ppermute | solution.py:26
  11.4 5.9 %collective-permute-start.2 = (bf16[4,24,4]{2,1,0:T(8,128)(2,1)S(1)}, bf16[4,24,4]{2,1,0:T(8,128)(2,1)S(1)}, u32[]{:S(2)}, u32[]{:S(2)}) collective-permute-start(bf16[4,24,4]{2,1,0:T(8,128)(2,1)S(1)} %get-tuple-element.68), channel_id=1, source_target_pairs={{0,1},{1,2},{2,3},{3,4},{4,5},{5,6},{6,7},{7,8},{8,9},{9,10},{10,1... | collective-permute-start | bytes 2312 | tf_op jit(solution)/shard_map/while/body/eval_jaxpr/ppermute | solution.py:24
  14.9 5.7 %copy-start = (bf16[4,16,16]{2,1,0:T(8,128)(2,1)S(1)}, bf16[4,16,16]{2,1,0:T(8,128)(2,1)}, u32[]{:S(2)}) copy-start(bf16[4,16,16]{2,1,0:T(8,128)(2,1)} %param.5) | copy-start | bytes 6148
  14.9 5.7 %collective-permute-start.3 = (bf16[4,24,4]{2,1,0:T(8,128)(2,1)S(1)}, bf16[4,24,4]{2,1,0:T(8,128)(2,1)S(1)}, u32[]{:S(2)}, u32[]{:S(2)}) collective-permute-start(bf16[4,24,4]{2,1,0:T(8,128)(2,1)S(1)} %get-tuple-element.69), channel_id=1, source_target_pairs={{1,0},{2,1},{3,2},{4,3},{5,4},{6,5},{7,6},{8,7},{9,8},{10,9},{11,1... | collective-permute-start | bytes 2312 | tf_op jit(solution)/shard_map/while/body/eval_jaxpr/ppermute | solution.py:26
  17.2 3.8 %copy-start.2 = (bf16[64,9,9]{0,2,1:T(8,128)(2,1)S(1)}, bf16[64,9,9]{0,2,1:T(8,128)(2,1)}, u32[]{:S(2)}) copy-start(bf16[64,9,9]{0,2,1:T(8,128)(2,1)} %param.6) | copy-start | bytes 31108
  17.2 3.8 %copy-start.3 = (f32[64]{0:T(128)S(1)}, f32[64]{0:T(128)}, u32[]{:S(2)}) copy-start(f32[64]{0:T(128)} %param.7) | copy-start | bytes 772
  26.0 8.5 %collective-permute-start.4 = (bf16[4,64,4,16]{1,0,3,2:T(4,128)(2,1)S(1)}, bf16[4,64,4,16]{1,0,3,2:T(4,128)(2,1)S(1)}, u32[]{:S(2)}, u32[]{:S(2)}) collective-permute-start(bf16[4,64,4,16]{1,0,3,2:T(4,128)(2,1)S(1)} %get-tuple-element.64), channel_id=1, source_target_pairs={{0,32},{32,64},{64,96},{96,128},{128,160},{160,192},{192,224},{1,3... | collective-permute-start | bytes 98312 | tf_op jit(solution)/shard_map/while/body/eval_jaxpr/ppermute | solution.py:24
  29.1 7.1 %collective-permute-start.5 = (bf16[4,64,4,16]{1,0,3,2:T(4,128)(2,1)S(1)}, bf16[4,64,4,16]{1,0,3,2:T(4,128)(2,1)S(1)}, u32[]{:S(2)}, u32[]{:S(2)}) collective-permute-start(bf16[4,64,4,16]{1,0,3,2:T(4,128)(2,1)S(1)} %get-tuple-element.65), channel_id=1, source_target_pairs={{32,0},{64,32},{96,64},{128,96},{160,128},{192,160},{224,192},{33,... | collective-permute-start | bytes 98312 | tf_op jit(solution)/shard_map/while/body/eval_jaxpr/ppermute | solution.py:26
  36.3 5.7 %collective-permute-start.6 = (bf16[4,64,24,4]{1,0,3,2:T(4,128)(2,1)S(1)}, bf16[4,64,24,4]{1,0,3,2:T(4,128)(2,1)S(1)}, u32[]{:S(2)}, u32[]{:S(2)}) collective-permute-start(bf16[4,64,24,4]{1,0,3,2:T(4,128)(2,1)S(1)} %get-tuple-element.62), channel_id=1, source_target_pairs={{0,1},{1,2},{2,3},{3,4},{4,5},{5,6},{6,7},{7,8},{8,9},{9,10},{10,1... | collective-permute-start | bytes 147464 | tf_op jit(solution)/shard_map/while/body/eval_jaxpr/ppermute | solution.py:24
  39.8 6.8 %collective-permute-start.7 = (bf16[4,64,24,4]{1,0,3,2:T(4,128)(2,1)S(1)}, bf16[4,64,24,4]{1,0,3,2:T(4,128)(2,1)S(1)}, u32[]{:S(2)}, u32[]{:S(2)}) collective-permute-start(bf16[4,64,24,4]{1,0,3,2:T(4,128)(2,1)S(1)} %get-tuple-element.63), channel_id=1, source_target_pairs={{1,0},{2,1},{3,2},{4,3},{5,4},{6,5},{7,6},{8,7},{9,8},{10,9},{11,1... | collective-permute-start | bytes 147464 | tf_op jit(solution)/shard_map/while/body/eval_jaxpr/ppermute | solution.py:26
  142.1 20.6 %copy-start.1 = (bf16[4,16,16]{2,1,0:T(8,128)(2,1)}, bf16[4,16,16]{2,1,0:T(8,128)(2,1)S(1)}, u32[]{:S(2)}) copy-start(bf16[4,16,16]{2,1,0:T(8,128)(2,1)S(1)} %get-tuple-element.57) | copy-start | bytes 6148
  142.1 8.5 %collective-permute-start.8 = (bf16[4,4,16]{2,1,0:T(4,128)(2,1)S(1)}, bf16[4,4,16]{2,1,0:T(4,128)(2,1)S(1)}, u32[]{:S(2)}, u32[]{:S(2)}) collective-permute-start(bf16[4,4,16]{2,1,0:T(4,128)(2,1)S(1)} %get-tuple-element.70), channel_id=1, source_target_pairs={{0,32},{32,64},{64,96},{96,128},{128,160},{160,192},{192,224},{1,3... | collective-permute-start | bytes 1544 | tf_op jit(solution)/shard_map/while/body/eval_jaxpr/ppermute | solution.py:24
  144.3 7.4 %collective-permute-start.9 = (bf16[4,4,16]{2,1,0:T(4,128)(2,1)S(1)}, bf16[4,4,16]{2,1,0:T(4,128)(2,1)S(1)}, u32[]{:S(2)}, u32[]{:S(2)}) collective-permute-start(bf16[4,4,16]{2,1,0:T(4,128)(2,1)S(1)} %get-tuple-element.71), channel_id=1, source_target_pairs={{32,0},{64,32},{96,64},{128,96},{160,128},{192,160},{224,192},{33,... | collective-permute-start | bytes 1544 | tf_op jit(solution)/shard_map/while/body/eval_jaxpr/ppermute | solution.py:26
  151.8 6.9 %collective-permute-start.10 = (bf16[4,24,4]{2,1,0:T(8,128)(2,1)S(1)}, bf16[4,24,4]{2,1,0:T(8,128)(2,1)S(1)}, u32[]{:S(2)}, u32[]{:S(2)}) collective-permute-start(bf16[4,24,4]{2,1,0:T(8,128)(2,1)S(1)} %get-tuple-element.66), channel_id=1, source_target_pairs={{0,1},{1,2},{2,3},{3,4},{4,5},{5,6},{6,7},{7,8},{8,9},{9,10},{10,1... | collective-permute-start | bytes 2312 | tf_op jit(solution)/shard_map/while/body/eval_jaxpr/ppermute | solution.py:24
  156.9 5.7 %collective-permute-start.11 = (bf16[4,24,4]{2,1,0:T(8,128)(2,1)S(1)}, bf16[4,24,4]{2,1,0:T(8,128)(2,1)S(1)}, u32[]{:S(2)}, u32[]{:S(2)}) collective-permute-start(bf16[4,24,4]{2,1,0:T(8,128)(2,1)S(1)} %get-tuple-element.67), channel_id=1, source_target_pairs={{1,0},{2,1},{3,2},{4,3},{5,4},{6,5},{7,6},{8,7},{9,8},{10,9},{11,1... | collective-permute-start | bytes 2312 | tf_op jit(solution)/shard_map/while/body/eval_jaxpr/ppermute | solution.py:26
where the time goes:
time: 279 us; the launch traced here: 273 us
  matrix products  108 us (39%)
  blocking collectives  97.3 us (35%)
  starting transfers between devices  40.8 us (15%)
  waiting for transfers between devices  16.2 us (6%)
  other arithmetic  5.04 us (2%)
  between operations  3.58 us (1%)
    conv_general_dilated x3, matrix products, cross_correlate(): lax.conv_general_dilated(source, kernels, (1, 1), ((margin, margin), (mar...  103 us
    psum x5, blocking collectives, over_axes(): x = lax.psum(x, axis)  97.3 us
    ppermute x6, starting transfers between devices, extended(): lax.ppermute(tail, axis, [(i, (i + 1) % count) for i in range(ends)])  20.7 us
    ppermute x6, starting transfers between devices, extended(): lax.ppermute(head, axis, [((i + 1) % count, i) for i in range(ends)])  20.1 us
    ppermute x6, waiting for transfers between devices, extended(): lax.ppermute(head, axis, [((i + 1) % count, i) for i in range(ends)])  15.9 us
  transfers between devices with their start and end apart: 12, of which 7 were waited for; matrix products, arithmetic and copies ran while one was open for 1% of the time, Pallas kernels for 0%

commit v1 on v0

v1 whole, which is shorter than its diff:
```python
import jax
import jax.numpy as jnp
from jax import lax
from jax.experimental import pallas as pl
from jax.experimental.pallas import tpu as pltpu
from jax.sharding import Mesh
from jax.sharding import PartitionSpec as P

ROW = ("row_0", "row_1")
COL = ("col_0", "col_1")
LANES = 128
INTERPRET = False


def call(kernel, out_shape, scratch, name, smem=()):
    outs = out_shape if isinstance(out_shape, (list, tuple)) else (out_shape,)

    def run(*args):
        specs = [
            pl.BlockSpec(memory_space=pltpu.SMEM if at in smem else pltpu.VMEM)
            for at in range(len(args))
        ]
        return pl.pallas_call(
            kernel,
            out_shape=out_shape,
            in_specs=specs,
            out_specs=tuple(pl.BlockSpec(memory_space=pltpu.VMEM) for _ in outs),
            scratch_shapes=scratch,
            name=name,
            interpret=INTERPRET,
        )(*args)

    return run


def edges(axis, tail, head):
    count = lax.axis_size(axis)
    ends = count - 1
    return (
        lax.ppermute(tail, axis, [(i, (i + 1) % count) for i in range(ends)]),
        lax.ppermute(head, axis, [((i + 1) % count, i) for i in range(ends)]),
    )


def extended(cells, sides, width):
    for axis, dim in sides:
        size = cells.shape[dim]
        before, after = edges(
            axis,
            lax.slice_in_dim(cells, size - width, size, axis=dim),
            lax.slice_in_dim(cells, 0, width, axis=dim),
        )
        cells = jnp.concatenate([before, cells, after], axis=dim)
    return cells


def folded(cells, sides, width):
    for axis, dim in sides:
        size = cells.shape[dim]
        before, after = edges(
            axis,
            lax.slice_in_dim(cells, size - width, size, axis=dim),
            lax.slice_in_dim(cells, 0, width, axis=dim),
        )
        middle = list(cells.shape)
        middle[dim] = size - 2 * width
        cells = cells + jnp.concatenate([before, jnp.zeros(middle, cells.dtype), after], axis=dim)
    return cells


def summed(x, axes):
    count = lax.axis_size(axes)
    parts = lax.all_to_all(
        jnp.broadcast_to(x[None], (count,) + x.shape), axes, 0, 0, tiled=True
    )
    return jnp.sum(parts, axis=0)


def block_sum(x):
    x = x + pltpu.roll(x, x.shape[1] // 2, 1)
    rows = x.shape[0]
    even = lax.broadcasted_iota(jnp.int32, x.shape, 0) % 2 == 0
    return x + jnp.where(even, pltpu.roll(x, rows - 1, 0), pltpu.roll(x, 1, 0))


def body(images, filters, hidden_bias, visible_unit_bias, unit_noise):
    n_img, tile_rows, tile_cols = images.shape
    channels, side, _ = filters.shape
    margin = side // 2
    high, wide = tile_rows + 2 * margin, tile_cols + 2 * margin
    rows = n_img * tile_rows
    units = tile_cols * channels
    taps = side * wide
    chunks = units // LANES
    f32, bf16 = jnp.float32, jnp.bfloat16

    def patches(wide_ref, out_ref):
        for n in range(n_img):
            out_ref[n * tile_rows : (n + 1) * tile_rows, :] = jnp.concatenate(
                [wide_ref[n, r : r + tile_rows, :] for r in range(side)], axis=1
            )

    def prep_kernel(pair_ref, noise_ref, w_ref, t_ref, wide_ref):
        wide_ref[...] = jnp.zeros_like(wide_ref)
        for r in range(side):
            block = pair_ref[r]
            for v in range(chunks):
                wide_ref[pl.ds(r * wide + 2 * v, side + 1), pl.ds(v * LANES, LANES)] = block
        w_ref[...] = wide_ref[...].astype(bf16)
        t_ref[...] = 1.0 / jnp.log(noise_ref[...].astype(f32))

    def up_kernel(vis_ref, w_ref, t_ref, bias_ref, part_ref, prob_ref, a_ref, hid_ref, img_ref, col_ref, samp_ref):
        img_ref[...] = vis_ref[...].astype(f32)
        patches(img_ref, col_ref)
        a_ref[...] = col_ref[...].astype(bf16)
        a = a_ref[...]
        for v in range(chunks):
            at = slice(v * LANES, (v + 1) * LANES)
            act = jnp.dot(a, w_ref[:, at], preferred_element_type=f32) + bias_ref[...]
            lift = jnp.exp(act)
            prob = lift / (1.0 + block_sum(lift))
            prob_ref[:, at] = prob.astype(bf16)
            hid_ref[:, at] = jnp.sum(prob, axis=0, keepdims=True)
            cold = lift * t_ref[:, at]
            cold = cold * cold
            samp_ref[:, at] = (cold / (1.0 + block_sum(cold))).astype(bf16)
        down = lax.dot_general(
            samp_ref[...], w_ref[...], (((1,), (1,)), ((), ())), preferred_element_type=f32
        )
        part_ref[...] = jnp.zeros_like(part_ref)
        for r in range(side):
            piece = down[:, r * wide : (r + 1) * wide]
            for n in range(n_img):
                part_ref[n, r : r + tile_rows, :] += piece[n * tile_rows : (n + 1) * tile_rows]

    def down_kernel(
        edge_ref, vb_ref, tot_ref, vis_ref, w_ref, bias_ref, prob_ref, a_ref, hid_ref,
        recon_ref, pack_ref, img_ref, col_ref, a2_ref, p2_ref, g_ref, cmb_ref,
    ):
        p = lax.broadcasted_iota(jnp.int32, (n_img, high, wide), 1)
        q = lax.broadcasted_iota(jnp.int32, (n_img, high, wide), 2)
        inside = (p >= edge_ref[0]) & (p < edge_ref[1]) & (q >= edge_ref[2]) & (q < edge_ref[3])
        recon = (tot_ref[...] + vb_ref[0]).astype(bf16).astype(f32)
        recon = jnp.where(inside, recon, 0.0)
        img_ref[...] = recon
        mine = img_ref[:, margin : margin + tile_rows, margin : margin + tile_cols]
        recon_ref[...] = mine.astype(bf16)
        seen = jnp.sum(jnp.sum(vis_ref[...].astype(f32) - mine, axis=0), keepdims=True)
        patches(img_ref, col_ref)
        a2_ref[:rows, :] = a_ref[...]
        a2_ref[rows:, :] = -col_ref[...].astype(bf16)
        p2_ref[:rows, :] = prob_ref[...]
        a = col_ref[...].astype(bf16)
        hidden = jnp.zeros((1, LANES), f32)
        for v in range(chunks):
            at = slice(v * LANES, (v + 1) * LANES)
            act = jnp.dot(a, w_ref[:, at], preferred_element_type=f32) + bias_ref[...]
            lift = jnp.exp(act)
            prob = lift / (1.0 + block_sum(lift))
            p2_ref[rows:, at] = prob.astype(bf16)
            hidden = hidden + (hid_ref[:, at] - jnp.sum(prob, axis=0, keepdims=True))
        g_ref[...] = lax.dot_general(
            a2_ref[...], p2_ref[...], (((0,), (0,)), ((), ())), preferred_element_type=f32
        )
        for r in range(side):
            acc = g_ref[pl.ds(r * wide, side + 1), pl.ds(0, LANES)]
            for v in range(1, chunks):
                acc = acc + g_ref[pl.ds(r * wide + 2 * v, side + 1), pl.ds(v * LANES, LANES)]
            half = pltpu.roll(acc, channels, 1)
            cmb_ref[r * side : (r + 1) * side, :] = acc[:side] + half[1 : side + 1]
        count = side * side
        first = (count + 1) // 2
        lane = lax.broadcasted_iota(jnp.int32, (first, LANES), 1)
        lower = cmb_ref[:first, :]
        upper = pltpu.roll(cmb_ref[count - first : count, :], channels, 1)
        pack_ref[...] = jnp.zeros_like(pack_ref)
        pack_ref[:first, :] = jnp.where(lane < channels, lower, upper)
        hidden = hidden + pltpu.roll(hidden, channels, 1)
        lane = lax.broadcasted_iota(jnp.int32, (1, LANES), 1)
        pack_ref[first : first + 1, :] = jnp.where(lane < channels, hidden, seen)

    taps_first = filters.astype(f32).transpose(1, 2, 0)
    pairs = jnp.concatenate(
        [jnp.pad(taps_first, ((0, 0), (0, 1), (0, 0))), jnp.pad(taps_first, ((0, 0), (1, 0), (0, 0)))],
        axis=2,
    )
    bias = jnp.concatenate([hidden_bias, hidden_bias])[None]
    shape = jax.ShapeDtypeStruct
    w, t = call(
        prep_kernel,
        (shape((taps, units), bf16), shape((rows, units), f32)),
        [pltpu.VMEM((taps, units), f32)],
        "prep",
    )(pairs, unit_noise.reshape(rows, units))

    visible_wide = extended(images, ((ROW, 1), (COL, 2)), margin)
    part, prob, a, hid = call(
        up_kernel,
        (
            shape((n_img, high, wide), f32),
            shape((rows, units), bf16),
            shape((rows, taps), bf16),
            shape((1, units), f32),
        ),
        [
            pltpu.VMEM((n_img, high, wide), f32),
            pltpu.VMEM((rows, taps), f32),
            pltpu.VMEM((rows, units), bf16),
        ],
        "up",
    )(visible_wide, w, t, bias)

    total = folded(part, ((ROW, 1), (COL, 2)), 2 * margin)

    def limits(axis, size, extent):
        at, last = lax.axis_index(axis), lax.axis_size(axis) - 1
        return [jnp.where(at == 0, margin, 0), jnp.where(at == last, size + margin, extent)]

    bounds = jnp.stack(limits(ROW, tile_rows, high) + limits(COL, tile_cols, wide)).astype(jnp.int32)
    n_pack = -(-((side * side + 1) // 2 + 1) // 8) * 8
    recon, pack = call(
        down_kernel,
        (shape(images.shape, bf16), shape((n_pack, LANES), f32)),
        [
            pltpu.VMEM((n_img, high, wide), f32),
            pltpu.VMEM((rows, taps), f32),
            pltpu.VMEM((2 * rows, taps), bf16),
            pltpu.VMEM((2 * rows, units), bf16),
            pltpu.VMEM((taps, units), f32),
            pltpu.VMEM((side * side, LANES), f32),
        ],
        "down",
        smem=(0, 1),
    )(bounds, visible_unit_bias[None], total, images, w, bias, prob, a, hid)

    for axes in (("img", "row_1"), "col_1", ("col_0", "row_0")):
        pack = summed(pack, axes)
    scale = 1.0 / float(
        rows * tile_cols * lax.axis_size("img") * lax.axis_size(ROW) * lax.axis_size(COL)
    )
    count = side * side
    first = (count + 1) // 2
    pack = pack * scale
    grad = jnp.concatenate([pack[:first, :channels], pack[2 * first - count : first, channels:]], axis=0)
    grad = grad.T.reshape(channels, side, side)
    return (recon, grad, pack[first, :channels], pack[first, channels])


def solution(mesh):
    split = Mesh(
        mesh.devices.reshape(mesh.shape["img"], 2, 4, 4, 8),
        ("img", "row_0", "row_1", "col_0", "col_1"),
    )
    placed = (P("img", ROW, COL), P(), P(), P(), P("img", ROW, COL))
    return jax.shard_map(
        body,
        mesh=split,
        in_specs=placed,
        out_specs=(P("img", ROW, COL), P(), P(), P()),
        check_vma=False,
    )
```

time: 279 us -> 102 us (0.37)
  the two profiles are of different devices: /device:TPU:64 before, /device:TPU:2 now
where the time goes in v1:
time: 102 us; the launch traced here: 101 us
  blocking collectives  50.6 us (50%)
  starting transfers between devices  22.9 us (22%)
  waiting for transfers between devices  10.8 us (11%)
  Pallas kernels  7.06 us (7%)
  local copies, waits for them, and re-layouts  4.35 us (4%)
  other arithmetic  4.34 us (4%)
  between operations  1.46 us (1%)
    all_to_all x3, blocking collectives, summed(): lax.all_to_all(jnp.broadcast_to(x[None], (count,) + x.shape), axes, 0, 0,...  50.6 us
    ppermute x4, starting transfers between devices, edges(): lax.ppermute(tail, axis, [(i, (i + 1) % count) for i in range(ends)])  12.1 us
    ppermute x4, waiting for transfers between devices, edges(): lax.ppermute(head, axis, [((i + 1) % count, i) for i in range(ends)])  10.8 us
    ppermute x4, starting transfers between devices, edges(): lax.ppermute(head, axis, [((i + 1) % count, i) for i in range(ends)])  10.7 us
    pallas_call x3, Pallas kernels, run(): pl.pallas_call(kernel, out_shape=out_shape, in_specs=specs, out_specs=tup...  7.06 us
  transfers between devices with their start and end apart: 8, of which 3 were waited for; matrix products, arithmetic and copies ran while one was open for 3% of the time, Pallas kernels for 2%

profile of v1, /device:TPU:2, one launch (start us, length us, event | category | flops | bytes accessed | tf_op | source)
XLA Modules:
  0.0 101.4 jit_solution(3820108857856947168)
XLA Ops:
  0.6 0.7 fusion.3
  1.4 3.4 %collective-permute-start = (bf16[4,4,16]{2,1,0:T(4,128)(2,1)S(1)}, bf16[4,4,16]{2,1,0:T(4,128)(2,1)S(1)}, u32[]{:S(2)}, u32[]{:S(2)}) collective-permute-start(bf16[4,4,16]{2,1,0:T(4,128)(2,1)S(1)} %get-tuple-element.26), channel_id=1, source_target_pairs={{0,32},{32,64},{64,96},{96,128},{128,160},{160,192},{192,224},{1,3... | collective-permute-start | bytes 1544 | tf_op jit(solution)/shard_map/ppermute | solution.py:40
  4.8 5.7 %collective-permute-start.1 = (bf16[4,4,16]{2,1,0:T(4,128)(2,1)S(1)}, bf16[4,4,16]{2,1,0:T(4,128)(2,1)S(1)}, u32[]{:S(2)}, u32[]{:S(2)}) collective-permute-start(bf16[4,4,16]{2,1,0:T(4,128)(2,1)S(1)} %get-tuple-element.27), channel_id=1, source_target_pairs={{32,0},{64,32},{96,64},{128,96},{160,128},{192,160},{224,192},{33,... | collective-permute-start | bytes 1544 | tf_op jit(solution)/shard_map/ppermute | solution.py:41
  10.4 0.8 convert_bitcast_fusion
  11.2 0.0 copy-start
  11.2 0.7 select_maximum_fusion.pair_ref
  11.9 0.0 collective-permute-done
  11.9 0.0 collective-permute-done.1
  11.9 0.0 copy-done
  12.0 0.1 fusion.2
  12.1 0.0 copy-start.2
  12.1 1.9 %collective-permute-start.2 = (bf16[4,24,4]{2,1,0:T(8,128)(2,1)S(1)}, bf16[4,24,4]{2,1,0:T(8,128)(2,1)S(1)}, u32[]{:S(2)}, u32[]{:S(2)}) collective-permute-start(bf16[4,24,4]{2,1,0:T(8,128)(2,1)S(1)} %get-tuple-element.24), channel_id=1, source_target_pairs={{0,1},{1,2},{2,3},{3,4},{4,5},{5,6},{6,7},{7,8},{8,9},{9,10},{10,1... | collective-permute-start | bytes 2312 | tf_op jit(solution)/shard_map/ppermute | solution.py:40
  14.0 1.3 %collective-permute-start.3 = (bf16[4,24,4]{2,1,0:T(8,128)(2,1)S(1)}, bf16[4,24,4]{2,1,0:T(8,128)(2,1)S(1)}, u32[]{:S(2)}, u32[]{:S(2)}) collective-permute-start(bf16[4,24,4]{2,1,0:T(8,128)(2,1)S(1)} %get-tuple-element.25), channel_id=1, source_target_pairs={{1,0},{2,1},{3,2},{4,3},{5,4},{6,5},{7,6},{8,7},{9,8},{10,9},{11,1... | collective-permute-start | bytes 2312 | tf_op jit(solution)/shard_map/ppermute | solution.py:41
  15.3 0.0 copy-done.2
  15.3 0.6 maximum_bitcast_fusion.1.bias_ref
  15.9 1.9 %prep.1 = (bf16[216,1024]{1,0:T(8,128)(2,1)}, f32[64,1024]{1,0:T(8,128)}) custom-call(f32[9,10,128]{2,1,0:T(8,128)} %select_maximum_fusion.pair_ref, bf16[64,1024]{1,0:T(8,128)(2,1)} %bitcast.20), custom_call_target="tpu_custom_call" | custom-call | tf_op jit(solution)/shard_map/prep/pallas_call | solution.py:23
  17.8 0.0 collective-permute-done.2
  17.8 1.9 %collective-permute-done.3 = bf16[4,24,4]{2,1,0:T(8,128)(2,1)S(1)} collective-permute-done((bf16[4,24,4]{2,1,0:T(8,128)(2,1)S(1)}, bf16[4,24,4]{2,1,0:T(8,128)(2,1)S(1)}, u32[]{:S(2)}, u32[]{:S(2)}) %collective-permute-start.3) | collective-permute-done | bytes 800 | tf_op jit(solution)/shard_map/ppermute | solution.py:41
  19.7 0.7 pad_maximum_fusion.1.vis_ref
  20.4 2.6 %up.1 = (f32[4,24,24]{2,1,0:T(8,128)}, bf16[64,1024]{1,0:T(8,128)(2,1)}, bf16[64,216]{1,0:T(8,128)(2,1)}, f32[1,1024]{1,0:T(1,128)}) custom-call(bf16[4,24,24]{2,1,0:T(8,128)(2,1)} %pad_maximum_fusion.1.vis_ref, bf16[216,1024]{1,0:T(8,128)(2,1)} %get-tuple-element.12.w_ref, f32[64,1024]{1,0:T(8,128)} %get-tuple-element.13.t_ref, ...), custom_call_target="tpu_custom_call" | custom-call | tf_op jit(solution)/shard_map/up/pallas_call | solution.py:23
  23.0 0.0 copy-start.1
  23.0 0.8 fusion.1
  23.8 3.4 %collective-permute-start.4 = (f32[4,8,24]{2,1,0:T(8,128)S(1)}, f32[4,8,24]{2,1,0:T(8,128)S(1)}, u32[]{:S(2)}, u32[]{:S(2)}) collective-permute-start(f32[4,8,24]{2,1,0:T(8,128)S(1)} %get-tuple-element.22), channel_id=1, source_target_pairs={{0,32},{32,64},{64,96},{96,128},{128,160},{160,192},{192,224},{1,3... | collective-permute-start | bytes 9224 | tf_op jit(solution)/shard_map/ppermute | solution.py:40
  27.1 2.5 %collective-permute-start.5 = (f32[4,8,24]{2,1,0:T(8,128)S(1)}, f32[4,8,24]{2,1,0:T(8,128)S(1)}, u32[]{:S(2)}, u32[]{:S(2)}) collective-permute-start(f32[4,8,24]{2,1,0:T(8,128)S(1)} %get-tuple-element.23), channel_id=1, source_target_pairs={{32,0},{64,32},{96,64},{128,96},{160,128},{192,160},{224,192},{33,... | collective-permute-start | bytes 9224 | tf_op jit(solution)/shard_map/ppermute | solution.py:41
  29.6 0.1 pad.16.clone
  29.7 0.0 collective-permute-done.4
  29.7 5.2 %collective-permute-done.5 = f32[4,8,24]{2,1,0:T(8,128)S(1)} collective-permute-done((f32[4,8,24]{2,1,0:T(8,128)S(1)}, f32[4,8,24]{2,1,0:T(8,128)S(1)}, u32[]{:S(2)}, u32[]{:S(2)}) %collective-permute-start.5) | collective-permute-done | bytes 3104 | tf_op jit(solution)/shard_map/ppermute | solution.py:41
  34.9 0.0 copy-done.1
  34.9 0.1 maximum_add_fusion
  35.0 0.1 fusion
  35.0 3.5 %collective-permute-start.6 = (f32[4,24,8]{2,1,0:T(8,128)S(1)}, f32[4,24,8]{2,1,0:T(8,128)S(1)}, u32[]{:S(2)}, u32[]{:S(2)}) collective-permute-start(f32[4,24,8]{2,1,0:T(8,128)S(1)} %get-tuple-element.20), channel_id=1, source_target_pairs={{0,1},{1,2},{2,3},{3,4},{4,5},{5,6},{6,7},{7,8},{8,9},{9,10},{10,1... | collective-permute-start | bytes 9224 | tf_op jit(solution)/shard_map/ppermute | solution.py:40
  38.5 1.3 %collective-permute-start.7 = (f32[4,24,8]{2,1,0:T(8,128)S(1)}, f32[4,24,8]{2,1,0:T(8,128)S(1)}, u32[]{:S(2)}, u32[]{:S(2)}) collective-permute-start(f32[4,24,8]{2,1,0:T(8,128)S(1)} %get-tuple-element.21), channel_id=1, source_target_pairs={{1,0},{2,1},{3,2},{4,3},{5,4},{6,5},{7,6},{8,7},{9,8},{10,9},{11,1... | collective-permute-start | bytes 9224 | tf_op jit(solution)/shard_map/ppermute | solution.py:41
  39.8 0.7 pad_add_fusion.edge_ref
  41.1 0.0 collective-permute-done.6
  41.2 3.7 %collective-permute-done.7 = f32[4,24,8]{2,1,0:T(8,128)S(1)} collective-permute-done((f32[4,24,8]{2,1,0:T(8,128)S(1)}, f32[4,24,8]{2,1,0:T(8,128)S(1)}, u32[]{:S(2)}, u32[]{:S(2)}) %collective-permute-start.7) | collective-permute-done | bytes 3104 | tf_op jit(solution)/shard_map/ppermute | solution.py:41
  44.8 0.7 maximum_add_fusion.1.tot_ref
  45.5 2.6 %down.1 = (bf16[4,16,16]{2,1,0:T(8,128)(2,1)}, f32[48,128]{1,0:T(8,128)}) custom-call(s32[4]{0:T(128)} %pad_add_fusion.edge_ref, f32[1]{0:T(128)} %bitcast.18.vb_ref, f32[4,24,24]{2,1,0:T(8,128)} %maximum_add_fusion.1.tot_ref, bf16[4,16,16]{2,1,0:T(8,128)(2,1)} %vis_ref.1, bf16[216,1024]{1,0:T(8,128)(2,1)} %get-tuple-element.12.w_ref, ...), custom_call_target="tpu_custom_call" | custom-call | tf_op jit(solution)/shard_map/down/pallas_call | solution.py:23
  48.1 0.8 broadcast_in_dim.34
  48.9 10.9 %all_to_all.15 = f32[8,48,128]{2,1,0:T(8,128)S(1)} all-to-all(f32[8,48,128]{2,1,0:T(8,128)S(1)} %broadcast_in_dim.34), channel_id=1, replica_groups=mesh['img'=2,'row_0'=2,'row_1'=4,'col_0'=4,'col_1'=8] {'img','row_1'}, dimensions={0} | all-to-all | bytes 393216 | tf_op jit(solution)/shard_map/all_to_all | solution.py:73
  59.8 21.9 %all_to_all.16 = f32[8,48,128]{2,1,0:T(8,128)S(1)} all-to-all(f32[8,48,128]{2,1,0:T(8,128)S(1)} %broadcast_in_dim.35), channel_id=1, replica_groups=mesh['img'=2,'row_0'=2,'row_1'=4,'col_0'=4,'col_1'=8] {'col_1'}, dimensions={0} | all-to-all | bytes 393216 | tf_op jit(solution)/shard_map/all_to_all | solution.py:73
  81.8 17.8 %all_to_all.17 = f32[8,48,128]{2,1,0:T(8,128)S(1)} all-to-all(f32[8,48,128]{2,1,0:T(8,128)S(1)} %broadcast_in_dim.36), channel_id=1, replica_groups=mesh['img'=2,'row_0'=2,'row_1'=4,'col_0'=4,'col_1'=8] {'col_0','row_0'}, dimensions={0} | all-to-all | bytes 393216 | tf_op jit(solution)/shard_map/all_to_all | solution.py:73
  99.6 0.1 slice.53
  99.7 0.6 slice.55
  100.3 0.5 slice_bitcast_fusion
  100.8 0.6 reshape.18
  (9 shorter events, 0.1 us)
Async XLA Ops:
  1.4 10.6 %collective-permute-start = (bf16[4,4,16]{2,1,0:T(4,128)(2,1)S(1)}, bf16[4,4,16]{2,1,0:T(4,128)(2,1)S(1)}, u32[]{:S(2)}, u32[]{:S(2)}) collective-permute-start(bf16[4,4,16]{2,1,0:T(4,128)(2,1)S(1)} %get-tuple-element.26), channel_id=1, source_target_pairs={{0,32},{32,64},{64,96},{96,128},{128,160},{160,192},{192,224},{1,3... | collective-permute-start | bytes 1544 | tf_op jit(solution)/shard_map/ppermute | solution.py:40
  4.8 7.2 %collective-permute-start.1 = (bf16[4,4,16]{2,1,0:T(4,128)(2,1)S(1)}, bf16[4,4,16]{2,1,0:T(4,128)(2,1)S(1)}, u32[]{:S(2)}, u32[]{:S(2)}) collective-permute-start(bf16[4,4,16]{2,1,0:T(4,128)(2,1)S(1)} %get-tuple-element.27), channel_id=1, source_target_pairs={{32,0},{64,32},{96,64},{128,96},{160,128},{192,160},{224,192},{33,... | collective-permute-start | bytes 1544 | tf_op jit(solution)/shard_map/ppermute | solution.py:41
  11.2 0.7 copy-start
  12.1 3.2 %copy-start.2 = (f32[64]{0:T(128)S(1)}, f32[64]{0:T(128)}, u32[]{:S(2)}) copy-start(f32[64]{0:T(128)} %param.7) | copy-start | bytes 772
  12.1 5.7 %collective-permute-start.2 = (bf16[4,24,4]{2,1,0:T(8,128)(2,1)S(1)}, bf16[4,24,4]{2,1,0:T(8,128)(2,1)S(1)}, u32[]{:S(2)}, u32[]{:S(2)}) collective-permute-start(bf16[4,24,4]{2,1,0:T(8,128)(2,1)S(1)} %get-tuple-element.24), channel_id=1, source_target_pairs={{0,1},{1,2},{2,3},{3,4},{4,5},{5,6},{6,7},{7,8},{8,9},{9,10},{10,1... | collective-permute-start | bytes 2312 | tf_op jit(solution)/shard_map/ppermute | solution.py:40
  14.0 5.7 %collective-permute-start.3 = (bf16[4,24,4]{2,1,0:T(8,128)(2,1)S(1)}, bf16[4,24,4]{2,1,0:T(8,128)(2,1)S(1)}, u32[]{:S(2)}, u32[]{:S(2)}) collective-permute-start(bf16[4,24,4]{2,1,0:T(8,128)(2,1)S(1)} %get-tuple-element.25), channel_id=1, source_target_pairs={{1,0},{2,1},{3,2},{4,3},{5,4},{6,5},{7,6},{8,7},{9,8},{10,9},{11,1... | collective-permute-start | bytes 2312 | tf_op jit(solution)/shard_map/ppermute | solution.py:41
  23.0 11.9 %copy-start.1 = (f32[4,24,24]{2,1,0:T(8,128)S(1)}, f32[4,24,24]{2,1,0:T(8,128)}, u32[]{:S(2)}) copy-start(f32[4,24,24]{2,1,0:T(8,128)} %get-tuple-element.14) | copy-start | bytes 27652
  23.8 6.0 %collective-permute-start.4 = (f32[4,8,24]{2,1,0:T(8,128)S(1)}, f32[4,8,24]{2,1,0:T(8,128)S(1)}, u32[]{:S(2)}, u32[]{:S(2)}) collective-permute-start(f32[4,8,24]{2,1,0:T(8,128)S(1)} %get-tuple-element.22), channel_id=1, source_target_pairs={{0,32},{32,64},{64,96},{96,128},{128,160},{160,192},{192,224},{1,3... | collective-permute-start | bytes 9224 | tf_op jit(solution)/shard_map/ppermute | solution.py:40
  27.1 7.7 %collective-permute-start.5 = (f32[4,8,24]{2,1,0:T(8,128)S(1)}, f32[4,8,24]{2,1,0:T(8,128)S(1)}, u32[]{:S(2)}, u32[]{:S(2)}) collective-permute-start(f32[4,8,24]{2,1,0:T(8,128)S(1)} %get-tuple-element.23), channel_id=1, source_target_pairs={{32,0},{64,32},{96,64},{128,96},{160,128},{192,160},{224,192},{33,... | collective-permute-start | bytes 9224 | tf_op jit(solution)/shard_map/ppermute | solution.py:41
  35.0 6.1 %collective-permute-start.6 = (f32[4,24,8]{2,1,0:T(8,128)S(1)}, f32[4,24,8]{2,1,0:T(8,128)S(1)}, u32[]{:S(2)}, u32[]{:S(2)}) collective-permute-start(f32[4,24,8]{2,1,0:T(8,128)S(1)} %get-tuple-element.20), channel_id=1, source_target_pairs={{0,1},{1,2},{2,3},{3,4},{4,5},{5,6},{6,7},{7,8},{8,9},{9,10},{10,1... | collective-permute-start | bytes 9224 | tf_op jit(solution)/shard_map/ppermute | solution.py:40
  38.5 6.3 %collective-permute-start.7 = (f32[4,24,8]{2,1,0:T(8,128)S(1)}, f32[4,24,8]{2,1,0:T(8,128)S(1)}, u32[]{:S(2)}, u32[]{:S(2)}) collective-permute-start(f32[4,24,8]{2,1,0:T(8,128)S(1)} %get-tuple-element.21), channel_id=1, source_target_pairs={{1,0},{2,1},{3,2},{4,3},{5,4},{6,5},{7,6},{8,7},{9,8},{10,9},{11,1... | collective-permute-start | bytes 9224 | tf_op jit(solution)/shard_map/ppermute | solution.py:41

commit v2 on v1

v2 whole, which is shorter than its diff:
```python
import jax
import jax.numpy as jnp
from jax import lax
from jax.experimental import pallas as pl
from jax.experimental.pallas import tpu as pltpu
from jax.sharding import Mesh
from jax.sharding import PartitionSpec as P

ROW = ("row_0", "row_1")
COL = ("col_0", "col_1")
LANES = 128
INTERPRET = False
GRANT = 8 << 20


def call(kernel, out_shape, scratch, name, smem=()):
    outs = out_shape if isinstance(out_shape, (list, tuple)) else (out_shape,)

    def run(*args):
        specs = [
            pl.BlockSpec(memory_space=pltpu.SMEM if at in smem else pltpu.VMEM)
            for at in range(len(args))
        ]
        return pl.pallas_call(
            kernel,
            out_shape=out_shape,
            in_specs=specs,
            out_specs=tuple(pl.BlockSpec(memory_space=pltpu.VMEM) for _ in outs),
            scratch_shapes=scratch,
            compiler_params=pltpu.CompilerParams(vmem_limit_bytes=GRANT),
            name=name,
            interpret=INTERPRET,
        )(*args)

    return run


def edges(axis, tail, head):
    count = lax.axis_size(axis)
    ends = count - 1
    return (
        lax.ppermute(tail, axis, [(i, (i + 1) % count) for i in range(ends)]),
        lax.ppermute(head, axis, [((i + 1) % count, i) for i in range(ends)]),
    )


def block_sum(x):
    x = x + pltpu.roll(x, x.shape[1] // 2, 1)
    rows = x.shape[0]
    even = lax.broadcasted_iota(jnp.int32, x.shape, 0) % 2 == 0
    return x + jnp.where(even, pltpu.roll(x, rows - 1, 0), pltpu.roll(x, 1, 0))


def body(images, filters, hidden_bias, visible_unit_bias, unit_noise):
    n_img, tile_rows, tile_cols = images.shape
    channels, side, _ = filters.shape
    margin = side // 2
    reach = 2 * margin
    far = 3 * margin
    high, wide = tile_rows + 2 * margin, tile_cols + 2 * margin
    tall = tile_rows + 2 * reach
    rows = n_img * tile_rows
    units = tile_cols * channels
    taps = side * wide
    chunks = units // LANES
    lower = (side + 1) // 2 * side
    used = lower + 1
    n_pack = -(-(used + 1) // 16) * 16
    f32, bf16 = jnp.float32, jnp.bfloat16
    shape = jax.ShapeDtypeStruct

    def patches(wide_ref, out_ref, count):
        for n in range(n_img):
            out_ref[n * count : (n + 1) * count, :] = jnp.concatenate(
                [wide_ref[n, r : r + count, :] for r in range(side)], axis=1
            )

    def band_kernel(pair_ref, w_ref, wide_ref):
        wide_ref[...] = jnp.zeros_like(wide_ref)
        for r in range(side):
            block = pair_ref[r]
            for v in range(chunks):
                wide_ref[pl.ds(r * wide + 2 * v, side + 1), pl.ds(v * LANES, LANES)] = block
        w_ref[...] = wide_ref[...].astype(bf16)

    def draw_kernel(noise_ref, before_ref, after_ref, t_ref):
        def inverse(u):
            u = u.astype(f32)
            return jnp.where(u > 0.0, 1.0 / jnp.log(u), 0.0)

        for n in range(n_img):
            t_ref[n, :reach, :] = inverse(before_ref[n, :, :units])
            t_ref[n, reach : reach + tile_rows, :] = inverse(noise_ref[n])
            t_ref[n, reach + tile_rows :, :] = inverse(after_ref[n, :, :units])

    def up_kernel(
        vis_ref, w_ref, t_ref, bias_ref,
        part_ref, head_ref, tail_ref, prob_ref, a_ref, hid_ref, img_ref, col_ref, samp_ref, down_ref,
    ):
        img_ref[...] = vis_ref[...].astype(f32)
        patches(img_ref, col_ref, tall)
        a = col_ref[...].astype(bf16)
        for n in range(n_img):
            at = n * tall + reach
            a_ref[n * tile_rows : (n + 1) * tile_rows, :] = col_ref[at : at + tile_rows, :].astype(bf16)
        for v in range(chunks):
            at = slice(v * LANES, (v + 1) * LANES)
            act = jnp.dot(a, w_ref[:, at], preferred_element_type=f32) + bias_ref[...]
            lift = jnp.exp(act)
            hidden = jnp.zeros((1, LANES), f32)
            for n in range(n_img):
                mine = lift[n * tall + reach : n * tall + reach + tile_rows]
                prob = mine / (1.0 + block_sum(mine))
                prob_ref[n * tile_rows : (n + 1) * tile_rows, at] = prob.astype(bf16)
                hidden = hidden + jnp.sum(prob, axis=0, keepdims=True)
            hid_ref[:, at] = hidden
            t = t_ref[:, :, at].reshape(n_img * tall, LANES)
            cold = jnp.where(t == 0.0, 0.0, lift * t)
            cold = cold * cold
            samp_ref[:, at] = (cold / (1.0 + block_sum(cold))).astype(bf16)
        down_ref[...] = lax.dot_general(
            samp_ref[...], w_ref[...], (((1,), (1,)), ((), ())), preferred_element_type=f32
        )
        for n in range(n_img):
            total = jnp.zeros((high, wide), f32)
            for r in range(side):
                at = n * tall + reach - r
                total = total + down_ref[at : at + high, r * wide : (r + 1) * wide]
            part_ref[n] = total
            head_ref[n] = total[:, :reach]
            tail_ref[n] = total[:, wide - reach :]

    def down_kernel(
        edge_ref, vb_ref, part_ref, before_ref, after_ref, vis_ref, w_ref, bias_ref, prob_ref, a_ref, hid_ref,
        recon_ref, pack_ref, img_ref, col_ref, a2_ref, p2_ref, g_ref, cmb_ref, sum_ref,
    ):
        p = lax.broadcasted_iota(jnp.int32, (high, wide), 0)
        q = lax.broadcasted_iota(jnp.int32, (high, wide), 1)
        inside = (p >= edge_ref[0]) & (p < edge_ref[1]) & (q >= edge_ref[2]) & (q < edge_ref[3])
        gap = jnp.zeros((high, wide - 2 * reach), f32)
        seen = jnp.zeros((tile_rows, tile_cols), f32)
        for n in range(n_img):
            total = part_ref[n] + jnp.concatenate([before_ref[n], gap, after_ref[n]], axis=1)
            recon = (total + vb_ref[0]).astype(bf16).astype(f32)
            img_ref[n] = jnp.where(inside, recon, 0.0)
            mine = img_ref[n, margin : margin + tile_rows, margin : margin + tile_cols]
            recon_ref[n] = mine.astype(bf16)
            seen = seen + (vis_ref[n].astype(f32) - mine)
        seen = jnp.sum(seen, keepdims=True)
        patches(img_ref, col_ref, tile_rows)
        a = col_ref[...].astype(bf16)
        a2_ref[:rows, :] = a_ref[...]
        a2_ref[rows:, :] = -a
        p2_ref[:rows, :] = prob_ref[...]
        hidden = jnp.zeros((1, LANES), f32)
        for v in range(chunks):
            at = slice(v * LANES, (v + 1) * LANES)
            act = jnp.dot(a, w_ref[:, at], preferred_element_type=f32) + bias_ref[...]
            lift = jnp.exp(act)
            prob = lift / (1.0 + block_sum(lift))
            p2_ref[rows:, at] = prob.astype(bf16)
            hidden = hidden + (hid_ref[:, at] - jnp.sum(prob, axis=0, keepdims=True))
        g_ref[...] = lax.dot_general(
            a2_ref[...], p2_ref[...], (((0,), (0,)), ((), ())), preferred_element_type=f32
        )
        for r in range(side):
            acc = g_ref[pl.ds(r * wide, side + 1), pl.ds(0, LANES)]
            for v in range(1, chunks):
                acc = acc + g_ref[pl.ds(r * wide + 2 * v, side + 1), pl.ds(v * LANES, LANES)]
            half = pltpu.roll(acc, channels, 1)
            first = acc[:side] + half[1 : side + 1]
            second = half[:side] + acc[1 : side + 1]
            lane = lax.broadcasted_iota(jnp.int32, (side, LANES), 1)
            cmb_ref[r * side : (r + 1) * side, :] = jnp.where(lane < channels, first, second)
        upper = side * side - lower
        lane = lax.broadcasted_iota(jnp.int32, (lower, LANES), 1)
        sum_ref[...] = jnp.zeros_like(sum_ref)
        sum_ref[:lower, :] = jnp.where(lane < channels, cmb_ref[:lower, :], 0.0)
        lane = lax.broadcasted_iota(jnp.int32, (upper, LANES), 1)
        sum_ref[:upper, :] += jnp.where(lane < channels, 0.0, cmb_ref[lower:, :])
        hidden = hidden + pltpu.roll(hidden, channels, 1)
        lane = lax.broadcasted_iota(jnp.int32, (1, LANES), 1)
        last = jnp.where(lane < channels, hidden, seen)
        sum_ref[lower:used, :] = last
        sum_ref[used : used + 1, :] = last - last.astype(bf16).astype(f32)
        packed = sum_ref[...].astype(bf16)
        for at in range(pack_ref.shape[0]):
            pack_ref[at] = packed

    def spread_kernel(parts_ref, pack_ref, sum_ref):
        sum_ref[...] = jnp.sum(parts_ref[...].astype(f32), axis=0)
        last = sum_ref[lower:used, :] + sum_ref[used : used + 1, :]
        sum_ref[lower:used, :] = last
        sum_ref[used : used + 1, :] = last - last.astype(bf16).astype(f32)
        packed = sum_ref[...].astype(bf16)
        for at in range(pack_ref.shape[0]):
            pack_ref[at] = packed

    def finish_kernel(parts_ref, grad_ref, hid_ref, seen_ref, sum_ref):
        sum_ref[...] = jnp.sum(parts_ref[...].astype(f32), axis=0) * scale
        last = sum_ref[lower:used, :] + sum_ref[used : used + 1, :]
        hid_ref[...] = last[:, :channels]
        seen_ref[...] = last[:, channels : channels + 1]
        for r in range(side):
            half, at = (0, r * side) if r * side < lower else (channels, r * side - lower)
            grad_ref[r] = sum_ref[at : at + side, half : half + channels]

    taps_first = filters.astype(f32).transpose(1, 2, 0)
    pairs = jnp.concatenate(
        [jnp.pad(taps_first, ((0, 0), (0, 1), (0, 0))), jnp.pad(taps_first, ((0, 0), (1, 0), (0, 0)))],
        axis=2,
    )
    bias = jnp.concatenate([hidden_bias, hidden_bias])[None]
    (w,) = call(
        band_kernel, (shape((taps, units), bf16),), [pltpu.VMEM((taps, units), f32)], "band"
    )(pairs)

    def joined(noise, pixels):
        more = jnp.pad(pixels[:, reach:], ((0, 0), (0, 2 * reach - far), (0, 0)))
        return jnp.concatenate([noise, pixels[:, :reach], more], axis=2)

    def pixels_of(payload):
        return jnp.concatenate(
            [payload[:, :, units : units + tile_cols], payload[:, : far - reach, units + tile_cols :]], axis=1
        )

    before, after = edges(
        ROW,
        joined(unit_noise[:, tile_rows - reach :], images[:, tile_rows - far :]),
        joined(unit_noise[:, :reach], images[:, :far]),
    )
    column = jnp.concatenate([pixels_of(before), images, pixels_of(after)], axis=1)
    left, right = edges(COL, column[:, :, tile_cols - margin :], column[:, :, :margin])
    (t,) = call(draw_kernel, (shape((n_img, tall, units), f32),), [], "draw")(unit_noise, before, after)
    visible_wide = jnp.concatenate([left, column, right], axis=2)
    part, head, tail, prob, a, hid = call(
        up_kernel,
        (
            shape((n_img, high, wide), f32),
            shape((n_img, high, reach), f32),
            shape((n_img, high, reach), f32),
            shape((rows, units), bf16),
            shape((rows, taps), bf16),
            shape((1, units), f32),
        ),
        [
            pltpu.VMEM(visible_wide.shape, f32),
            pltpu.VMEM((n_img * tall, taps), f32),
            pltpu.VMEM((n_img * tall, units), bf16),
            pltpu.VMEM((n_img * tall, taps), f32),
        ],
        "up",
    )(visible_wide, w, t, bias)

    left, right = edges(COL, tail, head)

    def limits(axis, size, extent):
        at, last = lax.axis_index(axis), lax.axis_size(axis) - 1
        return [jnp.where(at == 0, margin, 0), jnp.where(at == last, size + margin, extent)]

    bounds = jnp.stack(limits(ROW, tile_rows, high) + limits(COL, tile_cols, wide)).astype(jnp.int32)
    groups = (("img", "row_1"), "col_1", ("col_0", "row_0"))
    copies = [lax.axis_size(axes) for axes in groups]
    recon, pack = call(
        down_kernel,
        (shape(images.shape, bf16), shape((copies[0], n_pack, LANES), bf16)),
        [
            pltpu.VMEM((n_img, high, wide), f32),
            pltpu.VMEM((rows, taps), f32),
            pltpu.VMEM((2 * rows, taps), bf16),
            pltpu.VMEM((2 * rows, units), bf16),
            pltpu.VMEM((taps, units), f32),
            pltpu.VMEM((side * side, LANES), f32),
            pltpu.VMEM((n_pack, LANES), f32),
        ],
        "down",
        smem=(0, 1),
    )(bounds, visible_unit_bias[None], part, left, right, images, w, bias, prob, a, hid)

    scale = 1.0 / float(
        rows * tile_cols * lax.axis_size("img") * lax.axis_size(ROW) * lax.axis_size(COL)
    )
    for axes, following in zip(groups, copies[1:] + [None]):
        parts = lax.all_to_all(pack, axes, 0, 0, tiled=True)
        scratch = [pltpu.VMEM((n_pack, LANES), f32)]
        if following:
            (pack,) = call(spread_kernel, (shape((following, n_pack, LANES), bf16),), scratch, "spread")(parts)
    grad, hidden, seen = call(
        finish_kernel,
        (shape((side, side, channels), f32), shape((1, channels), f32), shape((1, 1), f32)),
        scratch,
        "finish",
    )(parts)
    return (recon, grad.transpose(2, 0, 1), hidden[0], seen[0, 0])


def solution(mesh):
    split = Mesh(
        mesh.devices.reshape(mesh.shape["img"], 2, 4, 4, 8),
        ("img", "row_0", "row_1", "col_0", "col_1"),
    )
    placed = (P("img", ROW, COL), P(), P(), P(), P("img", ROW, COL))
    return jax.shard_map(
        body,
        mesh=split,
        in_specs=placed,
        out_specs=(P("img", ROW, COL), P(), P(), P()),
        check_vma=False,
    )
```

time: 102 us -> 84 us (0.82)
  starting transfers between devices: 22.9 us -> 17.2 us
  other arithmetic: 4.34 us -> 0.36 us
  blocking collectives: 50.6 us -> 47.6 us
  Pallas kernels: 7.06 us -> 4.16 us
  local copies, waits for them, and re-layouts: 4.35 us -> 3.11 us
  waiting for transfers between devices: 10.8 us -> 9.6 us
    ppermute x4 -> x3, starting transfers between devices: 12.1 us -> 8.94 us  [edges(): lax.ppermute(tail, axis, [(i, (i + 1) % count) for i in range(ends)])]
    all_to_all x3, blocking collectives: 50.6 us -> 47.6 us  [body(): parts = lax.all_to_all(pack, axes, 0, 0, tiled=True)]
    pallas_call x3 -> x7, Pallas kernels: 7.06 us -> 4.16 us  [run(): pl.pallas_call(kernel, out_shape=out_shape, in_specs=specs, out_specs=tup...]
    ppermute x4 -> x3, starting transfers between devices: 10.7 us -> 8.26 us  [edges(): lax.ppermute(head, axis, [((i + 1) % count, i) for i in range(ends)])]
    ppermute x4 -> x3, waiting for transfers between devices: 10.8 us -> 9.43 us  [edges(): lax.ppermute(head, axis, [((i + 1) % count, i) for i in range(ends)])]
    slice x6 -> x8, local copies, waits for them, and re-layouts: 2.33 us -> 1.95 us  [the longest x1 0.88 us: body(): unit_noise[:, :reach]]
  transfers between devices with their start and end apart: 8 -> 6, of which waited for: 3 -> 4; matrix products, arithmetic and copies ran while one was open for 3% -> 1% of each run, Pallas kernels for 2% -> 0%
where the time goes in v2:
time: 84 us; the launch traced here: 83.5 us
  blocking collectives  47.6 us (57%)
  starting transfers between devices  17.2 us (20%)
  waiting for transfers between devices  9.6 us (11%)
  Pallas kernels  4.16 us (5%)
  local copies, waits for them, and re-layouts  3.11 us (4%)
  between operations  1.48 us (2%)
    all_to_all x3, blocking collectives, body(): parts = lax.all_to_all(pack, axes, 0, 0, tiled=True)  47.6 us
    ppermute x3, waiting for transfers between devices, edges(): lax.ppermute(head, axis, [((i + 1) % count, i) for i in range(ends)])  9.43 us
    ppermute x3, starting transfers between devices, edges(): lax.ppermute(tail, axis, [(i, (i + 1) % count) for i in range(ends)])  8.94 us
    ppermute x3, starting transfers between devices, edges(): lax.ppermute(head, axis, [((i + 1) % count, i) for i in range(ends)])  8.26 us
    pallas_call x7, Pallas kernels, run(): pl.pallas_call(kernel, out_shape=out_shape, in_specs=specs, out_specs=tup...  4.16 us
  transfers between devices with their start and end apart: 6, of which 4 were waited for; matrix products, arithmetic and copies ran while one was open for 1% of the time, Pallas kernels for 0%

profile of v2, /device:TPU:2, one launch (start us, length us, event | category | flops | bytes accessed | tf_op | source)
XLA Modules:
  0.0 83.5 jit_solution(5523808518129754806)
XLA Ops:
  0.6 0.0 copy-start.1
  0.6 0.8 fusion.3
  1.5 0.0 copy-done.1
  1.5 0.9 %fusion = (bf16[4,8,1024]{2,1,0:T(8,128)(2,1)S(1)}, bf16[4,8,1024]{2,1,0:T(8,128)(2,1)S(1)}) fusion(bf16[4,16,1024]{2,1,0:T(8,128)(2,1)} %noise_ref.1), kind=kLoop, calls=%fused_computation.7 | loop fusion | bytes 262144 | tf_op jit(solution)/shard_map/slice | solution.py:230
  2.4 0.1 concatenate.18
  2.5 3.4 %collective-permute-start = (bf16[4,8,1056]{2,1,0:T(8,128)(2,1)S(1)}, bf16[4,8,1056]{2,1,0:T(8,128)(2,1)S(1)}, u32[]{:S(2)}, u32[]{:S(2)}) collective-permute-start(bf16[4,8,1056]{2,1,0:T(8,128)(2,1)S(1)} %concatenate.18), channel_id=1, source_target_pairs={{0,32},{32,64},{64,96},{96,128},{128,160},{160,192},{192,224},{1,3... | collective-permute-start | bytes 202760 | tf_op jit(solution)/shard_map/ppermute | solution.py:42
  5.9 0.0 copy-start.2
  5.9 0.1 concatenate.19
  6.0 5.7 %collective-permute-start.1 = (bf16[4,8,1056]{2,1,0:T(8,128)(2,1)S(1)}, bf16[4,8,1056]{2,1,0:T(8,128)(2,1)S(1)}, u32[]{:S(2)}, u32[]{:S(2)}) collective-permute-start(bf16[4,8,1056]{2,1,0:T(8,128)(2,1)S(1)} %concatenate.19), channel_id=1, source_target_pairs={{32,0},{64,32},{96,64},{128,96},{160,128},{192,160},{224,192},{33,... | collective-permute-start | bytes 202760 | tf_op jit(solution)/shard_map/ppermute | solution.py:43
  11.7 0.0 copy-done.2
  11.7 0.1 select_maximum_fusion.pair_ref
  11.8 0.1 band.1.w_ref
  11.9 0.0 copy-start.3
  11.9 0.6 copy-done.3
  12.6 0.1 maximum_bitcast_fusion.bias_ref
  12.6 0.0 collective-permute-done.before_ref
  12.7 0.1 slice.55
  12.7 0.9 %collective-permute-done.1.after_ref = bf16[4,8,1056]{2,1,0:T(8,128)(2,1)S(1)} collective-permute-done((bf16[4,8,1056]{2,1,0:T(8,128)(2,1)S(1)}, bf16[4,8,1056]{2,1,0:T(8,128)(2,1)S(1)}, u32[]{:S(2)}, u32[]{:S(2)}) %collective-permute-start.1) | collective-permute-done | bytes 67616 | tf_op jit(solution)/shard_map/ppermute | solution.py:43
  13.6 0.1 slice.57
  13.7 0.0 copy-start
  13.7 0.3 concatenate.20
  14.0 0.1 fusion.1
  14.1 2.1 %collective-permute-start.2 = (bf16[4,40,4]{2,1,0:T(8,128)(2,1)S(1)}, bf16[4,40,4]{2,1,0:T(8,128)(2,1)S(1)}, u32[]{:S(2)}, u32[]{:S(2)}) collective-permute-start(bf16[4,40,4]{2,1,0:T(8,128)(2,1)S(1)} %get-tuple-element.28), channel_id=1, source_target_pairs={{0,1},{1,2},{2,3},{3,4},{4,5},{5,6},{6,7},{7,8},{8,9},{9,10},{10,1... | collective-permute-start | bytes 3848 | tf_op jit(solution)/shard_map/ppermute | solution.py:42
  16.2 1.3 %collective-permute-start.3 = (bf16[4,40,4]{2,1,0:T(8,128)(2,1)S(1)}, bf16[4,40,4]{2,1,0:T(8,128)(2,1)S(1)}, u32[]{:S(2)}, u32[]{:S(2)}) collective-permute-start(bf16[4,40,4]{2,1,0:T(8,128)(2,1)S(1)} %get-tuple-element.29), channel_id=1, source_target_pairs={{1,0},{2,1},{3,2},{4,3},{5,4},{6,5},{7,6},{8,7},{9,8},{10,9},{11,1... | collective-permute-start | bytes 3848 | tf_op jit(solution)/shard_map/ppermute | solution.py:43
  17.5 0.0 copy-done
  17.5 0.1 draw.1.t_ref
  17.7 0.2 collective-permute-done.2
  17.8 4.2 %collective-permute-done.3 = bf16[4,40,4]{2,1,0:T(8,128)(2,1)S(1)} collective-permute-done((bf16[4,40,4]{2,1,0:T(8,128)(2,1)S(1)}, bf16[4,40,4]{2,1,0:T(8,128)(2,1)S(1)}, u32[]{:S(2)}, u32[]{:S(2)}) %collective-permute-start.3) | collective-permute-done | bytes 1312 | tf_op jit(solution)/shard_map/ppermute | solution.py:43
  22.1 0.1 pad_maximum_fusion.vis_ref
  22.2 1.1 %up.1 = (f32[4,24,24]{2,1,0:T(8,128)S(1)}, f32[4,24,8]{2,1,0:T(8,128)S(1)}, f32[4,24,8]{2,1,0:T(8,128)S(1)}, bf16[64,1024]{1,0:T(8,128)(2,1)S(1)}, bf16[64,216]{1,0:T(8,128)(2,1)S(1)}, /*index=5*/f32[1,1024]{1,0:T(1,128)S(1)}) custom-call(bf16[4,40,24]{2,1,0:T(8,128)(2,1)S(1)} %pad_maximum_fusion.vis_ref, bf16[216,1024]{1,0:T(8,128)(2,1)S(1)} %band.1.w_ref, ...), custom_call_target="tpu_custom_call" | custom-call | tf_op jit(solution)/shard_map/up/pallas_call | solution.py:24
  23.3 3.5 %collective-permute-start.4 = (f32[4,24,8]{2,1,0:T(8,128)S(1)}, f32[4,24,8]{2,1,0:T(8,128)S(1)}, u32[]{:S(2)}, u32[]{:S(2)}) collective-permute-start(f32[4,24,8]{2,1,0:T(8,128)S(1)} %get-tuple-element.16), channel_id=1, source_target_pairs={{0,1},{1,2},{2,3},{3,4},{4,5},{5,6},{6,7},{7,8},{8,9},{9,10},{10,1... | collective-permute-start | bytes 9224 | tf_op jit(solution)/shard_map/ppermute | solution.py:42
  26.8 1.3 %collective-permute-start.5 = (f32[4,24,8]{2,1,0:T(8,128)S(1)}, f32[4,24,8]{2,1,0:T(8,128)S(1)}, u32[]{:S(2)}, u32[]{:S(2)}) collective-permute-start(f32[4,24,8]{2,1,0:T(8,128)S(1)} %get-tuple-element.17), channel_id=1, source_target_pairs={{1,0},{2,1},{3,2},{4,3},{5,4},{6,5},{7,6},{8,7},{9,8},{10,9},{11,1... | collective-permute-start | bytes 9224 | tf_op jit(solution)/shard_map/ppermute | solution.py:43
  28.1 0.1 pad_add_fusion.edge_ref
  28.8 0.0 collective-permute-done.4.before_ref
  28.8 4.3 %collective-permute-done.5.after_ref = f32[4,24,8]{2,1,0:T(8,128)S(1)} collective-permute-done((f32[4,24,8]{2,1,0:T(8,128)S(1)}, f32[4,24,8]{2,1,0:T(8,128)S(1)}, u32[]{:S(2)}, u32[]{:S(2)}) %collective-permute-start.5) | collective-permute-done | bytes 3104 | tf_op jit(solution)/shard_map/ppermute | solution.py:43
  33.1 2.0 %down.1 = (bf16[4,16,16]{2,1,0:T(8,128)(2,1)}, bf16[8,48,128]{2,1,0:T(8,128)(2,1)S(1)}) custom-call(s32[4]{0:T(128)S(1)} %pad_add_fusion.edge_ref, f32[1]{0:T(128)} %bitcast.12.vb_ref, f32[4,24,24]{2,1,0:T(8,128)S(1)} %get-tuple-element.15.part_ref, f32[4,24,8]{2,1,0:T(8,128)S(1)} %collective-permute-done.4.before_ref, ...), custom_call_target="tpu_custom_call" | custom-call | tf_op jit(solution)/shard_map/down/pallas_call | solution.py:24
  35.1 11.5 %all_to_all.15.parts_ref = bf16[8,48,128]{2,1,0:T(8,128)(2,1)S(1)} all-to-all(bf16[8,48,128]{2,1,0:T(8,128)(2,1)S(1)} %get-tuple-element.22), channel_id=1, replica_groups=mesh['img'=2,'row_0'=2,'row_1'=4,'col_0'=4,'col_1'=8] {'img','row_1'}, dimensions={0} | all-to-all | bytes 196608 | tf_op jit(solution)/shard_map/all_to_all | solution.py:284
  46.6 19.2 %all_to_all.16.parts_ref = bf16[8,48,128]{2,1,0:T(8,128)(2,1)S(1)} all-to-all(bf16[8,48,128]{2,1,0:T(8,128)(2,1)S(1)} %spread.2), channel_id=1, replica_groups=mesh['img'=2,'row_0'=2,'row_1'=4,'col_0'=4,'col_1'=8] {'col_1'}, dimensions={0} | all-to-all | bytes 196608 | tf_op jit(solution)/shard_map/all_to_all | solution.py:284
  65.9 16.9 %all_to_all.17.parts_ref = bf16[8,48,128]{2,1,0:T(8,128)(2,1)S(1)} all-to-all(bf16[8,48,128]{2,1,0:T(8,128)(2,1)S(1)} %spread.3), channel_id=1, replica_groups=mesh['img'=2,'row_0'=2,'row_1'=4,'col_0'=4,'col_1'=8] {'col_0','row_0'}, dimensions={0} | all-to-all | bytes 196608 | tf_op jit(solution)/shard_map/all_to_all | solution.py:284
  82.8 0.7 finish.1
  (8 shorter events, 0.1 us)
Async XLA Ops:
  0.6 0.8 %copy-start.1 = (bf16[4,16,16]{2,1,0:T(8,128)(2,1)S(1)}, bf16[4,16,16]{2,1,0:T(8,128)(2,1)}, u32[]{:S(2)}) copy-start(bf16[4,16,16]{2,1,0:T(8,128)(2,1)} %vis_ref.1) | copy-start | bytes 6148
  2.5 10.2 %collective-permute-start = (bf16[4,8,1056]{2,1,0:T(8,128)(2,1)S(1)}, bf16[4,8,1056]{2,1,0:T(8,128)(2,1)S(1)}, u32[]{:S(2)}, u32[]{:S(2)}) collective-permute-start(bf16[4,8,1056]{2,1,0:T(8,128)(2,1)S(1)} %concatenate.18), channel_id=1, source_target_pairs={{0,32},{32,64},{64,96},{96,128},{128,160},{160,192},{192,224},{1,3... | collective-permute-start | bytes 202760 | tf_op jit(solution)/shard_map/ppermute | solution.py:42
  5.9 5.8 %copy-start.2 = (bf16[64,9,9]{0,2,1:T(8,128)(2,1)S(1)}, bf16[64,9,9]{0,2,1:T(8,128)(2,1)}, u32[]{:S(2)}) copy-start(bf16[64,9,9]{0,2,1:T(8,128)(2,1)} %param.6) | copy-start | bytes 31108
  6.0 7.6 %collective-permute-start.1 = (bf16[4,8,1056]{2,1,0:T(8,128)(2,1)S(1)}, bf16[4,8,1056]{2,1,0:T(8,128)(2,1)S(1)}, u32[]{:S(2)}, u32[]{:S(2)}) collective-permute-start(bf16[4,8,1056]{2,1,0:T(8,128)(2,1)S(1)} %concatenate.19), channel_id=1, source_target_pairs={{32,0},{64,32},{96,64},{128,96},{160,128},{192,160},{224,192},{33,... | collective-permute-start | bytes 202760 | tf_op jit(solution)/shard_map/ppermute | solution.py:43
  11.9 0.7 copy-start.3
  13.7 3.8 %copy-start = (bf16[4,16,1024]{2,1,0:T(8,128)(2,1)S(1)}, bf16[4,16,1024]{2,1,0:T(8,128)(2,1)}, u32[]{:S(2)}) copy-start(bf16[4,16,1024]{2,1,0:T(8,128)(2,1)} %noise_ref.1) | copy-start | bytes 393220
  14.1 3.7 %collective-permute-start.2 = (bf16[4,40,4]{2,1,0:T(8,128)(2,1)S(1)}, bf16[4,40,4]{2,1,0:T(8,128)(2,1)S(1)}, u32[]{:S(2)}, u32[]{:S(2)}) collective-permute-start(bf16[4,40,4]{2,1,0:T(8,128)(2,1)S(1)} %get-tuple-element.28), channel_id=1, source_target_pairs={{0,1},{1,2},{2,3},{3,4},{4,5},{5,6},{6,7},{7,8},{8,9},{9,10},{10,1... | collective-permute-start | bytes 3848 | tf_op jit(solution)/shard_map/ppermute | solution.py:42
  16.2 5.9 %collective-permute-start.3 = (bf16[4,40,4]{2,1,0:T(8,128)(2,1)S(1)}, bf16[4,40,4]{2,1,0:T(8,128)(2,1)S(1)}, u32[]{:S(2)}, u32[]{:S(2)}) collective-permute-start(bf16[4,40,4]{2,1,0:T(8,128)(2,1)S(1)} %get-tuple-element.29), channel_id=1, source_target_pairs={{1,0},{2,1},{3,2},{4,3},{5,4},{6,5},{7,6},{8,7},{9,8},{10,9},{11,1... | collective-permute-start | bytes 3848 | tf_op jit(solution)/shard_map/ppermute | solution.py:43
  23.3 5.5 %collective-permute-start.4 = (f32[4,24,8]{2,1,0:T(8,128)S(1)}, f32[4,24,8]{2,1,0:T(8,128)S(1)}, u32[]{:S(2)}, u32[]{:S(2)}) collective-permute-start(f32[4,24,8]{2,1,0:T(8,128)S(1)} %get-tuple-element.16), channel_id=1, source_target_pairs={{0,1},{1,2},{2,3},{3,4},{4,5},{5,6},{6,7},{7,8},{8,9},{9,10},{10,1... | collective-permute-start | bytes 9224 | tf_op jit(solution)/shard_map/ppermute | solution.py:42
  26.8 6.3 %collective-permute-start.5 = (f32[4,24,8]{2,1,0:T(8,128)S(1)}, f32[4,24,8]{2,1,0:T(8,128)S(1)}, u32[]{:S(2)}, u32[]{:S(2)}) collective-permute-start(f32[4,24,8]{2,1,0:T(8,128)S(1)} %get-tuple-element.17), channel_id=1, source_target_pairs={{1,0},{2,1},{3,2},{4,3},{5,4},{6,5},{7,6},{8,7},{9,8},{10,9},{11,1... | collective-permute-start | bytes 9224 | tf_op jit(solution)/shard_map/ppermute | solution.py:43

commit v3 on v2

v3 whole, which is shorter than its diff:
```python
import jax
import jax.numpy as jnp
from jax import lax
from jax.experimental import pallas as pl
from jax.experimental.pallas import tpu as pltpu
from jax.sharding import Mesh
from jax.sharding import PartitionSpec as P

ROW = ("row_0", "row_1")
COL = ("col_0", "col_1")
LANES = 128
GROUPS = (("img", "col_1"), ("row_1", "col_0", "row_0"))
INTERPRET = False
GRANT = 8 << 20


def call(kernel, out_shape, scratch, name, smem=()):
    outs = out_shape if isinstance(out_shape, (list, tuple)) else (out_shape,)

    def run(*args):
        specs = [
            pl.BlockSpec(memory_space=pltpu.SMEM if at in smem else pltpu.VMEM)
            for at in range(len(args))
        ]
        return pl.pallas_call(
            kernel,
            out_shape=out_shape,
            in_specs=specs,
            out_specs=tuple(pl.BlockSpec(memory_space=pltpu.VMEM) for _ in outs),
            scratch_shapes=scratch,
            compiler_params=pltpu.CompilerParams(vmem_limit_bytes=GRANT),
            name=name,
            interpret=INTERPRET,
        )(*args)

    return run


def edges(axis, tail, head):
    count = lax.axis_size(axis)
    ends = count - 1
    return (
        lax.ppermute(tail, axis, [(i, (i + 1) % count) for i in range(ends)]),
        lax.ppermute(head, axis, [((i + 1) % count, i) for i in range(ends)]),
    )


def block_sum(x):
    x = x + pltpu.roll(x, x.shape[1] // 2, 1)
    rows = x.shape[0]
    even = lax.broadcasted_iota(jnp.int32, x.shape, 0) % 2 == 0
    return x + jnp.where(even, pltpu.roll(x, rows - 1, 0), pltpu.roll(x, 1, 0))


def body(images, filters, hidden_bias, visible_unit_bias, unit_noise):
    n_img, tile_rows, tile_cols = images.shape
    channels, side, _ = filters.shape
    margin = side // 2
    reach = 2 * margin
    far = 3 * margin
    high = tile_rows + 2 * margin
    tall, taller = tile_rows + 2 * reach, tile_rows + 2 * far
    broad = tile_cols + margin
    wide = broad + 2 * margin
    rows = n_img * tile_rows
    own, units, extra = tile_cols * channels, broad * channels, margin * channels
    taps = side * wide
    chunks, edge = units // LANES, extra // LANES
    count = side * side
    quarter = -(-count // 4)
    part_rows = -(-(quarter + 2) // 8) * 8
    f32, bf16 = jnp.float32, jnp.bfloat16
    shape = jax.ShapeDtypeStruct
    scale = 1.0 / float(
        rows * tile_cols * lax.axis_size("img") * lax.axis_size(ROW) * lax.axis_size(COL)
    )

    def patches(wide_ref, out_ref, size):
        for n in range(n_img):
            out_ref[n * size : (n + 1) * size, :] = jnp.concatenate(
                [wide_ref[n, r : r + size, :] for r in range(side)], axis=1
            )

    def pack_kernel(vis_ref, noise_ref, down_ref, up_ref):
        def beside(first, last, size):
            more = jnp.concatenate([last, jnp.zeros((size - last.shape[0], tile_cols), f32)], axis=0)
            return jnp.concatenate([first, more], axis=1).astype(bf16)

        for n in range(n_img):
            pixels = vis_ref[n].astype(f32)
            down_ref[n, :, :own] = noise_ref[n, tile_rows - reach :, :]
            lowest = pixels[tile_rows - far :]
            down_ref[n, :, own:] = beside(lowest[:reach], lowest[reach:], reach)
            up_ref[n, :, :own] = noise_ref[n, :reach, :]
            up_ref[n, :, own:] = beside(pixels[:reach], pixels[reach:far], reach)

    def mid_kernel(vis_ref, noise_ref, before_ref, after_ref, column_ref, send_ref, col_ref):
        for n in range(n_img):
            for at, payload in ((0, before_ref), (far + tile_rows, after_ref)):
                pixels = payload[n, :, own:].astype(f32)
                col_ref[at : at + reach, :] = pixels[:, :tile_cols]
                col_ref[at + reach : at + far, :] = pixels[: far - reach, tile_cols:]
            col_ref[far : far + tile_rows, :] = vis_ref[n].astype(f32)
            column_ref[n] = col_ref[...].astype(bf16)
            send_ref[n, :reach, :extra] = before_ref[n, :, :extra]
            send_ref[n, reach : reach + tile_rows, :extra] = noise_ref[n, :, :extra]
            send_ref[n, reach + tile_rows :, :extra] = after_ref[n, :, :extra]
            over = taller - tall
            low = jnp.concatenate(
                [col_ref[tall:, :reach], jnp.zeros((tall - over, reach), f32)], axis=0
            )
            send_ref[n, :, extra:] = jnp.concatenate([col_ref[:tall, :reach], low], axis=1).astype(bf16)

    def band_kernel(pair_ref, w_ref, wide_ref):
        wide_ref[...] = jnp.zeros_like(wide_ref)
        for r in range(side):
            block = pair_ref[r]
            for v in range(chunks):
                wide_ref[pl.ds(r * wide + 2 * v, side + 1), pl.ds(v * LANES, LANES)] = block
        w_ref[...] = wide_ref[...].astype(bf16)

    def inverse(u):
        u = u.astype(f32)
        return jnp.where(u > 0.0, 1.0 / jnp.log(u), 0.0)

    def draw_kernel(noise_ref, before_ref, after_ref, t_ref):
        for n in range(n_img):
            t_ref[n, :reach, :] = inverse(before_ref[n, :, :own])
            t_ref[n, reach : reach + tile_rows, :] = inverse(noise_ref[n])
            t_ref[n, reach + tile_rows :, :] = inverse(after_ref[n, :, :own])

    def up_kernel(
        flag_ref, column_ref, next_ref, w_ref, t_ref, bias_ref,
        part_ref, send_ref, prob_ref, a_ref, hid_ref, img_ref, col_ref, samp_ref, down_ref,
    ):
        starts, goes_on = flag_ref[0:1, :], flag_ref[3:4, :]
        for n in range(n_img):
            pixels = next_ref[n, :, extra:].astype(f32)
            beyond = jnp.concatenate([pixels[:, :reach], pixels[: taller - tall, reach:]], axis=0)
            img_ref[n] = jnp.concatenate(
                [jnp.zeros((taller, margin), f32), column_ref[n].astype(f32), beyond], axis=1
            )
        patches(img_ref, col_ref, tall)
        a = col_ref[...].astype(bf16)
        for n in range(n_img):
            at = n * tall + reach
            a_ref[n * tile_rows : (n + 1) * tile_rows, :] = col_ref[at : at + tile_rows, :].astype(bf16)
        for v in range(chunks):
            at = slice(v * LANES, (v + 1) * LANES)
            act = jnp.dot(a, w_ref[:, at], preferred_element_type=f32) + bias_ref[...]
            lift = jnp.exp(act)
            hidden = jnp.zeros((1, LANES), f32)
            for n in range(n_img):
                mine = lift[n * tall + reach : n * tall + reach + tile_rows]
                prob = mine / (1.0 + block_sum(mine))
                if v < edge:
                    prob = jnp.where(starts > 0.0, prob, 0.0)
                if v >= chunks - edge:
                    prob = jnp.where(goes_on > 0.0, prob, 0.0)
                prob_ref[n * tile_rows : (n + 1) * tile_rows, at] = prob.astype(bf16)
                hidden = hidden + jnp.sum(prob, axis=0, keepdims=True)
            hid_ref[:, at] = hidden
            if v >= chunks - edge:
                far_at = slice(v * LANES - own, (v + 1) * LANES - own)
                t = inverse(next_ref[:, :, far_at]).reshape(n_img * tall, LANES)
            else:
                t = t_ref[:, :, at].reshape(n_img * tall, LANES)
            if v < edge:
                t = t * starts
            cold = jnp.where(t == 0.0, 0.0, lift * t)
            cold = cold * cold
            samp_ref[:, at] = (cold / (1.0 + block_sum(cold))).astype(bf16)
        down_ref[...] = lax.dot_general(
            samp_ref[...], w_ref[...], (((1,), (1,)), ((), ())), preferred_element_type=f32
        )
        for n in range(n_img):
            total = jnp.zeros((high, wide), f32)
            for r in range(side):
                at = n * tall + reach - r
                total = total + down_ref[at : at + high, r * wide : (r + 1) * wide]
            part_ref[n] = total[:, margin : margin + tile_cols]
            send_ref[n] = total[:, wide - 2 * reach :]

    def down_kernel(
        flag_ref, part_ref, before_ref, vis_ref, w_ref, bias_ref, prob_ref, a_ref, hid_ref,
        recon_ref, pack_ref, img_ref, col_ref, a2_ref, p2_ref, g_ref, cmb_ref, sum_ref,
    ):
        follows, ends = flag_ref[1:2, :], flag_ref[2:3, :]
        p = lax.broadcasted_iota(jnp.int32, (high, wide), 0)
        q = lax.broadcasted_iota(jnp.int32, (high, wide), 1)
        inside = (
            ((p >= margin) | (flag_ref[4:5, :wide] == 0.0))
            & ((p < margin + tile_rows) | (flag_ref[5:6, :wide] == 0.0))
            & ((q >= reach) | (follows[:, :wide] > 0.0))
            & (q < reach + tile_cols)
        )
        seen = jnp.zeros((tile_rows, tile_cols), f32)
        for n in range(n_img):
            total = jnp.concatenate(
                [before_ref[n], jnp.zeros((high, wide - 2 * reach), f32)], axis=1
            ) + jnp.concatenate(
                [jnp.zeros((high, reach), f32), part_ref[n], jnp.zeros((high, wide - reach - tile_cols), f32)],
                axis=1,
            )
            recon = (total + flag_ref[6:7, :wide]).astype(bf16).astype(f32)
            img_ref[n] = jnp.where(inside, recon, 0.0)
            mine = img_ref[n, margin : margin + tile_rows, reach : reach + tile_cols]
            recon_ref[n] = mine.astype(bf16)
            seen = seen + (vis_ref[n].astype(f32) - mine)
        seen = jnp.sum(seen, keepdims=True)
        patches(img_ref, col_ref, tile_rows)
        a = col_ref[...].astype(bf16)
        a2_ref[:rows, :] = a_ref[...]
        a2_ref[rows:, :] = -a
        p2_ref[:rows, :] = prob_ref[...]
        hidden = jnp.zeros((1, LANES), f32)
        for v in range(chunks):
            at = slice(v * LANES, (v + 1) * LANES)
            act = jnp.dot(a, w_ref[:, at], preferred_element_type=f32) + bias_ref[...]
            lift = jnp.exp(act)
            prob = lift / (1.0 + block_sum(lift))
            if v < edge:
                prob = jnp.where(follows > 0.0, prob, 0.0)
            if v >= chunks - edge:
                prob = jnp.where(ends > 0.0, prob, 0.0)
            p2_ref[rows:, at] = prob.astype(bf16)
            hidden = hidden + (hid_ref[:, at] - jnp.sum(prob, axis=0, keepdims=True))
        g_ref[...] = lax.dot_general(
            a2_ref[...], p2_ref[...], (((0,), (0,)), ((), ())), preferred_element_type=f32
        )
        lane = lax.broadcasted_iota(jnp.int32, (side, LANES), 1)
        cmb_ref[...] = jnp.zeros_like(cmb_ref)
        for r in range(side):
            acc = g_ref[pl.ds(r * wide, side + 1), pl.ds(0, LANES)]
            for v in range(1, chunks):
                acc = acc + g_ref[pl.ds(r * wide + 2 * v, side + 1), pl.ds(v * LANES, LANES)]
            half = pltpu.roll(acc, channels, 1)
            cmb_ref[r * side : (r + 1) * side, :] = jnp.where(
                lane < channels, acc[:side] + half[1 : side + 1], half[:side] + acc[1 : side + 1]
            )
        hidden = hidden + pltpu.roll(hidden, channels, 1)
        lane = lax.broadcasted_iota(jnp.int32, (quarter, LANES), 1)
        copies = pack_ref.shape[0] // 2
        for half, last in ((0, hidden), (1, jnp.broadcast_to(seen, (1, LANES)))):
            at = 2 * half * quarter
            sum_ref[...] = jnp.zeros_like(sum_ref)
            sum_ref[:quarter, :] = jnp.where(
                lane < channels, cmb_ref[at : at + quarter, :], cmb_ref[at + quarter : at + 2 * quarter, :]
            )
            packed = split(sum_ref, last)
            for to in range(copies):
                pack_ref[half * copies + to] = packed

    def split(sum_ref, last):
        sum_ref[quarter : quarter + 1, :] = last
        sum_ref[quarter + 1 : quarter + 2, :] = last - last.astype(bf16).astype(f32)
        return sum_ref[...].astype(bf16)

    def added(parts_ref, sum_ref):
        sum_ref[...] = jnp.sum(parts_ref[...].astype(f32), axis=0)
        return sum_ref[quarter : quarter + 1, :] + sum_ref[quarter + 1 : quarter + 2, :]

    def spread_kernel(parts_ref, pack_ref, sum_ref):
        packed = split(sum_ref, added(parts_ref, sum_ref))
        for to in range(pack_ref.shape[0]):
            pack_ref[to] = packed

    def share_kernel(parts_ref, pack_ref, sum_ref):
        last = added(parts_ref, sum_ref)
        sum_ref[quarter : quarter + 1, :] = last
        for to in range(pack_ref.shape[0]):
            pack_ref[to] = sum_ref[...] * scale

    def finish_kernel(halves_ref, recon_in_ref, recon_ref, grad_ref, hid_ref, seen_ref, flat_ref):
        recon_ref[...] = recon_in_ref[...]
        for half in range(2):
            for side_of in range(2):
                at = (2 * half + side_of) * quarter
                flat_ref[at : at + quarter, :] = halves_ref[
                    half, :quarter, side_of * channels : (side_of + 1) * channels
                ]
        for r in range(side):
            grad_ref[r] = flat_ref[r * side : (r + 1) * side, :]
        hid_ref[...] = halves_ref[0, quarter : quarter + 1, :channels]
        seen_ref[...] = halves_ref[1, quarter : quarter + 1, :1]

    taps_first = filters.astype(f32).transpose(1, 2, 0)
    pairs = jnp.concatenate(
        [jnp.pad(taps_first, ((0, 0), (0, 1), (0, 0))), jnp.pad(taps_first, ((0, 0), (1, 0), (0, 0)))],
        axis=2,
    )
    bias = jnp.concatenate([hidden_bias, hidden_bias])[None]
    col_at, row_at = lax.axis_index(COL), lax.axis_index(ROW)
    first, last = col_at == 0, col_at == lax.axis_size(COL) - 1
    top, bottom = row_at == 0, row_at == lax.axis_size(ROW) - 1
    line = lax.broadcasted_iota(jnp.int32, (8, LANES), 0)
    flags = jnp.zeros((8, LANES), f32)
    for at, value in enumerate(
        (first, ~first, last, ~last, top, bottom, visible_unit_bias)
    ):
        flags = jnp.where(line == at, jnp.asarray(value, f32), flags)

    payload = shape((n_img, reach, own + 2 * tile_cols), bf16)
    downward, upward = call(pack_kernel, (payload, payload), [], "pack")(images, unit_noise)
    before, after = edges(ROW, downward, upward)
    (w,) = call(
        band_kernel, (shape((taps, units), bf16),), [pltpu.VMEM((taps, units), f32)], "band"
    )(pairs)
    column, leftward = call(
        mid_kernel,
        (shape((n_img, taller, tile_cols), bf16), shape((n_img, tall, extra + 2 * reach), bf16)),
        [pltpu.VMEM((taller, tile_cols), f32)],
        "mid",
    )(images, unit_noise, before, after)

    steps = lax.axis_size(COL) - 1
    beyond = lax.ppermute(leftward, COL, [(i + 1, i) for i in range(steps)])
    (t,) = call(draw_kernel, (shape((n_img, tall, own), f32),), [], "draw")(unit_noise, before, after)
    part, rightward, prob, a, hid = call(
        up_kernel,
        (
            shape((n_img, high, tile_cols), f32),
            shape((n_img, high, 2 * reach), f32),
            shape((rows, units), bf16),
            shape((rows, taps), bf16),
            shape((1, units), f32),
        ),
        [
            pltpu.VMEM((n_img, taller, wide), f32),
            pltpu.VMEM((n_img * tall, taps), f32),
            pltpu.VMEM((n_img * tall, units), bf16),
            pltpu.VMEM((n_img * tall, taps), f32),
        ],
        "up",
    )(flags, column, beyond, w, t, bias)

    shares = lax.ppermute(rightward, COL, [(i, i + 1) for i in range(steps)])
    sizes = [lax.axis_size(axes) for axes in GROUPS]
    recon, pack = call(
        down_kernel,
        (shape(images.shape, bf16), shape((sizes[0], part_rows, LANES), bf16)),
        [
            pltpu.VMEM((n_img, high, wide), f32),
            pltpu.VMEM((rows, taps), f32),
            pltpu.VMEM((2 * rows, taps), bf16),
            pltpu.VMEM((2 * rows, units), bf16),
            pltpu.VMEM((taps, units), f32),
            pltpu.VMEM((4 * quarter, LANES), f32),
            pltpu.VMEM((part_rows, LANES), f32),
        ],
        "down",
    )(flags, part, shares, images, w, bias, prob, a, hid)

    scratch = [pltpu.VMEM((part_rows, LANES), f32)]
    for axes, following in zip(GROUPS, sizes[1:] + [None]):
        parts = lax.all_to_all(pack, axes, 0, 0, tiled=True)
        if following:
            (pack,) = call(
                spread_kernel, (shape((following, part_rows, LANES), bf16),), scratch, "spread"
            )(parts)
    (pack,) = call(share_kernel, (shape((2, part_rows, LANES), f32),), scratch, "share")(parts)
    halves = lax.all_to_all(pack, "img", 0, 0, tiled=True)
    recon, grad, hidden, seen = call(
        finish_kernel,
        (
            shape(images.shape, bf16),
            shape((side, side, channels), f32),
            shape((1, channels), f32),
            shape((1, 1), f32),
        ),
        [pltpu.VMEM((4 * quarter, channels), f32)],
        "finish",
    )(halves, recon)
    return (recon, grad.transpose(2, 0, 1), hidden[0], seen[0, 0])


def solution(mesh):
    split = Mesh(
        mesh.devices.reshape(mesh.shape["img"], 2, 4, 4, 8),
        ("img", "row_0", "row_1", "col_0", "col_1"),
    )
    placed = (P("img", ROW, COL), P(), P(), P(), P("img", ROW, COL))
    return jax.shard_map(
        body,
        mesh=split,
        in_specs=placed,
        out_specs=(P("img", ROW, COL), P(), P(), P()),
        check_vma=False,
    )
```

time: 84 us -> 75.4 us (0.90)
  the two profiles are of different devices: /device:TPU:2 before, /device:TPU:1 now
where the time goes in v3:
time: 75.4 us; the launch traced here: 74.9 us
  blocking collectives  50.4 us (67%)
  starting transfers between devices  9.72 us (13%)
  waiting for transfers between devices  7.68 us (10%)
  Pallas kernels  3.74 us (5%)
  local copies, waits for them, and re-layouts  1.64 us (2%)
  between operations  1.47 us (2%)
    all_to_all x2, blocking collectives, body(): parts = lax.all_to_all(pack, axes, 0, 0, tiled=True)  44.2 us
    all_to_all x1, blocking collectives, body(): halves = lax.all_to_all(pack, 'img', 0, 0, tiled=True)  6.24 us
    ppermute x1, starting transfers between devices, edges(): lax.ppermute(tail, axis, [(i, (i + 1) % count) for i in range(ends)])  3.94 us
    ppermute x1, waiting for transfers between devices, body(): beyond = lax.ppermute(leftward, COL, [(i + 1, i) for i in range(steps)])  3.83 us
    pallas_call x9, Pallas kernels, run(): pl.pallas_call(kernel, out_shape=out_shape, in_specs=specs, out_specs=tup...  3.74 us
    ppermute x1, starting transfers between devices, body(): shares = lax.ppermute(rightward, COL, [(i, i + 1) for i in range(steps)])  3.2 us
    ppermute x1, waiting for transfers between devices, edges(): lax.ppermute(head, axis, [((i + 1) % count, i) for i in range(ends)])  2.69 us
    unnamed x12, local copies, waits for them, and re-layouts  1.64 us
  transfers between devices with their start and end apart: 4, of which 3 were waited for; matrix products, arithmetic and copies ran while one was open for 0% of the time, Pallas kernels for 0%

profile of v3, /device:TPU:1, one launch (start us, length us, event | category | flops | bytes accessed | tf_op | source)
XLA Modules:
  0.0 74.9 jit_solution(7826517371761197446)
XLA Ops:
  0.6 0.0 copy-start
  0.6 0.9 %copy-done = bf16[4,16,1024]{2,1,0:T(8,128)(2,1)S(1)} copy-done((bf16[4,16,1024]{2,1,0:T(8,128)(2,1)S(1)}, bf16[4,16,1024]{2,1,0:T(8,128)(2,1)}, u32[]{:S(2)}) %copy-start) | copy-done | bytes 131096
  1.5 0.0 copy-start.2
  1.5 0.7 copy-done.2
  2.3 0.1 pack.1
  2.3 0.0 copy-start.4
  2.4 3.9 %collective-permute-start = (bf16[4,8,1056]{2,1,0:T(8,128)(2,1)S(1)}, bf16[4,8,1056]{2,1,0:T(8,128)(2,1)S(1)}, u32[]{:S(2)}, u32[]{:S(2)}) collective-permute-start(bf16[4,8,1056]{2,1,0:T(8,128)(2,1)S(1)} %get-tuple-element.19), channel_id=1, source_target_pairs={{0,32},{32,64},{64,96},{96,128},{128,160},{160,192},{192,224},{1,3... | collective-permute-start | bytes 202760 | tf_op jit(solution)/shard_map/ppermute | solution.py:43
  6.3 1.3 %collective-permute-start.1 = (bf16[4,8,1056]{2,1,0:T(8,128)(2,1)S(1)}, bf16[4,8,1056]{2,1,0:T(8,128)(2,1)S(1)}, u32[]{:S(2)}, u32[]{:S(2)}) collective-permute-start(bf16[4,8,1056]{2,1,0:T(8,128)(2,1)S(1)} %get-tuple-element.20), channel_id=1, source_target_pairs={{32,0},{64,32},{96,64},{128,96},{160,128},{192,160},{224,192},{33,... | collective-permute-start | bytes 202760 | tf_op jit(solution)/shard_map/ppermute | solution.py:44
  8.3 0.0 copy-done.4
  8.4 0.1 select_select_fusion.flag_ref
  8.4 0.1 select_maximum_fusion.pair_ref
  8.5 0.0 copy-start.1
  8.6 0.0 copy-start.3
  8.6 0.1 band.1.w_ref
  8.7 0.0 collective-permute-done.before_ref
  8.7 2.7 %collective-permute-done.1.after_ref = bf16[4,8,1056]{2,1,0:T(8,128)(2,1)S(1)} collective-permute-done((bf16[4,8,1056]{2,1,0:T(8,128)(2,1)S(1)}, bf16[4,8,1056]{2,1,0:T(8,128)(2,1)S(1)}, u32[]{:S(2)}, u32[]{:S(2)}) %collective-permute-start.1) | collective-permute-done | bytes 67616 | tf_op jit(solution)/shard_map/ppermute | solution.py:44
  11.4 0.0 copy-done.1
  11.4 0.0 copy-done.3
  11.4 0.2 mid.1
  11.6 0.0 copy-start.5
  11.6 1.3 %collective-permute-start.2 = (bf16[4,32,272]{2,1,0:T(8,128)(2,1)S(1)}, bf16[4,32,272]{2,1,0:T(8,128)(2,1)S(1)}, u32[]{:S(2)}, u32[]{:S(2)}) collective-permute-start(bf16[4,32,272]{2,1,0:T(8,128)(2,1)S(1)} %get-tuple-element.22), channel_id=1, source_target_pairs={{1,0},{2,1},{3,2},{4,3},{5,4},{6,5},{7,6},{8,7},{9,8},{10,9},{11,1... | collective-permute-start | bytes 208904 | tf_op jit(solution)/shard_map/ppermute | solution.py:317
  12.9 0.0 copy-done.5
  12.9 0.1 maximum_bitcast_fusion.bias_ref
  13.0 0.1 draw.1.t_ref
  13.1 3.8 %collective-permute-done.2.next_ref = bf16[4,32,272]{2,1,0:T(8,128)(2,1)S(1)} collective-permute-done((bf16[4,32,272]{2,1,0:T(8,128)(2,1)S(1)}, bf16[4,32,272]{2,1,0:T(8,128)(2,1)S(1)}, u32[]{:S(2)}, u32[]{:S(2)}) %collective-permute-start.2) | collective-permute-done | bytes 69664 | tf_op jit(solution)/shard_map/ppermute | solution.py:317
  16.9 1.4 %up.1 = (f32[4,24,16]{2,1,0:T(8,128)S(1)}, f32[4,24,16]{2,1,0:T(8,128)S(1)}, bf16[64,1280]{1,0:T(8,128)(2,1)S(1)}, bf16[64,252]{1,0:T(8,128)(2,1)S(1)}, f32[1,1280]{1,0:T(1,128)S(1)}) custom-call(f32[8,128]{1,0:T(8,128)S(1)} %select_select_fusion.flag_ref, bf16[4,40,16]{2,1,0:T(8,128)(2,1)S(1)} %get-tuple-element.21.column_ref, ...), custom_call_target="tpu_custom_call" | custom-call | tf_op jit(solution)/shard_map/up/pallas_call | solution.py:25
  18.4 3.2 %collective-permute-start.3 = (f32[4,24,16]{2,1,0:T(8,128)S(1)}, f32[4,24,16]{2,1,0:T(8,128)S(1)}, u32[]{:S(2)}, u32[]{:S(2)}) collective-permute-start(f32[4,24,16]{2,1,0:T(8,128)S(1)} %get-tuple-element.24), channel_id=1, source_target_pairs={{0,1},{1,2},{2,3},{3,4},{4,5},{5,6},{6,7},{7,8},{8,9},{9,10},{10,1... | collective-permute-start | bytes 18440 | tf_op jit(solution)/shard_map/ppermute | solution.py:337
  21.6 1.2 %collective-permute-done.3.before_ref = f32[4,24,16]{2,1,0:T(8,128)S(1)} collective-permute-done((f32[4,24,16]{2,1,0:T(8,128)S(1)}, f32[4,24,16]{2,1,0:T(8,128)S(1)}, u32[]{:S(2)}, u32[]{:S(2)}) %collective-permute-start.3) | collective-permute-done | bytes 6176 | tf_op jit(solution)/shard_map/ppermute | solution.py:337
  22.7 1.0 %down.1 = (bf16[4,16,16]{2,1,0:T(8,128)(2,1)S(1)}, bf16[16,24,128]{2,1,0:T(8,128)(2,1)S(1)}) custom-call(f32[8,128]{1,0:T(8,128)S(1)} %select_select_fusion.flag_ref, f32[4,24,16]{2,1,0:T(8,128)S(1)} %get-tuple-element.23.part_ref, f32[4,24,16]{2,1,0:T(8,128)S(1)} %collective-permute-done.3.before_ref, bf16[4,16,16]{2,1,0:T(8,128)(2,1)S(1)} %copy-done.3, ...), custom_call_target="tpu_custom_call" | custom-call | tf_op jit(solution)/shard_map/down/pallas_call | solution.py:25
  23.7 20.6 %all_to_all.15.parts_ref = bf16[16,24,128]{2,1,0:T(8,128)(2,1)S(1)} all-to-all(bf16[16,24,128]{2,1,0:T(8,128)(2,1)S(1)} %get-tuple-element.28), channel_id=1, replica_groups=mesh['img'=2,'row_0'=2,'row_1'=4,'col_0'=4,'col_1'=8] {'img','col_1'}, dimensions={0} | all-to-all | bytes 196608 | tf_op jit(solution)/shard_map/all_to_all | solution.py:356
  44.3 23.6 %all_to_all.16.parts_ref = bf16[32,24,128]{2,1,0:T(8,128)(2,1)S(1)} all-to-all(bf16[32,24,128]{2,1,0:T(8,128)(2,1)S(1)} %spread.1), channel_id=1, replica_groups=mesh['img'=2,'row_0'=2,'row_1'=4,'col_0'=4,'col_1'=8] {'row_1','col_0','..., dimensions={0} | all-to-all | bytes 393216 | tf_op jit(solution)/shard_map/all_to_all | solution.py:356
  68.0 6.2 %all_to_all.17.halves_ref = f32[2,24,128]{2,1,0:T(8,128)S(1)} all-to-all(f32[2,24,128]{2,1,0:T(8,128)S(1)} %share.1), channel_id=1, replica_groups=mesh['img'=2,'row_0'=2,'row_1'=4,'col_0'=4,'col_1'=8] {'img'}, dimensions={0} | all-to-all | bytes 49152 | tf_op jit(solution)/shard_map/all_to_all | solution.py:362
  74.2 0.7 finish.1
  (7 shorter events, 0.1 us)
Async XLA Ops:
  0.6 0.9 %copy-start = (bf16[4,16,1024]{2,1,0:T(8,128)(2,1)S(1)}, bf16[4,16,1024]{2,1,0:T(8,128)(2,1)}, u32[]{:S(2)}) copy-start(bf16[4,16,1024]{2,1,0:T(8,128)(2,1)} %noise_ref.5) | copy-start | bytes 393220
  1.5 0.7 copy-start.2
  2.3 6.0 %copy-start.4 = (bf16[64,9,9]{0,2,1:T(8,128)(2,1)S(1)}, bf16[64,9,9]{0,2,1:T(8,128)(2,1)}, u32[]{:S(2)}) copy-start(bf16[64,9,9]{0,2,1:T(8,128)(2,1)} %param.6) | copy-start | bytes 31108
  2.4 6.3 %collective-permute-start = (bf16[4,8,1056]{2,1,0:T(8,128)(2,1)S(1)}, bf16[4,8,1056]{2,1,0:T(8,128)(2,1)S(1)}, u32[]{:S(2)}, u32[]{:S(2)}) collective-permute-start(bf16[4,8,1056]{2,1,0:T(8,128)(2,1)S(1)} %get-tuple-element.19), channel_id=1, source_target_pairs={{0,32},{32,64},{64,96},{96,128},{128,160},{160,192},{192,224},{1,3... | collective-permute-start | bytes 202760 | tf_op jit(solution)/shard_map/ppermute | solution.py:43
  6.3 5.1 %collective-permute-start.1 = (bf16[4,8,1056]{2,1,0:T(8,128)(2,1)S(1)}, bf16[4,8,1056]{2,1,0:T(8,128)(2,1)S(1)}, u32[]{:S(2)}, u32[]{:S(2)}) collective-permute-start(bf16[4,8,1056]{2,1,0:T(8,128)(2,1)S(1)} %get-tuple-element.20), channel_id=1, source_target_pairs={{32,0},{64,32},{96,64},{128,96},{160,128},{192,160},{224,192},{33,... | collective-permute-start | bytes 202760 | tf_op jit(solution)/shard_map/ppermute | solution.py:44
  8.5 2.9 %copy-start.1 = (bf16[4,16,1024]{2,1,0:T(8,128)(2,1)S(1)}, bf16[4,16,1024]{2,1,0:T(8,128)(2,1)}, u32[]{:S(2)}) copy-start(bf16[4,16,1024]{2,1,0:T(8,128)(2,1)} %noise_ref.5) | copy-start | bytes 393220
  8.6 2.8 %copy-start.3 = (bf16[4,16,16]{2,1,0:T(8,128)(2,1)S(1)}, bf16[4,16,16]{2,1,0:T(8,128)(2,1)}, u32[]{:S(2)}) copy-start(bf16[4,16,16]{2,1,0:T(8,128)(2,1)} %vis_ref.5) | copy-start | bytes 6148
  11.6 1.3 %copy-start.5 = (f32[64]{0:T(128)S(1)}, f32[64]{0:T(128)}, u32[]{:S(2)}) copy-start(f32[64]{0:T(128)} %param.7) | copy-start | bytes 772
  11.6 5.4 %collective-permute-start.2 = (bf16[4,32,272]{2,1,0:T(8,128)(2,1)S(1)}, bf16[4,32,272]{2,1,0:T(8,128)(2,1)S(1)}, u32[]{:S(2)}, u32[]{:S(2)}) collective-permute-start(bf16[4,32,272]{2,1,0:T(8,128)(2,1)S(1)} %get-tuple-element.22), channel_id=1, source_target_pairs={{1,0},{2,1},{3,2},{4,3},{5,4},{6,5},{7,6},{8,7},{9,8},{10,9},{11,1... | collective-permute-start | bytes 208904 | tf_op jit(solution)/shard_map/ppermute | solution.py:317
  18.4 4.4 %collective-permute-start.3 = (f32[4,24,16]{2,1,0:T(8,128)S(1)}, f32[4,24,16]{2,1,0:T(8,128)S(1)}, u32[]{:S(2)}, u32[]{:S(2)}) collective-permute-start(f32[4,24,16]{2,1,0:T(8,128)S(1)} %get-tuple-element.24), channel_id=1, source_target_pairs={{0,1},{1,2},{2,3},{3,4},{4,5},{5,6},{6,7},{7,8},{8,9},{9,10},{10,1... | collective-permute-start | bytes 18440 | tf_op jit(solution)/shard_map/ppermute | solution.py:337

commit v4 on v3

--- a/solution.py
+++ b/solution.py
@@ -9,17 +9,17 @@
 ROW = ("row_0", "row_1")
 COL = ("col_0", "col_1")
 LANES = 128
-GROUPS = (("img", "col_1"), ("row_1", "col_0", "row_0"))
+GROUPS = (("img", "row_1"), ("col_1",), ("row_0", "col_0"))
 INTERPRET = False
 GRANT = 8 << 20
 
 
-def call(kernel, out_shape, scratch, name, smem=()):
+def call(kernel, out_shape, scratch, name, left=()):
     outs = out_shape if isinstance(out_shape, (list, tuple)) else (out_shape,)
 
     def run(*args):
         specs = [
-            pl.BlockSpec(memory_space=pltpu.SMEM if at in smem else pltpu.VMEM)
+            pl.BlockSpec(memory_space=pltpu.HBM if at in left else pltpu.VMEM)
             for at in range(len(args))
         ]
         return pl.pallas_call(
@@ -34,6 +34,10 @@
         )(*args)
 
     return run
+
+
+def in_hbm(x):
+    return x if INTERPRET else pltpu.with_memory_space_constraint(x, pltpu.HBM)
 
 
 def edges(axis, tail, head):
@@ -68,7 +72,8 @@
     chunks, edge = units // LANES, extra // LANES
     count = side * side
     quarter = -(-count // 4)
-    part_rows = -(-(quarter + 2) // 8) * 8
+    half_rows = -(-(quarter + 2) // 8) * 8
+    part_rows = 2 * half_rows
     f32, bf16 = jnp.float32, jnp.bfloat16
     shape = jax.ShapeDtypeStruct
     scale = 1.0 / float(
@@ -81,18 +86,31 @@
                 [wide_ref[n, r : r + size, :] for r in range(side)], axis=1
             )
 
-    def pack_kernel(vis_ref, noise_ref, down_ref, up_ref):
+    def pack_kernel(vis_hbm, noise_hbm, down_ref, up_ref, vis_ref, sems):
+        moves = [
+            pltpu.make_async_copy(vis_hbm, vis_ref, sems.at[0]),
+            pltpu.make_async_copy(
+                noise_hbm.at[:, pl.ds(tile_rows - reach, reach), :], down_ref.at[:, :, pl.ds(0, own)], sems.at[1]
+            ),
+            pltpu.make_async_copy(
+                noise_hbm.at[:, pl.ds(0, reach), :], up_ref.at[:, :, pl.ds(0, own)], sems.at[2]
+            ),
+        ]
+        for move in moves:
+            move.start()
+        moves[0].wait()
+
         def beside(first, last, size):
             more = jnp.concatenate([last, jnp.zeros((size - last.shape[0], tile_cols), f32)], axis=0)
             return jnp.concatenate([first, more], axis=1).astype(bf16)
 
         for n in range(n_img):
             pixels = vis_ref[n].astype(f32)
-            down_ref[n, :, :own] = noise_ref[n, tile_rows - reach :, :]
             lowest = pixels[tile_rows - far :]
             down_ref[n, :, own:] = beside(lowest[:reach], lowest[reach:], reach)
-            up_ref[n, :, :own] = noise_ref[n, :reach, :]
             up_ref[n, :, own:] = beside(pixels[:reach], pixels[reach:far], reach)
+        for move in moves[1:]:
+            move.wait()
 
     def mid_kernel(vis_ref, noise_ref, before_ref, after_ref, column_ref, send_ref, col_ref):
         for n in range(n_img):
@@ -102,14 +120,12 @@
                 col_ref[at + reach : at + far, :] = pixels[: far - reach, tile_cols:]
             col_ref[far : far + tile_rows, :] = vis_ref[n].astype(f32)
             column_ref[n] = col_ref[...].astype(bf16)
-            send_ref[n, :reach, :extra] = before_ref[n, :, :extra]
-            send_ref[n, reach : reach + tile_rows, :extra] = noise_ref[n, :, :extra]
-            send_ref[n, reach + tile_rows :, :extra] = after_ref[n, :, :extra]
-            over = taller - tall
-            low = jnp.concatenate(
-                [col_ref[tall:, :reach], jnp.zeros((tall - over, reach), f32)], axis=0
-            )
-            send_ref[n, :, extra:] = jnp.concatenate([col_ref[:tall, :reach], low], axis=1).astype(bf16)
+            send_ref[n, :reach, :] = before_ref[n, :, :extra]
+            send_ref[n, reach : reach + tile_rows, :] = noise_ref[n, :, :extra]
+            send_ref[n, reach + tile_rows : tall, :] = after_ref[n, :, :extra]
+            blocks = [col_ref[at : at + reach, :reach] for at in range(0, taller, reach)]
+            blocks.append(jnp.zeros((reach, extra - taller), f32))
+            send_ref[n, tall:, :] = jnp.concatenate(blocks, axis=1).astype(bf16)
 
     def band_kernel(pair_ref, w_ref, wide_ref):
         wide_ref[...] = jnp.zeros_like(wide_ref)
@@ -135,8 +151,10 @@
     ):
         starts, goes_on = flag_ref[0:1, :], flag_ref[3:4, :]
         for n in range(n_img):
-            pixels = next_ref[n, :, extra:].astype(f32)
-            beyond = jnp.concatenate([pixels[:, :reach], pixels[: taller - tall, reach:]], axis=0)
+            pixels = next_ref[n, tall:, :].astype(f32)
+            beyond = jnp.concatenate(
+                [pixels[:, at : at + reach] for at in range(0, taller, reach)], axis=0
+            )
             img_ref[n] = jnp.concatenate(
                 [jnp.zeros((taller, margin), f32), column_ref[n].astype(f32), beyond], axis=1
             )
@@ -162,7 +180,7 @@
             hid_ref[:, at] = hidden
             if v >= chunks - edge:
                 far_at = slice(v * LANES - own, (v + 1) * LANES - own)
-                t = inverse(next_ref[:, :, far_at]).reshape(n_img * tall, LANES)
+                t = inverse(next_ref[:, :tall, far_at]).reshape(n_img * tall, LANES)
             else:
                 t = t_ref[:, :, at].reshape(n_img * tall, LANES)
             if v < edge:
@@ -173,13 +191,15 @@
         down_ref[...] = lax.dot_general(
             samp_ref[...], w_ref[...], (((1,), (1,)), ((), ())), preferred_element_type=f32
         )
+        shares = []
         for n in range(n_img):
             total = jnp.zeros((high, wide), f32)
             for r in range(side):
                 at = n * tall + reach - r
                 total = total + down_ref[at : at + high, r * wide : (r + 1) * wide]
             part_ref[n] = total[:, margin : margin + tile_cols]
-            send_ref[n] = total[:, wide - 2 * reach :]
+            shares.append(total[:, wide - 2 * reach :])
+        send_ref[...] = jnp.concatenate(shares, axis=1)
 
     def down_kernel(
         flag_ref, part_ref, before_ref, vis_ref, w_ref, bias_ref, prob_ref, a_ref, hid_ref,
@@ -197,7 +217,11 @@
         seen = jnp.zeros((tile_rows, tile_cols), f32)
         for n in range(n_img):
             total = jnp.concatenate(
-                [before_ref[n], jnp.zeros((high, wide - 2 * reach), f32)], axis=1
+                [
+                    before_ref[:, n * 2 * reach : (n + 1) * 2 * reach],
+                    jnp.zeros((high, wide - 2 * reach), f32),
+                ],
+                axis=1,
             ) + jnp.concatenate(
                 [jnp.zeros((high, reach), f32), part_ref[n], jnp.zeros((high, wide - reach - tile_cols), f32)],
                 axis=1,
@@ -240,49 +264,45 @@
             )
         hidden = hidden + pltpu.roll(hidden, channels, 1)
         lane = lax.broadcasted_iota(jnp.int32, (quarter, LANES), 1)
-        copies = pack_ref.shape[0] // 2
+        sum_ref[...] = jnp.zeros_like(sum_ref)
         for half, last in ((0, hidden), (1, jnp.broadcast_to(seen, (1, LANES)))):
-            at = 2 * half * quarter
-            sum_ref[...] = jnp.zeros_like(sum_ref)
-            sum_ref[:quarter, :] = jnp.where(
+            at, to = 2 * half * quarter, half * half_rows
+            sum_ref[to : to + quarter, :] = jnp.where(
                 lane < channels, cmb_ref[at : at + quarter, :], cmb_ref[at + quarter : at + 2 * quarter, :]
             )
-            packed = split(sum_ref, last)
-            for to in range(copies):
-                pack_ref[half * copies + to] = packed
-
-    def split(sum_ref, last):
-        sum_ref[quarter : quarter + 1, :] = last
-        sum_ref[quarter + 1 : quarter + 2, :] = last - last.astype(bf16).astype(f32)
-        return sum_ref[...].astype(bf16)
+            sum_ref[to + quarter : to + quarter + 1, :] = last
+        sent(sum_ref, pack_ref)
+
+    def sent(sum_ref, pack_ref):
+        for half in range(2):
+            at = half * half_rows + quarter
+            last = sum_ref[at : at + 1, :]
+            sum_ref[at + 1 : at + 2, :] = last - last.astype(bf16).astype(f32)
+        packed = sum_ref[...].astype(bf16)
+        for to in range(pack_ref.shape[0]):
+            pack_ref[to] = packed
 
     def added(parts_ref, sum_ref):
         sum_ref[...] = jnp.sum(parts_ref[...].astype(f32), axis=0)
-        return sum_ref[quarter : quarter + 1, :] + sum_ref[quarter + 1 : quarter + 2, :]
+        for half in range(2):
+            at = half * half_rows + quarter
+            sum_ref[at : at + 1, :] += sum_ref[at + 1 : at + 2, :]
 
     def spread_kernel(parts_ref, pack_ref, sum_ref):
-        packed = split(sum_ref, added(parts_ref, sum_ref))
-        for to in range(pack_ref.shape[0]):
-            pack_ref[to] = packed
-
-    def share_kernel(parts_ref, pack_ref, sum_ref):
-        last = added(parts_ref, sum_ref)
-        sum_ref[quarter : quarter + 1, :] = last
-        for to in range(pack_ref.shape[0]):
-            pack_ref[to] = sum_ref[...] * scale
-
-    def finish_kernel(halves_ref, recon_in_ref, recon_ref, grad_ref, hid_ref, seen_ref, flat_ref):
+        added(parts_ref, sum_ref)
+        sent(sum_ref, pack_ref)
+
+    def finish_kernel(parts_ref, recon_in_ref, recon_ref, grad_ref, hid_ref, seen_ref, sum_ref, flat_ref):
         recon_ref[...] = recon_in_ref[...]
-        for half in range(2):
-            for side_of in range(2):
-                at = (2 * half + side_of) * quarter
-                flat_ref[at : at + quarter, :] = halves_ref[
-                    half, :quarter, side_of * channels : (side_of + 1) * channels
-                ]
+        added(parts_ref, sum_ref)
+        sum_ref[...] = sum_ref[...] * scale
+        for part in range(4):
+            at, lane = part // 2 * half_rows, part % 2 * channels
+            flat_ref[part * quarter : (part + 1) * quarter, :] = sum_ref[at : at + quarter, lane : lane + channels]
         for r in range(side):
             grad_ref[r] = flat_ref[r * side : (r + 1) * side, :]
-        hid_ref[...] = halves_ref[0, quarter : quarter + 1, :channels]
-        seen_ref[...] = halves_ref[1, quarter : quarter + 1, :1]
+        hid_ref[...] = sum_ref[quarter : quarter + 1, :channels]
+        seen_ref[...] = sum_ref[half_rows + quarter : half_rows + quarter + 1, :1]
 
     taps_first = filters.astype(f32).transpose(1, 2, 0)
     pairs = jnp.concatenate(
@@ -301,14 +321,20 @@
         flags = jnp.where(line == at, jnp.asarray(value, f32), flags)
 
     payload = shape((n_img, reach, own + 2 * tile_cols), bf16)
-    downward, upward = call(pack_kernel, (payload, payload), [], "pack")(images, unit_noise)
+    downward, upward = call(
+        pack_kernel,
+        (payload, payload),
+        [pltpu.VMEM(images.shape, bf16), pltpu.SemaphoreType.DMA((3,))],
+        "pack",
+        left=(0, 1),
+    )(in_hbm(images), in_hbm(unit_noise))
     before, after = edges(ROW, downward, upward)
     (w,) = call(
         band_kernel, (shape((taps, units), bf16),), [pltpu.VMEM((taps, units), f32)], "band"
     )(pairs)
     column, leftward = call(
         mid_kernel,
-        (shape((n_img, taller, tile_cols), bf16), shape((n_img, tall, extra + 2 * reach), bf16)),
+        (shape((n_img, taller, tile_cols), bf16), shape((n_img, tall + reach, extra), bf16)),
         [pltpu.VMEM((taller, tile_cols), f32)],
         "mid",
     )(images, unit_noise, before, after)
@@ -320,7 +346,7 @@
         up_kernel,
         (
             shape((n_img, high, tile_cols), f32),
-            shape((n_img, high, 2 * reach), f32),
+            shape((high, n_img * 2 * reach), f32),
             shape((rows, units), bf16),
             shape((rows, taps), bf16),
             shape((1, units), f32),
@@ -358,8 +384,6 @@
             (pack,) = call(
                 spread_kernel, (shape((following, part_rows, LANES), bf16),), scratch, "spread"
             )(parts)
-    (pack,) = call(share_kernel, (shape((2, part_rows, LANES), f32),), scratch, "share")(parts)
-    halves = lax.all_to_all(pack, "img", 0, 0, tiled=True)
     recon, grad, hidden, seen = call(
         finish_kernel,
         (
@@ -368,9 +392,9 @@
             shape((1, channels), f32),
             shape((1, 1), f32),
         ),
-        [pltpu.VMEM((4 * quarter, channels), f32)],
+        scratch + [pltpu.VMEM((4 * quarter, channels), f32)],
         "finish",
-    )(halves, recon)
+    )(parts, recon)
     return (recon, grad.transpose(2, 0, 1), hidden[0], seen[0, 0])
 
 

time: 75.4 us -> 72.5 us (0.962)
  the two profiles are of different devices: /device:TPU:1 before, /device:TPU:2 now
where the time goes in v4:
time: 72.5 us; the launch traced here: 72.1 us
  blocking collectives  46.2 us (64%)
  starting transfers between devices  12.5 us (17%)
  waiting for transfers between devices  7.05 us (10%)
  Pallas kernels  4.6 us (6%)
  between operations  1.48 us (2%)
    all_to_all x3, blocking collectives, body(): parts = lax.all_to_all(pack, axes, 0, 0, tiled=True)  46.2 us
    ppermute x1, starting transfers between devices, edges(): lax.ppermute(head, axis, [((i + 1) % count, i) for i in range(ends)])  5.68 us
    ppermute x1, waiting for transfers between devices, body(): beyond = lax.ppermute(leftward, COL, [(i + 1, i) for i in range(steps)])  4.8 us
    pallas_call x9, Pallas kernels, run(): pl.pallas_call(kernel, out_shape=out_shape, in_specs=specs, out_specs=tup...  4.6 us
    ppermute x1, starting transfers between devices, edges(): lax.ppermute(tail, axis, [(i, (i + 1) % count) for i in range(ends)])  3.4 us
    ppermute x1, starting transfers between devices, body(): shares = lax.ppermute(rightward, COL, [(i, i + 1) for i in range(steps)])  2.08 us
  transfers between devices with their start and end apart: 4, of which 3 were waited for; matrix products, arithmetic and copies ran while one was open for 0% of the time, Pallas kernels for 0%

profile of v4, /device:TPU:2, one launch (start us, length us, event | category | flops | bytes accessed | tf_op | source)
XLA Modules:
  0.0 72.1 jit_solution(18074334400119092530)
XLA Ops:
  0.6 0.9 %pack.1 = (bf16[4,8,1056]{2,1,0:T(8,128)(2,1)S(1)}, bf16[4,8,1056]{2,1,0:T(8,128)(2,1)S(1)}) custom-call(bf16[4,16,16]{2,1,0:T(8,128)(2,1)} %vis_ref.3, bf16[4,16,1024]{2,1,0:T(8,128)(2,1)} %noise_ref.3), custom_call_target="tpu_custom_call" | custom-call | tf_op jit(solution)/shard_map/pack/pallas_call | solution.py:25
  1.6 0.0 copy-start.2
  1.6 3.4 %collective-permute-start = (bf16[4,8,1056]{2,1,0:T(8,128)(2,1)S(1)}, bf16[4,8,1056]{2,1,0:T(8,128)(2,1)S(1)}, u32[]{:S(2)}, u32[]{:S(2)}) collective-permute-start(bf16[4,8,1056]{2,1,0:T(8,128)(2,1)S(1)} %get-tuple-element.19), channel_id=1, source_target_pairs={{0,32},{32,64},{64,96},{96,128},{128,160},{160,192},{192,224},{1,3... | collective-permute-start | bytes 202760 | tf_op jit(solution)/shard_map/ppermute | solution.py:47
  5.0 5.7 %collective-permute-start.1 = (bf16[4,8,1056]{2,1,0:T(8,128)(2,1)S(1)}, bf16[4,8,1056]{2,1,0:T(8,128)(2,1)S(1)}, u32[]{:S(2)}, u32[]{:S(2)}) collective-permute-start(bf16[4,8,1056]{2,1,0:T(8,128)(2,1)S(1)} %get-tuple-element.20), channel_id=1, source_target_pairs={{32,0},{64,32},{96,64},{128,96},{160,128},{192,160},{224,192},{33,... | collective-permute-start | bytes 202760 | tf_op jit(solution)/shard_map/ppermute | solution.py:48
  11.4 0.0 copy-done.2
  11.4 0.1 select_select_fusion.flag_ref
  11.5 0.1 select_maximum_fusion.pair_ref
  11.6 0.0 copy-start
  11.6 0.0 copy-start.1
  11.6 0.1 band.1.w_ref
  11.8 0.0 collective-permute-done.before_ref
  11.8 0.9 %collective-permute-done.1.after_ref = bf16[4,8,1056]{2,1,0:T(8,128)(2,1)S(1)} collective-permute-done((bf16[4,8,1056]{2,1,0:T(8,128)(2,1)S(1)}, bf16[4,8,1056]{2,1,0:T(8,128)(2,1)S(1)}, u32[]{:S(2)}, u32[]{:S(2)}) %collective-permute-start.1) | collective-permute-done | bytes 67616 | tf_op jit(solution)/shard_map/ppermute | solution.py:48
  12.6 0.0 copy-done
  12.6 0.0 copy-done.1
  12.6 0.2 mid.1
  12.8 0.0 copy-start.3
  12.8 1.3 %collective-permute-start.2 = (bf16[4,40,256]{2,1,0:T(8,128)(2,1)S(1)}, bf16[4,40,256]{2,1,0:T(8,128)(2,1)S(1)}, u32[]{:S(2)}, u32[]{:S(2)}) collective-permute-start(bf16[4,40,256]{2,1,0:T(8,128)(2,1)S(1)} %get-tuple-element.22), channel_id=1, source_target_pairs={{1,0},{2,1},{3,2},{4,3},{5,4},{6,5},{7,6},{8,7},{9,8},{10,9},{11,1... | collective-permute-start | bytes 245768 | tf_op jit(solution)/shard_map/ppermute | solution.py:343
  14.1 0.0 copy-done.3
  14.1 0.1 maximum_bitcast_fusion.bias_ref
  14.2 0.1 draw.1.t_ref
  14.4 4.8 %collective-permute-done.2.next_ref = bf16[4,40,256]{2,1,0:T(8,128)(2,1)S(1)} collective-permute-done((bf16[4,40,256]{2,1,0:T(8,128)(2,1)S(1)}, bf16[4,40,256]{2,1,0:T(8,128)(2,1)S(1)}, u32[]{:S(2)}, u32[]{:S(2)}) %collective-permute-start.2) | collective-permute-done | bytes 81952 | tf_op jit(solution)/shard_map/ppermute | solution.py:343
  19.2 1.4 %up.1 = (f32[4,24,16]{2,1,0:T(8,128)S(1)}, f32[24,64]{1,0:T(8,128)S(1)}, bf16[64,1280]{1,0:T(8,128)(2,1)S(1)}, bf16[64,252]{1,0:T(8,128)(2,1)S(1)}, f32[1,1280]{1,0:T(1,128)S(1)}) custom-call(f32[8,128]{1,0:T(8,128)S(1)} %select_select_fusion.flag_ref, bf16[4,40,16]{2,1,0:T(8,128)(2,1)S(1)} %get-tuple-element.21.column_ref, ...), custom_call_target="tpu_custom_call" | custom-call | tf_op jit(solution)/shard_map/up/pallas_call | solution.py:25
  20.6 2.1 %collective-permute-start.3 = (f32[24,64]{1,0:T(8,128)S(1)}, f32[24,64]{1,0:T(8,128)S(1)}, u32[]{:S(2)}, u32[]{:S(2)}) collective-permute-start(f32[24,64]{1,0:T(8,128)S(1)} %get-tuple-element.24), channel_id=1, source_target_pairs={{0,1},{1,2},{2,3},{3,4},{4,5},{5,6},{6,7},{7,8},{8,9},{9,10},{10,1... | collective-permute-start | bytes 18440 | tf_op jit(solution)/shard_map/ppermute | solution.py:363
  22.7 1.4 %collective-permute-done.3.before_ref = f32[24,64]{1,0:T(8,128)S(1)} collective-permute-done((f32[24,64]{1,0:T(8,128)S(1)}, f32[24,64]{1,0:T(8,128)S(1)}, u32[]{:S(2)}, u32[]{:S(2)}) %collective-permute-start.3) | collective-permute-done | bytes 6176 | tf_op jit(solution)/shard_map/ppermute | solution.py:363
  24.1 1.0 %down.1 = (bf16[4,16,16]{2,1,0:T(8,128)(2,1)S(1)}, bf16[8,48,128]{2,1,0:T(8,128)(2,1)S(1)}) custom-call(f32[8,128]{1,0:T(8,128)S(1)} %select_select_fusion.flag_ref, f32[4,24,16]{2,1,0:T(8,128)S(1)} %get-tuple-element.23.part_ref, f32[24,64]{1,0:T(8,128)S(1)} %collective-permute-done.3.before_ref, bf16[4,16,16]{2,1,0:T(8,128)(2,1)S(1)} %copy-done.1, ...), custom_call_target="tpu_custom_call" | custom-call | tf_op jit(solution)/shard_map/down/pallas_call | solution.py:25
  25.0 11.5 %all_to_all.15.parts_ref = bf16[8,48,128]{2,1,0:T(8,128)(2,1)S(1)} all-to-all(bf16[8,48,128]{2,1,0:T(8,128)(2,1)S(1)} %get-tuple-element.28), channel_id=1, replica_groups=mesh['img'=2,'row_0'=2,'row_1'=4,'col_0'=4,'col_1'=8] {'img','row_1'}, dimensions={0} | all-to-all | bytes 196608 | tf_op jit(solution)/shard_map/all_to_all | solution.py:382
  36.6 17.6 %all_to_all.16.parts_ref = bf16[8,48,128]{2,1,0:T(8,128)(2,1)S(1)} all-to-all(bf16[8,48,128]{2,1,0:T(8,128)(2,1)S(1)} %spread.2), channel_id=1, replica_groups=mesh['img'=2,'row_0'=2,'row_1'=4,'col_0'=4,'col_1'=8] {'col_1'}, dimensions={0} | all-to-all | bytes 196608 | tf_op jit(solution)/shard_map/all_to_all | solution.py:382
  54.2 17.2 %all_to_all.17.parts_ref = bf16[8,48,128]{2,1,0:T(8,128)(2,1)S(1)} all-to-all(bf16[8,48,128]{2,1,0:T(8,128)(2,1)S(1)} %spread.3), channel_id=1, replica_groups=mesh['img'=2,'row_0'=2,'row_1'=4,'col_0'=4,'col_1'=8] {'row_0','col_0'}, dimensions={0} | all-to-all | bytes 196608 | tf_op jit(solution)/shard_map/all_to_all | solution.py:382
  71.4 0.7 %finish.1 = (bf16[4,16,16]{2,1,0:T(8,128)(2,1)}, f32[9,9,64]{2,1,0:T(8,128)}, f32[1,64]{1,0:T(1,128)}, f32[1,1]{1,0:T(1,128)}) custom-call(bf16[8,48,128]{2,1,0:T(8,128)(2,1)S(1)} %all_to_all.17.parts_ref, bf16[4,16,16]{2,1,0:T(8,128)(2,1)S(1)} %get-tuple-element.29.recon_in_ref), custom_call_target="tpu_custom_call" | custom-call | tf_op jit(solution)/shard_map/finish/pallas_call | solution.py:25
  (7 shorter events, 0.1 us)
Async XLA Ops:
  1.6 9.8 %copy-start.2 = (bf16[64,9,9]{0,2,1:T(8,128)(2,1)S(1)}, bf16[64,9,9]{0,2,1:T(8,128)(2,1)}, u32[]{:S(2)}) copy-start(bf16[64,9,9]{0,2,1:T(8,128)(2,1)} %param.6) | copy-start | bytes 31108
  1.6 10.2 %collective-permute-start = (bf16[4,8,1056]{2,1,0:T(8,128)(2,1)S(1)}, bf16[4,8,1056]{2,1,0:T(8,128)(2,1)S(1)}, u32[]{:S(2)}, u32[]{:S(2)}) collective-permute-start(bf16[4,8,1056]{2,1,0:T(8,128)(2,1)S(1)} %get-tuple-element.19), channel_id=1, source_target_pairs={{0,32},{32,64},{64,96},{96,128},{128,160},{160,192},{192,224},{1,3... | collective-permute-start | bytes 202760 | tf_op jit(solution)/shard_map/ppermute | solution.py:47
  5.0 7.7 %collective-permute-start.1 = (bf16[4,8,1056]{2,1,0:T(8,128)(2,1)S(1)}, bf16[4,8,1056]{2,1,0:T(8,128)(2,1)S(1)}, u32[]{:S(2)}, u32[]{:S(2)}) collective-permute-start(bf16[4,8,1056]{2,1,0:T(8,128)(2,1)S(1)} %get-tuple-element.20), channel_id=1, source_target_pairs={{32,0},{64,32},{96,64},{128,96},{160,128},{192,160},{224,192},{33,... | collective-permute-start | bytes 202760 | tf_op jit(solution)/shard_map/ppermute | solution.py:48
  11.6 1.0 %copy-start = (bf16[4,16,1024]{2,1,0:T(8,128)(2,1)S(1)}, bf16[4,16,1024]{2,1,0:T(8,128)(2,1)}, u32[]{:S(2)}) copy-start(bf16[4,16,1024]{2,1,0:T(8,128)(2,1)} %noise_ref.3) | copy-start | bytes 393220
  11.6 1.0 %copy-start.1 = (bf16[4,16,16]{2,1,0:T(8,128)(2,1)S(1)}, bf16[4,16,16]{2,1,0:T(8,128)(2,1)}, u32[]{:S(2)}) copy-start(bf16[4,16,16]{2,1,0:T(8,128)(2,1)} %vis_ref.3) | copy-start | bytes 6148
  12.8 1.3 %copy-start.3 = (f32[64]{0:T(128)S(1)}, f32[64]{0:T(128)}, u32[]{:S(2)}) copy-start(f32[64]{0:T(128)} %param.7) | copy-start | bytes 772
  12.8 6.3 %collective-permute-start.2 = (bf16[4,40,256]{2,1,0:T(8,128)(2,1)S(1)}, bf16[4,40,256]{2,1,0:T(8,128)(2,1)S(1)}, u32[]{:S(2)}, u32[]{:S(2)}) collective-permute-start(bf16[4,40,256]{2,1,0:T(8,128)(2,1)S(1)} %get-tuple-element.22), channel_id=1, source_target_pairs={{1,0},{2,1},{3,2},{4,3},{5,4},{6,5},{7,6},{8,7},{9,8},{10,9},{11,1... | collective-permute-start | bytes 245768 | tf_op jit(solution)/shard_map/ppermute | solution.py:343
  20.6 3.5 %collective-permute-start.3 = (f32[24,64]{1,0:T(8,128)S(1)}, f32[24,64]{1,0:T(8,128)S(1)}, u32[]{:S(2)}, u32[]{:S(2)}) collective-permute-start(f32[24,64]{1,0:T(8,128)S(1)} %get-tuple-element.24), channel_id=1, source_target_pairs={{0,1},{1,2},{2,3},{3,4},{4,5},{5,6},{6,7},{7,8},{8,9},{9,10},{10,1... | collective-permute-start | bytes 18440 | tf_op jit(solution)/shard_map/ppermute | solution.py:363

commit v5 on v4

v5 whole, which is shorter than its diff:
```python
import jax
import jax.numpy as jnp
from jax import lax
from jax.experimental import pallas as pl
from jax.experimental.pallas import tpu as pltpu
from jax.sharding import Mesh
from jax.sharding import PartitionSpec as P

ROW = ("row_0", "row_1")
COL = ("col_0", "col_1", "col_2", "col_3")
LANES = 128
GROUPS = (("img", "row_1"), ("col_3", "col_2", "col_1"), ("row_0", "col_0"))
INTERPRET = False
SMALL = 0.0625
GRANT = 8 << 20


def call(kernel, out_shape, scratch, name, left=()):
    outs = out_shape if isinstance(out_shape, (list, tuple)) else (out_shape,)

    def run(*args):
        specs = [
            pl.BlockSpec(memory_space=pltpu.HBM if at in left else pltpu.VMEM)
            for at in range(len(args))
        ]
        return pl.pallas_call(
            kernel,
            out_shape=out_shape,
            in_specs=specs,
            out_specs=tuple(pl.BlockSpec(memory_space=pltpu.VMEM) for _ in outs),
            scratch_shapes=scratch,
            compiler_params=pltpu.CompilerParams(vmem_limit_bytes=GRANT),
            name=name,
            interpret=INTERPRET,
        )(*args)

    return run


def skipping(ref, lead, start, size):
    if INTERPRET:
        return ref[lead][start : start + 2 * size - 1 : 2]
    return ref[lead, pl.ds(start, size, 2), :]


def put_skipping(ref, lead, start, value):
    if INTERPRET:
        for at in range(value.shape[0]):
            ref[lead, start + 2 * at, :] = value[at]
    else:
        ref[lead, pl.ds(start, value.shape[0], 2), :] = value


def in_hbm(x):
    return x if INTERPRET else pltpu.with_memory_space_constraint(x, pltpu.HBM)


def edges(axis, tail, head):
    count = lax.axis_size(axis)
    ends = count - 1
    return (
        lax.ppermute(tail, axis, [(i, (i + 1) % count) for i in range(ends)]),
        lax.ppermute(head, axis, [((i + 1) % count, i) for i in range(ends)]),
    )


def body(images, filters, hidden_bias, visible_unit_bias, unit_noise):
    n_img, tile_rows, tile_cols = images.shape
    channels, side, _ = filters.shape
    margin = side // 2
    reach = 2 * margin
    far = 3 * margin
    high, wide = tile_rows + 2 * margin, tile_cols + 2 * margin
    tall, taller = tile_rows + 2 * reach, tile_rows + 2 * far
    broad = tile_cols + 2 * far
    rows, every = n_img * tile_rows, n_img * tall
    own, part = tile_cols * channels, reach * channels
    taps = side * wide
    chunks, edge = own // LANES, part // LANES
    few, some = tile_rows // 2, reach // 2
    count = side * side
    quarter = -(-count // 4)
    half_rows = -(-(quarter + 2) // 8) * 8
    part_rows = 2 * half_rows
    f32, bf16 = jnp.float32, jnp.bfloat16
    shape = jax.ShapeDtypeStruct
    scale = 1.0 / float(
        rows * tile_cols * lax.axis_size("img") * lax.axis_size(ROW) * lax.axis_size(COL)
    )

    def slots(odd, n):
        at = odd * (every // 2)
        beyond = at + n_img * few + n * reach
        return at + n * few, beyond, beyond + some

    def windows(ref, n, row, size, left):
        return jnp.concatenate(
            [skipping(ref, n, row + r, size)[:, left : left + wide] for r in range(side)], axis=1
        )

    def pack_kernel(vis_hbm, noise_hbm, down_ref, up_ref, vis_ref, sems):
        moves = [
            pltpu.make_async_copy(vis_hbm, vis_ref, sems.at[0]),
            pltpu.make_async_copy(
                noise_hbm.at[:, pl.ds(tile_rows - reach, reach), :], down_ref.at[:, :, pl.ds(0, own)], sems.at[1]
            ),
            pltpu.make_async_copy(
                noise_hbm.at[:, pl.ds(0, reach), :], up_ref.at[:, :, pl.ds(0, own)], sems.at[2]
            ),
        ]
        for move in moves:
            move.start()
        moves[0].wait()

        def beside(first, last, size):
            more = jnp.concatenate([last, jnp.zeros((size - last.shape[0], tile_cols), f32)], axis=0)
            return jnp.concatenate([first, more], axis=1).astype(bf16)

        for n in range(n_img):
            pixels = vis_ref[n].astype(f32)
            lowest = pixels[tile_rows - far :]
            down_ref[n, :, own:] = beside(lowest[:reach], lowest[reach:], reach)
            up_ref[n, :, own:] = beside(pixels[:reach], pixels[reach:far], reach)
        for move in moves[1:]:
            move.wait()

    def mid_kernel(vis_ref, noise_ref, before_ref, after_ref, column_ref, left_ref, right_ref):
        firsts, lasts = [], []
        for n in range(n_img):
            for at, payload in ((0, before_ref), (far + tile_rows, after_ref)):
                pixels = payload[n, :, own:].astype(f32)
                column_ref[n, at : at + reach, :] = pixels[:, :tile_cols]
                column_ref[n, at + reach : at + far, :] = pixels[: far - reach, tile_cols:]
            column_ref[n, far : far + tile_rows, :] = vis_ref[n].astype(f32)
            for ref, lane in ((left_ref, 0), (right_ref, own - part)):
                at = n * tall
                ref[at : at + reach, :] = before_ref[n, :, lane : lane + part]
                ref[at + reach : at + reach + tile_rows, :] = noise_ref[n, :, lane : lane + part]
                ref[at + reach + tile_rows : at + tall, :] = after_ref[n, :, lane : lane + part]
            for at in range(0, taller, reach):
                block = column_ref[n, at : at + reach, :]
                firsts.append(block[:, :far])
                lasts.append(block[:, tile_cols - far :])
        for ref, blocks in ((left_ref, firsts), (right_ref, lasts)):
            gap = jnp.zeros((reach, part - len(blocks) * far), f32)
            ref[every:, :] = jnp.concatenate(blocks + [gap], axis=1).astype(bf16)

    def band_kernel(pair_ref, w_ref, wide_ref):
        wide_ref[...] = jnp.zeros_like(wide_ref)
        for r in range(side):
            block = pair_ref[r]
            for v in range(chunks):
                wide_ref[pl.ds(r * wide + 2 * v, side + 1), pl.ds(v * LANES, LANES)] = block
        w_ref[...] = wide_ref[...].astype(bf16)

    def inverse(u):
        u = u.astype(f32)
        return jnp.where(u > 0.0, 1.0 / jnp.log(u), 0.0)

    def placed(tmp_ref, out_ref, n, lane):
        for odd in range(2):
            mine, above, below = slots(odd, n)
            for v in range(tmp_ref.shape[0]):
                lanes = slice(lane + v * LANES, lane + (v + 1) * LANES)
                line = skipping(tmp_ref, v, odd, tall // 2)
                out_ref[above : above + some, lanes] = line[:some]
                out_ref[mine : mine + few, lanes] = line[some : some + few]
                out_ref[below : below + some, lanes] = line[some + few :]

    def draw_kernel(noise_ref, before_ref, after_ref, t_ref, tmp_ref):
        for n in range(n_img):
            for v in range(chunks):
                at = slice(v * LANES, (v + 1) * LANES)
                tmp_ref[v, :reach, :] = inverse(before_ref[n, :, at])
                tmp_ref[v, reach : reach + tile_rows, :] = inverse(noise_ref[n, :, at])
                tmp_ref[v, reach + tile_rows :, :] = inverse(after_ref[n, :, at])
            placed(tmp_ref, t_ref, n, 0)

    def odds(even, odd):
        even, odd = even * SMALL, odd * SMALL
        total = even + odd
        total = total + pltpu.roll(total, channels, 1)
        share = 1.0 / (SMALL + total)
        return even * share, odd * share

    def main_kernel(
        flag_ref, column_ref, before_ref, after_ref, w_ref, t_ref, bias_ref, vis_ref,
        recon_ref, pack_ref,
        img_ref, col_ref, samp_ref, edge_ref, tmp_ref, back_ref, a2_ref, p2_ref, g_ref, cmb_ref, sum_ref,
    ):
        half = every // 2
        mine = n_img * few
        for n in range(n_img):
            strips = []
            for ref in (before_ref, after_ref):
                at = n * (taller // reach) * far
                strips.append(
                    jnp.concatenate(
                        [
                            ref[every:, at + k * far : at + (k + 1) * far].astype(f32)
                            for k in range(taller // reach)
                        ],
                        axis=0,
                    )
                )
            img_ref[n, :, :broad] = jnp.concatenate([strips[0], column_ref[n], strips[1]], axis=1)
        for at, ref in ((0, before_ref), (1, after_ref)):
            for n in range(n_img):
                for v in range(edge):
                    tmp_ref[v] = inverse(ref[n * tall : (n + 1) * tall, v * LANES : (v + 1) * LANES])
                placed(tmp_ref, edge_ref, n, at * part)
        hidden = jnp.zeros((1, LANES), f32)
        for block in range(2):
            for odd in range(2):
                for n in range(n_img):
                    own_at, above, below = slots(odd, n)
                    line = windows(img_ref, n, odd, tall // 2, block * tile_cols)
                    col_ref[above : above + some, :] = line[:some]
                    col_ref[own_at : own_at + few, :] = line[some : some + few]
                    col_ref[below : below + some, :] = line[some + few :]
            a = col_ref[...].astype(bf16)
            for v in range(chunks):
                at = slice(v * LANES, (v + 1) * LANES)
                act = jnp.dot(a, w_ref[:, at], preferred_element_type=f32) + bias_ref[...]
                lift = jnp.exp(act)
                first, second = lift[:half], lift[half:]
                inner = v >= edge if block == 0 else v < edge
                if inner:
                    to = (v - edge if block == 0 else v + edge) * LANES
                    probs = odds(first[:mine], second[:mine])
                    for odd in range(2):
                        p2_ref[odd * mine : (odd + 1) * mine, to : to + LANES] = probs[odd].astype(bf16)
                        hidden = hidden + jnp.sum(probs[odd], axis=0, keepdims=True)
                    t = t_ref[:, to : to + LANES]
                else:
                    to = (v if block == 0 else v) * LANES
                    t = edge_ref[:, to : to + LANES]
                cold = jnp.where(t == 0.0, 0.0, lift * t)
                cold = cold * cold
                samples = odds(cold[:half], cold[half:])
                for odd in range(2):
                    at_row = block * every + odd * half
                    samp_ref[at_row : at_row + half, at] = samples[odd].astype(bf16)
        for odd in range(2):
            for n in range(n_img):
                at = (odd * n_img + n) * few
                a2_ref[at : at + few, :] = windows(img_ref, n, reach + odd, few, reach).astype(bf16)

        down = lax.dot_general(
            samp_ref[...], w_ref[...], (((1,), (1,)), ((), ())), preferred_element_type=f32
        )
        down = jnp.concatenate([down, jnp.zeros((2 * every, -taps % LANES), f32)], axis=1)
        for block in range(2):
            for odd in range(2):
                for n in range(n_img):
                    own_at, above, below = (block * every + at for at in slots(odd, n))
                    to = (block * n_img + n) * tall
                    line = jnp.concatenate(
                        [down[above : above + some], down[own_at : own_at + few], down[below : below + some]], axis=0
                    )
                    for v in range(back_ref.shape[0]):
                        put_skipping(back_ref, v, to + odd, line[:, v * LANES : (v + 1) * LANES])
        p = lax.broadcasted_iota(jnp.int32, (high, wide), 0)
        q = lax.broadcasted_iota(jnp.int32, (high, wide), 1)
        inside = (
            ((p >= margin) | (flag_ref[2:3, :wide] == 0.0))
            & ((p < margin + tile_rows) | (flag_ref[3:4, :wide] == 0.0))
            & ((q >= margin) | (flag_ref[0:1, :wide] == 0.0))
            & ((q < margin + tile_cols) | (flag_ref[1:2, :wide] == 0.0))
        )
        seen = jnp.zeros((tile_rows, tile_cols), f32)
        gap = jnp.zeros((high, reach), f32)
        for n in range(n_img):
            totals = []
            for block in range(2):
                total = jnp.zeros((high, wide), f32)
                for r in range(side):
                    at = (block * n_img + n) * tall + reach - r
                    lane, over = r * wide, max((r + 1) * wide - LANES, 0)
                    if lane < LANES < lane + wide:
                        piece = jnp.concatenate(
                            [back_ref[0, at : at + high, lane:], back_ref[1, at : at + high, :over]], axis=1
                        )
                    else:
                        lane %= LANES
                        piece = back_ref[int(over > 0), at : at + high, lane : lane + wide]
                    total = total + piece
                totals.append(total)
            total = jnp.concatenate([totals[0][:, reach:], gap], axis=1) + jnp.concatenate(
                [gap, totals[1][:, : wide - reach]], axis=1
            )
            recon = (total + flag_ref[4:5, :wide]).astype(bf16).astype(f32)
            img_ref[n, :high, :wide] = jnp.where(inside, recon, 0.0)
            middle = img_ref[n, margin : margin + tile_rows, margin : margin + tile_cols]
            recon_ref[n] = middle.astype(bf16)
            seen = seen + (vis_ref[n].astype(f32) - middle)
        seen = jnp.sum(seen, keepdims=True)

        for odd in range(2):
            for n in range(n_img):
                at = (odd * n_img + n) * few
                col_ref[at : at + few, :] = windows(img_ref, n, odd, few, 0)
        a = col_ref[:rows, :].astype(bf16)
        a2_ref[rows:, :] = -a
        for v in range(chunks):
            at = slice(v * LANES, (v + 1) * LANES)
            act = jnp.dot(a, w_ref[:, at], preferred_element_type=f32) + bias_ref[...]
            lift = jnp.exp(act)
            probs = odds(lift[:mine], lift[mine:])
            for odd in range(2):
                to = rows + odd * mine
                p2_ref[to : to + mine, at] = probs[odd].astype(bf16)
                hidden = hidden - jnp.sum(probs[odd], axis=0, keepdims=True)
        g_ref[...] = lax.dot_general(
            a2_ref[...], p2_ref[...], (((0,), (0,)), ((), ())), preferred_element_type=f32
        )
        lane = lax.broadcasted_iota(jnp.int32, (side, LANES), 1)
        cmb_ref[...] = jnp.zeros_like(cmb_ref)
        for r in range(side):
            acc = g_ref[pl.ds(r * wide, side + 1), pl.ds(0, LANES)]
            for v in range(1, chunks):
                acc = acc + g_ref[pl.ds(r * wide + 2 * v, side + 1), pl.ds(v * LANES, LANES)]
            turned = pltpu.roll(acc, channels, 1)
            cmb_ref[r * side : (r + 1) * side, :] = jnp.where(
                lane < channels, acc[:side] + turned[1 : side + 1], turned[:side] + acc[1 : side + 1]
            )
        hidden = hidden + pltpu.roll(hidden, channels, 1)
        lane = lax.broadcasted_iota(jnp.int32, (quarter, LANES), 1)
        sum_ref[...] = jnp.zeros_like(sum_ref)
        for half, last in ((0, hidden), (1, jnp.broadcast_to(seen, (1, LANES)))):
            at, to = 2 * half * quarter, half * half_rows
            sum_ref[to : to + quarter, :] = jnp.where(
                lane < channels, cmb_ref[at : at + quarter, :], cmb_ref[at + quarter : at + 2 * quarter, :]
            )
            sum_ref[to + quarter : to + quarter + 1, :] = last
        sent(sum_ref, pack_ref)

    def sent(sum_ref, pack_ref):
        for half in range(2):
            at = half * half_rows + quarter
            last = sum_ref[at : at + 1, :]
            sum_ref[at + 1 : at + 2, :] = last - last.astype(bf16).astype(f32)
        packed = sum_ref[...].astype(bf16)
        for to in range(pack_ref.shape[0]):
            pack_ref[to] = packed

    def added(parts_ref, sum_ref):
        sum_ref[...] = jnp.sum(parts_ref[...].astype(f32), axis=0)
        for half in range(2):
            at = half * half_rows + quarter
            sum_ref[at : at + 1, :] += sum_ref[at + 1 : at + 2, :]

    def spread_kernel(parts_ref, pack_ref, sum_ref):
        added(parts_ref, sum_ref)
        sent(sum_ref, pack_ref)

    def finish_kernel(parts_ref, recon_in_ref, recon_ref, grad_ref, hid_ref, seen_ref, sum_ref, flat_ref):
        recon_ref[...] = recon_in_ref[...]
        added(parts_ref, sum_ref)
        sum_ref[...] = sum_ref[...] * scale
        for part in range(4):
            at, lane = part // 2 * half_rows, part % 2 * channels
            flat_ref[part * quarter : (part + 1) * quarter, :] = sum_ref[at : at + quarter, lane : lane + channels]
        for r in range(side):
            grad_ref[r] = flat_ref[r * side : (r + 1) * side, :]
        hid_ref[...] = sum_ref[quarter : quarter + 1, :channels]
        seen_ref[...] = sum_ref[half_rows + quarter : half_rows + quarter + 1, :1]

    taps_first = filters.astype(f32).transpose(1, 2, 0)
    pairs = jnp.concatenate(
        [jnp.pad(taps_first, ((0, 0), (0, 1), (0, 0))), jnp.pad(taps_first, ((0, 0), (1, 0), (0, 0)))],
        axis=2,
    )
    bias = jnp.concatenate([hidden_bias, hidden_bias])[None]
    col_at, row_at = lax.axis_index(COL), lax.axis_index(ROW)
    first, last = col_at == 0, col_at == lax.axis_size(COL) - 1
    top, bottom = row_at == 0, row_at == lax.axis_size(ROW) - 1
    line = lax.broadcasted_iota(jnp.int32, (8, LANES), 0)
    flags = jnp.zeros((8, LANES), f32)
    for at, value in enumerate((first, last, top, bottom, visible_unit_bias)):
        flags = jnp.where(line == at, jnp.asarray(value, f32), flags)

    payload = shape((n_img, reach, own + 2 * tile_cols), bf16)
    downward, upward = call(
        pack_kernel,
        (payload, payload),
        [pltpu.VMEM(images.shape, bf16), pltpu.SemaphoreType.DMA((3,))],
        "pack",
        left=(0, 1),
    )(in_hbm(images), in_hbm(unit_noise))
    before, after = edges(ROW, downward, upward)
    (w,) = call(
        band_kernel, (shape((taps, own), bf16),), [pltpu.VMEM((taps, own), f32)], "band"
    )(pairs)
    sideways = shape((every + reach, part), bf16)
    column, leftward, rightward = call(
        mid_kernel, (shape((n_img, taller, tile_cols), f32), sideways, sideways), [], "mid"
    )(images, unit_noise, before, after)

    left, right = edges(COL, rightward, leftward)
    (t,) = call(
        draw_kernel, (shape((every, own), f32),), [pltpu.VMEM((chunks, tall, LANES), f32)], "draw"
    )(unit_noise, before, after)
    sizes = [lax.axis_size(axes) for axes in GROUPS]
    recon, pack = call(
        main_kernel,
        (shape(images.shape, bf16), shape((sizes[0], part_rows, LANES), bf16)),
        [
            pltpu.VMEM((n_img, taller, LANES), f32),
            pltpu.VMEM((every, taps), f32),
            pltpu.VMEM((2 * every, own), bf16),
            pltpu.VMEM((every, 2 * part), f32),
            pltpu.VMEM((edge, tall, LANES), f32),
            pltpu.VMEM((-(-taps // LANES), 2 * every, LANES), f32),
            pltpu.VMEM((2 * rows, taps), bf16),
            pltpu.VMEM((2 * rows, own), bf16),
            pltpu.VMEM((taps, own), f32),
            pltpu.VMEM((4 * quarter, LANES), f32),
            pltpu.VMEM((part_rows, LANES), f32),
        ],
        "main",
    )(flags, column, left, right, w, t, bias, images)

    scratch = [pltpu.VMEM((part_rows, LANES), f32)]
    for axes, following in zip(GROUPS, sizes[1:] + [None]):
        parts = lax.all_to_all(pack, axes, 0, 0, tiled=True)
        if following:
            (pack,) = call(
                spread_kernel, (shape((following, part_rows, LANES), bf16),), scratch, "spread"
            )(parts)
    recon, grad, hidden, seen = call(
        finish_kernel,
        (
            shape(images.shape, bf16),
            shape((side, side, channels), f32),
            shape((1, channels), f32),
            shape((1, 1), f32),
        ),
        scratch + [pltpu.VMEM((4 * quarter, channels), f32)],
        "finish",
    )(parts, recon)
    return (recon, grad.transpose(2, 0, 1), hidden[0], seen[0, 0])


def solution(mesh):
    split = Mesh(
        mesh.devices.reshape(mesh.shape["img"], 2, 4, 4, 2, 2, 2),
        ("img",) + ROW + COL,
    )
    placed = (P("img", ROW, COL), P(), P(), P(), P("img", ROW, COL))
    return jax.shard_map(
        body,
        mesh=split,
        in_specs=placed,
        out_specs=(P("img", ROW, COL), P(), P(), P()),
        check_vma=False,
    )
```

time: 72.5 us -> 70.1 us (0.967)
  blocking collectives: 46.2 us -> 44.2 us
  waiting for transfers between devices: 7.05 us -> 5.73 us
    ppermute x2 -> x0, waiting for transfers between devices: 6.19 us -> none  [the longest x1 4.8 us: body(): beyond = lax.ppermute(leftward, COL, [(i + 1, i) for i in range(steps)])]
    ppermute x1 -> x2, waiting for transfers between devices: 0.86 us -> 5.49 us  [edges(): lax.ppermute(head, axis, [((i + 1) % count, i) for i in range(ends)])]
    ppermute x2 -> x0, starting transfers between devices: 3.37 us -> none  [the longest x1 2.08 us: body(): shares = lax.ppermute(rightward, COL, [(i, i + 1) for i in range(steps)])]
    ppermute x1 -> x2, starting transfers between devices: 3.4 us -> 5.62 us  [edges(): lax.ppermute(tail, axis, [(i, (i + 1) % count) for i in range(ends)])]
    all_to_all x3, blocking collectives: 46.2 us -> 44.2 us  [body(): parts = lax.all_to_all(pack, axes, 0, 0, tiled=True)]
    ppermute x1 -> x2, starting transfers between devices: 5.68 us -> 6.97 us  [edges(): lax.ppermute(head, axis, [((i + 1) % count, i) for i in range(ends)])]
    pallas_call x9 -> x8, Pallas kernels: 4.6 us -> 4.87 us  [run(): pl.pallas_call(kernel, out_shape=out_shape, in_specs=specs, out_specs=tup...]
where the time goes in v5:
time: 70.1 us; the launch traced here: 69.7 us
  blocking collectives  44.2 us (63%)
  starting transfers between devices  12.6 us (18%)
  waiting for transfers between devices  5.73 us (8%)
  Pallas kernels  4.87 us (7%)
  between operations  1.46 us (2%)
    all_to_all x3, blocking collectives, body(): parts = lax.all_to_all(pack, axes, 0, 0, tiled=True)  44.2 us
    ppermute x2, starting transfers between devices, edges(): lax.ppermute(head, axis, [((i + 1) % count, i) for i in range(ends)])  6.97 us
    ppermute x2, starting transfers between devices, edges(): lax.ppermute(tail, axis, [(i, (i + 1) % count) for i in range(ends)])  5.62 us
    ppermute x2, waiting for transfers between devices, edges(): lax.ppermute(head, axis, [((i + 1) % count, i) for i in range(ends)])  5.49 us
    pallas_call x8, Pallas kernels, run(): pl.pallas_call(kernel, out_shape=out_shape, in_specs=specs, out_specs=tup...  4.87 us
  transfers between devices with their start and end apart: 4, of which 3 were waited for; matrix products, arithmetic and copies ran while one was open for 0% of the time, Pallas kernels for 0%

profile of v5, /device:TPU:2, one launch (start us, length us, event | category | flops | bytes accessed | tf_op | source)
XLA Modules:
  0.0 69.7 jit_solution(17289180777258269488)
XLA Ops:
  0.6 0.0 copy-start.2
  0.6 0.9 %pack.1 = (bf16[4,8,1056]{2,1,0:T(8,128)(2,1)S(1)}, bf16[4,8,1056]{2,1,0:T(8,128)(2,1)S(1)}) custom-call(bf16[4,16,16]{2,1,0:T(8,128)(2,1)} %vis_ref.3, bf16[4,16,1024]{2,1,0:T(8,128)(2,1)} %noise_ref.3), custom_call_target="tpu_custom_call" | custom-call | tf_op jit(solution)/shard_map/pack/pallas_call | solution.py:26
  1.6 0.0 copy-start
  1.6 3.5 %collective-permute-start = (bf16[4,8,1056]{2,1,0:T(8,128)(2,1)S(1)}, bf16[4,8,1056]{2,1,0:T(8,128)(2,1)S(1)}, u32[]{:S(2)}, u32[]{:S(2)}) collective-permute-start(bf16[4,8,1056]{2,1,0:T(8,128)(2,1)S(1)} %get-tuple-element.15), channel_id=1, source_target_pairs={{0,32},{32,64},{64,96},{96,128},{128,160},{160,192},{192,224},{1,3... | collective-permute-start | bytes 202760 | tf_op jit(solution)/shard_map/ppermute | solution.py:62
  5.1 5.7 %collective-permute-start.1 = (bf16[4,8,1056]{2,1,0:T(8,128)(2,1)S(1)}, bf16[4,8,1056]{2,1,0:T(8,128)(2,1)S(1)}, u32[]{:S(2)}, u32[]{:S(2)}) collective-permute-start(bf16[4,8,1056]{2,1,0:T(8,128)(2,1)S(1)} %get-tuple-element.16), channel_id=1, source_target_pairs={{32,0},{64,32},{96,64},{128,96},{160,128},{192,160},{224,192},{33,... | collective-permute-start | bytes 202760 | tf_op jit(solution)/shard_map/ppermute | solution.py:63
  11.5 0.0 copy-done.2
  11.6 0.0 copy-start.1
  11.6 0.1 select_select_fusion.flag_ref
  11.6 0.0 collective-permute-done.before_ref
  11.7 1.1 %collective-permute-done.1.after_ref = bf16[4,8,1056]{2,1,0:T(8,128)(2,1)S(1)} collective-permute-done((bf16[4,8,1056]{2,1,0:T(8,128)(2,1)S(1)}, bf16[4,8,1056]{2,1,0:T(8,128)(2,1)S(1)}, u32[]{:S(2)}, u32[]{:S(2)}) %collective-permute-start.1) | collective-permute-done | bytes 67616 | tf_op jit(solution)/shard_map/ppermute | solution.py:63
  12.8 0.0 copy-done
  12.8 0.0 copy-done.1
  12.8 0.2 mid.1
  13.0 2.1 %collective-permute-start.2 = (bf16[136,512]{1,0:T(8,128)(2,1)S(1)}, bf16[136,512]{1,0:T(8,128)(2,1)S(1)}, u32[]{:S(2)}, u32[]{:S(2)}) collective-permute-start(bf16[136,512]{1,0:T(8,128)(2,1)S(1)} %get-tuple-element.18), channel_id=1, source_target_pairs={{0,1},{1,2},{2,3},{3,4},{4,5},{5,6},{6,7},{7,8},{8,9},{9,10},{10,1... | collective-permute-start | bytes 417800 | tf_op jit(solution)/shard_map/ppermute | solution.py:62
  15.1 1.3 %collective-permute-start.3 = (bf16[136,512]{1,0:T(8,128)(2,1)S(1)}, bf16[136,512]{1,0:T(8,128)(2,1)S(1)}, u32[]{:S(2)}, u32[]{:S(2)}) collective-permute-start(bf16[136,512]{1,0:T(8,128)(2,1)S(1)} %get-tuple-element.19), channel_id=1, source_target_pairs={{1,0},{2,1},{3,2},{4,3},{5,4},{6,5},{7,6},{8,7},{9,8},{10,9},{11,1... | collective-permute-start | bytes 417800 | tf_op jit(solution)/shard_map/ppermute | solution.py:63
  16.4 0.1 select_maximum_fusion.pair_ref
  16.4 0.0 copy-start.3
  16.5 0.1 band.1.w_ref
  16.6 0.5 copy-done.3
  17.1 0.1 maximum_bitcast_fusion.bias_ref
  17.2 0.2 draw.1.t_ref
  17.4 0.2 collective-permute-done.2.before_ref
  17.6 4.4 %collective-permute-done.3.after_ref = bf16[136,512]{1,0:T(8,128)(2,1)S(1)} collective-permute-done((bf16[136,512]{1,0:T(8,128)(2,1)S(1)}, bf16[136,512]{1,0:T(8,128)(2,1)S(1)}, u32[]{:S(2)}, u32[]{:S(2)}) %collective-permute-start.3) | collective-permute-done | bytes 139296 | tf_op jit(solution)/shard_map/ppermute | solution.py:63
  22.0 2.6 %main.1 = (bf16[4,16,16]{2,1,0:T(8,128)(2,1)S(1)}, bf16[8,48,128]{2,1,0:T(8,128)(2,1)S(1)}) custom-call(f32[8,128]{1,0:T(8,128)S(1)} %select_select_fusion.flag_ref, f32[4,40,16]{2,1,0:T(8,128)S(1)} %get-tuple-element.17.column_ref, bf16[136,512]{1,0:T(8,128)(2,1)S(1)} %collective-permute-done.2.before_ref, ...), custom_call_target="tpu_custom_call" | custom-call | tf_op jit(solution)/shard_map/main/pallas_call | solution.py:26
  24.7 11.5 %all_to_all.15.parts_ref = bf16[8,48,128]{2,1,0:T(8,128)(2,1)S(1)} all-to-all(bf16[8,48,128]{2,1,0:T(8,128)(2,1)S(1)} %get-tuple-element.20), channel_id=1, replica_groups=mesh['img'=2,'row_0'=2,'row_1'=4,'col_0'=4,'col_1'=2,'col_2'=2,'col_3'=2..., dimensions={0} | all-to-all | bytes 196608 | tf_op jit(solution)/shard_map/all_to_all | solution.py:426
  36.2 17.4 %all_to_all.16.parts_ref = bf16[8,48,128]{2,1,0:T(8,128)(2,1)S(1)} all-to-all(bf16[8,48,128]{2,1,0:T(8,128)(2,1)S(1)} %spread.2), channel_id=1, replica_groups=mesh['img'=2,'row_0'=2,'row_1'=4,'col_0'=4,'col_1'=2,'col_2'=2,'col_3'=2..., dimensions={0} | all-to-all | bytes 196608 | tf_op jit(solution)/shard_map/all_to_all | solution.py:426
  53.6 15.4 %all_to_all.17.parts_ref = bf16[8,48,128]{2,1,0:T(8,128)(2,1)S(1)} all-to-all(bf16[8,48,128]{2,1,0:T(8,128)(2,1)S(1)} %spread.3), channel_id=1, replica_groups=mesh['img'=2,'row_0'=2,'row_1'=4,'col_0'=4,'col_1'=2,'col_2'=2,'col_3'=2..., dimensions={0} | all-to-all | bytes 196608 | tf_op jit(solution)/shard_map/all_to_all | solution.py:426
  69.0 0.7 %finish.1 = (bf16[4,16,16]{2,1,0:T(8,128)(2,1)}, f32[9,9,64]{2,1,0:T(8,128)}, f32[1,64]{1,0:T(1,128)}, f32[1,1]{1,0:T(1,128)}) custom-call(bf16[8,48,128]{2,1,0:T(8,128)(2,1)S(1)} %all_to_all.17.parts_ref, bf16[4,16,16]{2,1,0:T(8,128)(2,1)S(1)} %get-tuple-element.21.recon_in_ref), custom_call_target="tpu_custom_call" | custom-call | tf_op jit(solution)/shard_map/finish/pallas_call | solution.py:26
  (6 shorter events, 0.1 us)
Async XLA Ops:
  0.6 10.9 %copy-start.2 = (bf16[64,9,9]{0,2,1:T(8,128)(2,1)S(1)}, bf16[64,9,9]{0,2,1:T(8,128)(2,1)}, u32[]{:S(2)}) copy-start(bf16[64,9,9]{0,2,1:T(8,128)(2,1)} %param.6) | copy-start | bytes 31108
  1.6 11.2 %copy-start = (bf16[4,16,1024]{2,1,0:T(8,128)(2,1)S(1)}, bf16[4,16,1024]{2,1,0:T(8,128)(2,1)}, u32[]{:S(2)}) copy-start(bf16[4,16,1024]{2,1,0:T(8,128)(2,1)} %noise_ref.3) | copy-start | bytes 393220
  1.6 10.1 %collective-permute-start = (bf16[4,8,1056]{2,1,0:T(8,128)(2,1)S(1)}, bf16[4,8,1056]{2,1,0:T(8,128)(2,1)S(1)}, u32[]{:S(2)}, u32[]{:S(2)}) collective-permute-start(bf16[4,8,1056]{2,1,0:T(8,128)(2,1)S(1)} %get-tuple-element.15), channel_id=1, source_target_pairs={{0,32},{32,64},{64,96},{96,128},{128,160},{160,192},{192,224},{1,3... | collective-permute-start | bytes 202760 | tf_op jit(solution)/shard_map/ppermute | solution.py:62
  5.1 7.7 %collective-permute-start.1 = (bf16[4,8,1056]{2,1,0:T(8,128)(2,1)S(1)}, bf16[4,8,1056]{2,1,0:T(8,128)(2,1)S(1)}, u32[]{:S(2)}, u32[]{:S(2)}) collective-permute-start(bf16[4,8,1056]{2,1,0:T(8,128)(2,1)S(1)} %get-tuple-element.16), channel_id=1, source_target_pairs={{32,0},{64,32},{96,64},{128,96},{160,128},{192,160},{224,192},{33,... | collective-permute-start | bytes 202760 | tf_op jit(solution)/shard_map/ppermute | solution.py:63
  11.6 1.2 %copy-start.1 = (bf16[4,16,16]{2,1,0:T(8,128)(2,1)S(1)}, bf16[4,16,16]{2,1,0:T(8,128)(2,1)}, u32[]{:S(2)}) copy-start(bf16[4,16,16]{2,1,0:T(8,128)(2,1)} %vis_ref.3) | copy-start | bytes 6148
  13.0 4.7 %collective-permute-start.2 = (bf16[136,512]{1,0:T(8,128)(2,1)S(1)}, bf16[136,512]{1,0:T(8,128)(2,1)S(1)}, u32[]{:S(2)}, u32[]{:S(2)}) collective-permute-start(bf16[136,512]{1,0:T(8,128)(2,1)S(1)} %get-tuple-element.18), channel_id=1, source_target_pairs={{0,1},{1,2},{2,3},{3,4},{4,5},{5,6},{6,7},{7,8},{8,9},{9,10},{10,1... | collective-permute-start | bytes 417800 | tf_op jit(solution)/shard_map/ppermute | solution.py:62
  15.1 6.9 %collective-permute-start.3 = (bf16[136,512]{1,0:T(8,128)(2,1)S(1)}, bf16[136,512]{1,0:T(8,128)(2,1)S(1)}, u32[]{:S(2)}, u32[]{:S(2)}) collective-permute-start(bf16[136,512]{1,0:T(8,128)(2,1)S(1)} %get-tuple-element.19), channel_id=1, source_target_pairs={{1,0},{2,1},{3,2},{4,3},{5,4},{6,5},{7,6},{8,7},{9,8},{10,9},{11,1... | collective-permute-start | bytes 417800 | tf_op jit(solution)/shard_map/ppermute | solution.py:63
  16.4 0.7 copy-start.3

commit v6 on v5

--- a/solution.py
+++ b/solution.py
@@ -9,7 +9,7 @@
 ROW = ("row_0", "row_1")
 COL = ("col_0", "col_1", "col_2", "col_3")
 LANES = 128
-GROUPS = (("img", "row_1"), ("col_3", "col_2", "col_1"), ("row_0", "col_0"))
+GROUPS = (("img", "row_1"), ("row_0", "col_0"), ("col_3", "col_2", "col_1"))
 INTERPRET = False
 SMALL = 0.0625
 GRANT = 8 << 20

time: 70.1 us -> 69.8 us (level)
  the two profiles are of different devices: /device:TPU:2 before, /device:TPU:8 now
where the time goes in v6:
time: 69.8 us; the launch traced here: 69.4 us
  blocking collectives  43.9 us (63%)
  starting transfers between devices  11.7 us (17%)
  waiting for transfers between devices  6.6 us (9%)
  Pallas kernels  4.86 us (7%)
  between operations  1.46 us (2%)
    all_to_all x3, blocking collectives, body(): parts = lax.all_to_all(pack, axes, 0, 0, tiled=True)  43.9 us
    ppermute x2, starting transfers between devices, edges(): lax.ppermute(tail, axis, [(i, (i + 1) % count) for i in range(ends)])  7.02 us
    ppermute x2, waiting for transfers between devices, edges(): lax.ppermute(head, axis, [((i + 1) % count, i) for i in range(ends)])  6.54 us
    pallas_call x8, Pallas kernels, run(): pl.pallas_call(kernel, out_shape=out_shape, in_specs=specs, out_specs=tup...  4.86 us
    ppermute x2, starting transfers between devices, edges(): lax.ppermute(head, axis, [((i + 1) % count, i) for i in range(ends)])  4.7 us
  transfers between devices with their start and end apart: 4, of which 3 were waited for; matrix products, arithmetic and copies ran while one was open for 0% of the time, Pallas kernels for 0%

profile of v6, /device:TPU:8, one launch (start us, length us, event | category | flops | bytes accessed | tf_op | source)
XLA Modules:
  0.0 69.4 jit_solution(6478609296983628310)
XLA Ops:
  0.6 0.0 copy-start.2
  0.6 0.9 %pack.1 = (bf16[4,8,1056]{2,1,0:T(8,128)(2,1)S(1)}, bf16[4,8,1056]{2,1,0:T(8,128)(2,1)S(1)}) custom-call(bf16[4,16,16]{2,1,0:T(8,128)(2,1)} %vis_ref.3, bf16[4,16,1024]{2,1,0:T(8,128)(2,1)} %noise_ref.3), custom_call_target="tpu_custom_call" | custom-call | tf_op jit(solution)/shard_map/pack/pallas_call | solution.py:26
  1.6 0.0 copy-start
  1.6 3.5 %collective-permute-start = (bf16[4,8,1056]{2,1,0:T(8,128)(2,1)S(1)}, bf16[4,8,1056]{2,1,0:T(8,128)(2,1)S(1)}, u32[]{:S(2)}, u32[]{:S(2)}) collective-permute-start(bf16[4,8,1056]{2,1,0:T(8,128)(2,1)S(1)} %get-tuple-element.15), channel_id=1, source_target_pairs={{0,32},{32,64},{64,96},{96,128},{128,160},{160,192},{192,224},{1,3... | collective-permute-start | bytes 202760 | tf_op jit(solution)/shard_map/ppermute | solution.py:62
  5.1 1.3 %collective-permute-start.1 = (bf16[4,8,1056]{2,1,0:T(8,128)(2,1)S(1)}, bf16[4,8,1056]{2,1,0:T(8,128)(2,1)S(1)}, u32[]{:S(2)}, u32[]{:S(2)}) collective-permute-start(bf16[4,8,1056]{2,1,0:T(8,128)(2,1)S(1)} %get-tuple-element.16), channel_id=1, source_target_pairs={{32,0},{64,32},{96,64},{128,96},{160,128},{192,160},{224,192},{33,... | collective-permute-start | bytes 202760 | tf_op jit(solution)/shard_map/ppermute | solution.py:63
  7.1 0.0 copy-done.2
  7.2 0.0 copy-start.1
  7.2 0.1 select_select_fusion.flag_ref
  7.3 0.0 collective-permute-done.before_ref
  7.3 4.1 %collective-permute-done.1.after_ref = bf16[4,8,1056]{2,1,0:T(8,128)(2,1)S(1)} collective-permute-done((bf16[4,8,1056]{2,1,0:T(8,128)(2,1)S(1)}, bf16[4,8,1056]{2,1,0:T(8,128)(2,1)S(1)}, u32[]{:S(2)}, u32[]{:S(2)}) %collective-permute-start.1) | collective-permute-done | bytes 67616 | tf_op jit(solution)/shard_map/ppermute | solution.py:63
  11.4 0.0 copy-done
  11.4 0.0 copy-done.1
  11.4 0.2 mid.1
  11.6 3.5 %collective-permute-start.2 = (bf16[136,512]{1,0:T(8,128)(2,1)S(1)}, bf16[136,512]{1,0:T(8,128)(2,1)S(1)}, u32[]{:S(2)}, u32[]{:S(2)}) collective-permute-start(bf16[136,512]{1,0:T(8,128)(2,1)S(1)} %get-tuple-element.18), channel_id=1, source_target_pairs={{0,1},{1,2},{2,3},{3,4},{4,5},{5,6},{6,7},{7,8},{8,9},{9,10},{10,1... | collective-permute-start | bytes 417800 | tf_op jit(solution)/shard_map/ppermute | solution.py:62
  15.1 3.4 %collective-permute-start.3 = (bf16[136,512]{1,0:T(8,128)(2,1)S(1)}, bf16[136,512]{1,0:T(8,128)(2,1)S(1)}, u32[]{:S(2)}, u32[]{:S(2)}) collective-permute-start(bf16[136,512]{1,0:T(8,128)(2,1)S(1)} %get-tuple-element.19), channel_id=1, source_target_pairs={{1,0},{2,1},{3,2},{4,3},{5,4},{6,5},{7,6},{8,7},{9,8},{10,9},{11,1... | collective-permute-start | bytes 417800 | tf_op jit(solution)/shard_map/ppermute | solution.py:63
  18.5 0.1 select_maximum_fusion.pair_ref
  18.6 0.0 copy-start.3
  18.6 0.1 band.1.w_ref
  18.7 0.5 copy-done.3
  19.2 0.1 maximum_bitcast_fusion.bias_ref
  19.3 0.2 draw.1.t_ref
  19.5 0.1 collective-permute-done.2.before_ref
  19.6 2.4 %collective-permute-done.3.after_ref = bf16[136,512]{1,0:T(8,128)(2,1)S(1)} collective-permute-done((bf16[136,512]{1,0:T(8,128)(2,1)S(1)}, bf16[136,512]{1,0:T(8,128)(2,1)S(1)}, u32[]{:S(2)}, u32[]{:S(2)}) %collective-permute-start.3) | collective-permute-done | bytes 139296 | tf_op jit(solution)/shard_map/ppermute | solution.py:63
  22.0 2.6 %main.1 = (bf16[4,16,16]{2,1,0:T(8,128)(2,1)S(1)}, bf16[8,48,128]{2,1,0:T(8,128)(2,1)S(1)}) custom-call(f32[8,128]{1,0:T(8,128)S(1)} %select_select_fusion.flag_ref, f32[4,40,16]{2,1,0:T(8,128)S(1)} %get-tuple-element.17.column_ref, bf16[136,512]{1,0:T(8,128)(2,1)S(1)} %collective-permute-done.2.before_ref, ...), custom_call_target="tpu_custom_call" | custom-call | tf_op jit(solution)/shard_map/main/pallas_call | solution.py:26
  24.6 12.1 %all_to_all.15.parts_ref = bf16[8,48,128]{2,1,0:T(8,128)(2,1)S(1)} all-to-all(bf16[8,48,128]{2,1,0:T(8,128)(2,1)S(1)} %get-tuple-element.20), channel_id=1, replica_groups=mesh['img'=2,'row_0'=2,'row_1'=4,'col_0'=4,'col_1'=2,'col_2'=2,'col_3'=2..., dimensions={0} | all-to-all | bytes 196608 | tf_op jit(solution)/shard_map/all_to_all | solution.py:426
  36.8 17.0 %all_to_all.16.parts_ref = bf16[8,48,128]{2,1,0:T(8,128)(2,1)S(1)} all-to-all(bf16[8,48,128]{2,1,0:T(8,128)(2,1)S(1)} %spread.2), channel_id=1, replica_groups=mesh['img'=2,'row_0'=2,'row_1'=4,'col_0'=4,'col_1'=2,'col_2'=2,'col_3'=2..., dimensions={0} | all-to-all | bytes 196608 | tf_op jit(solution)/shard_map/all_to_all | solution.py:426
  53.9 14.7 %all_to_all.17.parts_ref = bf16[8,48,128]{2,1,0:T(8,128)(2,1)S(1)} all-to-all(bf16[8,48,128]{2,1,0:T(8,128)(2,1)S(1)} %spread.3), channel_id=1, replica_groups=mesh['img'=2,'row_0'=2,'row_1'=4,'col_0'=4,'col_1'=2,'col_2'=2,'col_3'=2..., dimensions={0} | all-to-all | bytes 196608 | tf_op jit(solution)/shard_map/all_to_all | solution.py:426
  68.6 0.7 %finish.1 = (bf16[4,16,16]{2,1,0:T(8,128)(2,1)}, f32[9,9,64]{2,1,0:T(8,128)}, f32[1,64]{1,0:T(1,128)}, f32[1,1]{1,0:T(1,128)}) custom-call(bf16[8,48,128]{2,1,0:T(8,128)(2,1)S(1)} %all_to_all.17.parts_ref, bf16[4,16,16]{2,1,0:T(8,128)(2,1)S(1)} %get-tuple-element.21.recon_in_ref), custom_call_target="tpu_custom_call" | custom-call | tf_op jit(solution)/shard_map/finish/pallas_call | solution.py:26
  (6 shorter events, 0.1 us)
Async XLA Ops:
  0.6 6.5 %copy-start.2 = (bf16[64,9,9]{0,2,1:T(8,128)(2,1)S(1)}, bf16[64,9,9]{0,2,1:T(8,128)(2,1)}, u32[]{:S(2)}) copy-start(bf16[64,9,9]{0,2,1:T(8,128)(2,1)} %param.6) | copy-start | bytes 31108
  1.6 9.8 %copy-start = (bf16[4,16,1024]{2,1,0:T(8,128)(2,1)S(1)}, bf16[4,16,1024]{2,1,0:T(8,128)(2,1)}, u32[]{:S(2)}) copy-start(bf16[4,16,1024]{2,1,0:T(8,128)(2,1)} %noise_ref.3) | copy-start | bytes 393220
  1.6 5.7 %collective-permute-start = (bf16[4,8,1056]{2,1,0:T(8,128)(2,1)S(1)}, bf16[4,8,1056]{2,1,0:T(8,128)(2,1)S(1)}, u32[]{:S(2)}, u32[]{:S(2)}) collective-permute-start(bf16[4,8,1056]{2,1,0:T(8,128)(2,1)S(1)} %get-tuple-element.15), channel_id=1, source_target_pairs={{0,32},{32,64},{64,96},{96,128},{128,160},{160,192},{192,224},{1,3... | collective-permute-start | bytes 202760 | tf_op jit(solution)/shard_map/ppermute | solution.py:62
  5.1 6.2 %collective-permute-start.1 = (bf16[4,8,1056]{2,1,0:T(8,128)(2,1)S(1)}, bf16[4,8,1056]{2,1,0:T(8,128)(2,1)S(1)}, u32[]{:S(2)}, u32[]{:S(2)}) collective-permute-start(bf16[4,8,1056]{2,1,0:T(8,128)(2,1)S(1)} %get-tuple-element.16), channel_id=1, source_target_pairs={{32,0},{64,32},{96,64},{128,96},{160,128},{192,160},{224,192},{33,... | collective-permute-start | bytes 202760 | tf_op jit(solution)/shard_map/ppermute | solution.py:63
  7.2 4.2 %copy-start.1 = (bf16[4,16,16]{2,1,0:T(8,128)(2,1)S(1)}, bf16[4,16,16]{2,1,0:T(8,128)(2,1)}, u32[]{:S(2)}) copy-start(bf16[4,16,16]{2,1,0:T(8,128)(2,1)} %vis_ref.3) | copy-start | bytes 6148
  11.6 8.0 %collective-permute-start.2 = (bf16[136,512]{1,0:T(8,128)(2,1)S(1)}, bf16[136,512]{1,0:T(8,128)(2,1)S(1)}, u32[]{:S(2)}, u32[]{:S(2)}) collective-permute-start(bf16[136,512]{1,0:T(8,128)(2,1)S(1)} %get-tuple-element.18), channel_id=1, source_target_pairs={{0,1},{1,2},{2,3},{3,4},{4,5},{5,6},{6,7},{7,8},{8,9},{9,10},{10,1... | collective-permute-start | bytes 417800 | tf_op jit(solution)/shard_map/ppermute | solution.py:62
  15.1 6.9 %collective-permute-start.3 = (bf16[136,512]{1,0:T(8,128)(2,1)S(1)}, bf16[136,512]{1,0:T(8,128)(2,1)S(1)}, u32[]{:S(2)}, u32[]{:S(2)}) collective-permute-start(bf16[136,512]{1,0:T(8,128)(2,1)S(1)} %get-tuple-element.19), channel_id=1, source_target_pairs={{1,0},{2,1},{3,2},{4,3},{5,4},{6,5},{7,6},{8,7},{9,8},{10,9},{11,1... | collective-permute-start | bytes 417800 | tf_op jit(solution)/shard_map/ppermute | solution.py:63
  18.6 0.7 copy-start.3

commit v7 on v6

--- a/solution.py
+++ b/solution.py
@@ -7,9 +7,9 @@
 from jax.sharding import PartitionSpec as P
 
 ROW = ("row_0", "row_1")
-COL = ("col_0", "col_1", "col_2", "col_3")
+COL = ("col_0", "col_4", "col_1", "col_2", "col_3")
 LANES = 128
-GROUPS = (("img", "row_1"), ("row_0", "col_0"), ("col_3", "col_2", "col_1"))
+GROUPS = (("img", "row_1"), ("row_0", "col_4", "col_0"), ("col_3", "col_2", "col_1"))
 INTERPRET = False
 SMALL = 0.0625
 GRANT = 8 << 20
@@ -221,7 +221,9 @@
             a = col_ref[...].astype(bf16)
             for v in range(chunks):
                 at = slice(v * LANES, (v + 1) * LANES)
-                act = jnp.dot(a, w_ref[:, at], preferred_element_type=f32) + bias_ref[...]
+                if v % 2 == 0:
+                    pair = jnp.dot(a, w_ref[:, v * LANES : (v + 2) * LANES], preferred_element_type=f32)
+                act = pair[:, v % 2 * LANES : (v % 2 + 1) * LANES] + bias_ref[...]
                 lift = jnp.exp(act)
                 first, second = lift[:half], lift[half:]
                 inner = v >= edge if block == 0 else v < edge
@@ -304,7 +306,9 @@
         a2_ref[rows:, :] = -a
         for v in range(chunks):
             at = slice(v * LANES, (v + 1) * LANES)
-            act = jnp.dot(a, w_ref[:, at], preferred_element_type=f32) + bias_ref[...]
+            if v % 2 == 0:
+                pair = jnp.dot(a, w_ref[:, v * LANES : (v + 2) * LANES], preferred_element_type=f32)
+            act = pair[:, v % 2 * LANES : (v % 2 + 1) * LANES] + bias_ref[...]
             lift = jnp.exp(act)
             probs = odds(lift[:mine], lift[mine:])
             for odd in range(2):
@@ -444,7 +448,7 @@
 
 def solution(mesh):
     split = Mesh(
-        mesh.devices.reshape(mesh.shape["img"], 2, 4, 4, 2, 2, 2),
+        mesh.devices.reshape(mesh.shape["img"], 2, 4, 2, 2, 2, 2, 2),
         ("img",) + ROW + COL,
     )
     placed = (P("img", ROW, COL), P(), P(), P(), P("img", ROW, COL))

time: 69.8 us -> 69.9 us (level)
  the two profiles are of different devices: /device:TPU:8 before, /device:TPU:2 now
where the time goes in v7:
time: 69.9 us; the launch traced here: 69.5 us
  blocking collectives  44.1 us (63%)
  starting transfers between devices  12.6 us (18%)
  waiting for transfers between devices  5.73 us (8%)
  Pallas kernels  4.81 us (7%)
  between operations  1.46 us (2%)
    all_to_all x3, blocking collectives, body(): parts = lax.all_to_all(pack, axes, 0, 0, tiled=True)  44.1 us
    ppermute x2, starting transfers between devices, edges(): lax.ppermute(head, axis, [((i + 1) % count, i) for i in range(ends)])  6.97 us
    ppermute x2, starting transfers between devices, edges(): lax.ppermute(tail, axis, [(i, (i + 1) % count) for i in range(ends)])  5.62 us
    ppermute x2, waiting for transfers between devices, edges(): lax.ppermute(head, axis, [((i + 1) % count, i) for i in range(ends)])  5.49 us
    pallas_call x8, Pallas kernels, run(): pl.pallas_call(kernel, out_shape=out_shape, in_specs=specs, out_specs=tup...  4.81 us
  transfers between devices with their start and end apart: 4, of which 3 were waited for; matrix products, arithmetic and copies ran while one was open for 0% of the time, Pallas kernels for 0%

profile of v7, /device:TPU:2, one launch (start us, length us, event | category | flops | bytes accessed | tf_op | source)
XLA Modules:
  0.0 69.5 jit_solution(7228513671085869068)
XLA Ops:
  0.6 0.0 copy-start.2
  0.6 0.9 %pack.1 = (bf16[4,8,1056]{2,1,0:T(8,128)(2,1)S(1)}, bf16[4,8,1056]{2,1,0:T(8,128)(2,1)S(1)}) custom-call(bf16[4,16,16]{2,1,0:T(8,128)(2,1)} %vis_ref.3, bf16[4,16,1024]{2,1,0:T(8,128)(2,1)} %noise_ref.3), custom_call_target="tpu_custom_call" | custom-call | tf_op jit(solution)/shard_map/pack/pallas_call | solution.py:26
  1.6 0.0 copy-start
  1.6 3.5 %collective-permute-start = (bf16[4,8,1056]{2,1,0:T(8,128)(2,1)S(1)}, bf16[4,8,1056]{2,1,0:T(8,128)(2,1)S(1)}, u32[]{:S(2)}, u32[]{:S(2)}) collective-permute-start(bf16[4,8,1056]{2,1,0:T(8,128)(2,1)S(1)} %get-tuple-element.15), channel_id=1, source_target_pairs={{0,32},{32,64},{64,96},{96,128},{128,160},{160,192},{192,224},{1,3... | collective-permute-start | bytes 202760 | tf_op jit(solution)/shard_map/ppermute | solution.py:62
  5.1 5.7 %collective-permute-start.1 = (bf16[4,8,1056]{2,1,0:T(8,128)(2,1)S(1)}, bf16[4,8,1056]{2,1,0:T(8,128)(2,1)S(1)}, u32[]{:S(2)}, u32[]{:S(2)}) collective-permute-start(bf16[4,8,1056]{2,1,0:T(8,128)(2,1)S(1)} %get-tuple-element.16), channel_id=1, source_target_pairs={{32,0},{64,32},{96,64},{128,96},{160,128},{192,160},{224,192},{33,... | collective-permute-start | bytes 202760 | tf_op jit(solution)/shard_map/ppermute | solution.py:63
  11.5 0.0 copy-done.2
  11.6 0.0 copy-start.1
  11.6 0.1 select_select_fusion.flag_ref
  11.7 0.0 collective-permute-done.before_ref
  11.7 1.1 %collective-permute-done.1.after_ref = bf16[4,8,1056]{2,1,0:T(8,128)(2,1)S(1)} collective-permute-done((bf16[4,8,1056]{2,1,0:T(8,128)(2,1)S(1)}, bf16[4,8,1056]{2,1,0:T(8,128)(2,1)S(1)}, u32[]{:S(2)}, u32[]{:S(2)}) %collective-permute-start.1) | collective-permute-done | bytes 67616 | tf_op jit(solution)/shard_map/ppermute | solution.py:63
  12.8 0.0 copy-done
  12.8 0.0 copy-done.1
  12.8 0.2 mid.1
  13.0 2.1 %collective-permute-start.2 = (bf16[136,512]{1,0:T(8,128)(2,1)S(1)}, bf16[136,512]{1,0:T(8,128)(2,1)S(1)}, u32[]{:S(2)}, u32[]{:S(2)}) collective-permute-start(bf16[136,512]{1,0:T(8,128)(2,1)S(1)} %get-tuple-element.18), channel_id=1, source_target_pairs={{0,1},{1,2},{2,3},{3,4},{4,5},{5,6},{6,7},{7,8},{8,9},{9,10},{10,1... | collective-permute-start | bytes 417800 | tf_op jit(solution)/shard_map/ppermute | solution.py:62
  15.1 1.3 %collective-permute-start.3 = (bf16[136,512]{1,0:T(8,128)(2,1)S(1)}, bf16[136,512]{1,0:T(8,128)(2,1)S(1)}, u32[]{:S(2)}, u32[]{:S(2)}) collective-permute-start(bf16[136,512]{1,0:T(8,128)(2,1)S(1)} %get-tuple-element.19), channel_id=1, source_target_pairs={{1,0},{2,1},{3,2},{4,3},{5,4},{6,5},{7,6},{8,7},{9,8},{10,9},{11,1... | collective-permute-start | bytes 417800 | tf_op jit(solution)/shard_map/ppermute | solution.py:63
  16.4 0.1 select_maximum_fusion.pair_ref
  16.4 0.0 copy-start.3
  16.5 0.1 band.1.w_ref
  16.6 0.5 copy-done.3
  17.1 0.1 maximum_bitcast_fusion.bias_ref
  17.2 0.2 draw.1.t_ref
  17.4 0.2 collective-permute-done.2.before_ref
  17.6 4.4 %collective-permute-done.3.after_ref = bf16[136,512]{1,0:T(8,128)(2,1)S(1)} collective-permute-done((bf16[136,512]{1,0:T(8,128)(2,1)S(1)}, bf16[136,512]{1,0:T(8,128)(2,1)S(1)}, u32[]{:S(2)}, u32[]{:S(2)}) %collective-permute-start.3) | collective-permute-done | bytes 139296 | tf_op jit(solution)/shard_map/ppermute | solution.py:63
  22.0 2.6 %main.1 = (bf16[4,16,16]{2,1,0:T(8,128)(2,1)S(1)}, bf16[8,48,128]{2,1,0:T(8,128)(2,1)S(1)}) custom-call(f32[8,128]{1,0:T(8,128)S(1)} %select_select_fusion.flag_ref, f32[4,40,16]{2,1,0:T(8,128)S(1)} %get-tuple-element.17.column_ref, bf16[136,512]{1,0:T(8,128)(2,1)S(1)} %collective-permute-done.2.before_ref, ...), custom_call_target="tpu_custom_call" | custom-call | tf_op jit(solution)/shard_map/main/pallas_call | solution.py:26
  24.6 11.5 %all_to_all.15.parts_ref = bf16[8,48,128]{2,1,0:T(8,128)(2,1)S(1)} all-to-all(bf16[8,48,128]{2,1,0:T(8,128)(2,1)S(1)} %get-tuple-element.20), channel_id=1, replica_groups=mesh['img'=2,'row_0'=2,'row_1'=4,'col_0'=2,'col_4'=2,'col_1'=2,'col_2'=2..., dimensions={0} | all-to-all | bytes 196608 | tf_op jit(solution)/shard_map/all_to_all | solution.py:430
  36.1 19.4 %all_to_all.16.parts_ref = bf16[8,48,128]{2,1,0:T(8,128)(2,1)S(1)} all-to-all(bf16[8,48,128]{2,1,0:T(8,128)(2,1)S(1)} %spread.2), channel_id=1, replica_groups=mesh['img'=2,'row_0'=2,'row_1'=4,'col_0'=2,'col_4'=2,'col_1'=2,'col_2'=2..., dimensions={0} | all-to-all | bytes 196608 | tf_op jit(solution)/shard_map/all_to_all | solution.py:430
  55.5 13.2 %all_to_all.17.parts_ref = bf16[8,48,128]{2,1,0:T(8,128)(2,1)S(1)} all-to-all(bf16[8,48,128]{2,1,0:T(8,128)(2,1)S(1)} %spread.3), channel_id=1, replica_groups=mesh['img'=2,'row_0'=2,'row_1'=4,'col_0'=2,'col_4'=2,'col_1'=2,'col_2'=2..., dimensions={0} | all-to-all | bytes 196608 | tf_op jit(solution)/shard_map/all_to_all | solution.py:430
  68.7 0.7 %finish.1 = (bf16[4,16,16]{2,1,0:T(8,128)(2,1)}, f32[9,9,64]{2,1,0:T(8,128)}, f32[1,64]{1,0:T(1,128)}, f32[1,1]{1,0:T(1,128)}) custom-call(bf16[8,48,128]{2,1,0:T(8,128)(2,1)S(1)} %all_to_all.17.parts_ref, bf16[4,16,16]{2,1,0:T(8,128)(2,1)S(1)} %get-tuple-element.21.recon_in_ref), custom_call_target="tpu_custom_call" | custom-call | tf_op jit(solution)/shard_map/finish/pallas_call | solution.py:26
  (6 shorter events, 0.1 us)
Async XLA Ops:
  0.6 10.9 %copy-start.2 = (bf16[64,9,9]{0,2,1:T(8,128)(2,1)S(1)}, bf16[64,9,9]{0,2,1:T(8,128)(2,1)}, u32[]{:S(2)}) copy-start(bf16[64,9,9]{0,2,1:T(8,128)(2,1)} %param.6) | copy-start | bytes 31108
  1.6 11.2 %copy-start = (bf16[4,16,1024]{2,1,0:T(8,128)(2,1)S(1)}, bf16[4,16,1024]{2,1,0:T(8,128)(2,1)}, u32[]{:S(2)}) copy-start(bf16[4,16,1024]{2,1,0:T(8,128)(2,1)} %noise_ref.3) | copy-start | bytes 393220
  1.6 10.1 %collective-permute-start = (bf16[4,8,1056]{2,1,0:T(8,128)(2,1)S(1)}, bf16[4,8,1056]{2,1,0:T(8,128)(2,1)S(1)}, u32[]{:S(2)}, u32[]{:S(2)}) collective-permute-start(bf16[4,8,1056]{2,1,0:T(8,128)(2,1)S(1)} %get-tuple-element.15), channel_id=1, source_target_pairs={{0,32},{32,64},{64,96},{96,128},{128,160},{160,192},{192,224},{1,3... | collective-permute-start | bytes 202760 | tf_op jit(solution)/shard_map/ppermute | solution.py:62
  5.1 7.7 %collective-permute-start.1 = (bf16[4,8,1056]{2,1,0:T(8,128)(2,1)S(1)}, bf16[4,8,1056]{2,1,0:T(8,128)(2,1)S(1)}, u32[]{:S(2)}, u32[]{:S(2)}) collective-permute-start(bf16[4,8,1056]{2,1,0:T(8,128)(2,1)S(1)} %get-tuple-element.16), channel_id=1, source_target_pairs={{32,0},{64,32},{96,64},{128,96},{160,128},{192,160},{224,192},{33,... | collective-permute-start | bytes 202760 | tf_op jit(solution)/shard_map/ppermute | solution.py:63
  11.6 1.2 %copy-start.1 = (bf16[4,16,16]{2,1,0:T(8,128)(2,1)S(1)}, bf16[4,16,16]{2,1,0:T(8,128)(2,1)}, u32[]{:S(2)}) copy-start(bf16[4,16,16]{2,1,0:T(8,128)(2,1)} %vis_ref.3) | copy-start | bytes 6148
  13.0 4.7 %collective-permute-start.2 = (bf16[136,512]{1,0:T(8,128)(2,1)S(1)}, bf16[136,512]{1,0:T(8,128)(2,1)S(1)}, u32[]{:S(2)}, u32[]{:S(2)}) collective-permute-start(bf16[136,512]{1,0:T(8,128)(2,1)S(1)} %get-tuple-element.18), channel_id=1, source_target_pairs={{0,1},{1,2},{2,3},{3,4},{4,5},{5,6},{6,7},{7,8},{8,9},{9,10},{10,1... | collective-permute-start | bytes 417800 | tf_op jit(solution)/shard_map/ppermute | solution.py:62
  15.1 6.9 %collective-permute-start.3 = (bf16[136,512]{1,0:T(8,128)(2,1)S(1)}, bf16[136,512]{1,0:T(8,128)(2,1)S(1)}, u32[]{:S(2)}, u32[]{:S(2)}) collective-permute-start(bf16[136,512]{1,0:T(8,128)(2,1)S(1)} %get-tuple-element.19), channel_id=1, source_target_pairs={{1,0},{2,1},{3,2},{4,3},{5,4},{6,5},{7,6},{8,7},{9,8},{10,9},{11,1... | collective-permute-start | bytes 417800 | tf_op jit(solution)/shard_map/ppermute | solution.py:63
  16.4 0.7 copy-start.3

commit v8 on v7

--- a/solution.py
+++ b/solution.py
@@ -58,10 +58,8 @@
 def edges(axis, tail, head):
     count = lax.axis_size(axis)
     ends = count - 1
-    return (
-        lax.ppermute(tail, axis, [(i, (i + 1) % count) for i in range(ends)]),
-        lax.ppermute(head, axis, [((i + 1) % count, i) for i in range(ends)]),
-    )
+    after = lax.ppermute(head, axis, [((i + 1) % count, i) for i in range(ends)])
+    return lax.ppermute(tail, axis, [(i, (i + 1) % count) for i in range(ends)]), after
 
 
 def body(images, filters, hidden_bias, visible_unit_bias, unit_noise):

time: 69.9 us -> 69.9 us (level)
  no operation moved by 1% of the time
where the time goes in v8:
time: 69.9 us; the launch traced here: 69.5 us
  blocking collectives  44.1 us (63%)
  starting transfers between devices  12.6 us (18%)
  waiting for transfers between devices  5.73 us (8%)
  Pallas kernels  4.81 us (7%)
  between operations  1.46 us (2%)
    all_to_all x3, blocking collectives, body(): parts = lax.all_to_all(pack, axes, 0, 0, tiled=True)  44.1 us
    ppermute x2, starting transfers between devices, edges(): lax.ppermute(head, axis, [((i + 1) % count, i) for i in range(ends)])  6.97 us
    ppermute x2, starting transfers between devices, edges(): lax.ppermute(tail, axis, [(i, (i + 1) % count) for i in range(ends)])  5.62 us
    ppermute x2, waiting for transfers between devices, edges(): lax.ppermute(head, axis, [((i + 1) % count, i) for i in range(ends)])  5.49 us
    pallas_call x8, Pallas kernels, run(): pl.pallas_call(kernel, out_shape=out_shape, in_specs=specs, out_specs=tup...  4.81 us
  transfers between devices with their start and end apart: 4, of which 3 were waited for; matrix products, arithmetic and copies ran while one was open for 0% of the time, Pallas kernels for 0%

profile of v8, /device:TPU:2, one launch (start us, length us, event | category | flops | bytes accessed | tf_op | source)
XLA Modules:
  0.0 69.5 jit_solution(7228513671085869068)
XLA Ops:
  0.6 0.0 copy-start.2
  0.6 0.9 %pack.1 = (bf16[4,8,1056]{2,1,0:T(8,128)(2,1)S(1)}, bf16[4,8,1056]{2,1,0:T(8,128)(2,1)S(1)}) custom-call(bf16[4,16,16]{2,1,0:T(8,128)(2,1)} %vis_ref.3, bf16[4,16,1024]{2,1,0:T(8,128)(2,1)} %noise_ref.3), custom_call_target="tpu_custom_call" | custom-call | tf_op jit(solution)/shard_map/pack/pallas_call | solution.py:26
  1.6 0.0 copy-start
  1.6 3.5 %collective-permute-start = (bf16[4,8,1056]{2,1,0:T(8,128)(2,1)S(1)}, bf16[4,8,1056]{2,1,0:T(8,128)(2,1)S(1)}, u32[]{:S(2)}, u32[]{:S(2)}) collective-permute-start(bf16[4,8,1056]{2,1,0:T(8,128)(2,1)S(1)} %get-tuple-element.15), channel_id=1, source_target_pairs={{0,32},{32,64},{64,96},{96,128},{128,160},{160,192},{192,224},{1,3... | collective-permute-start | bytes 202760 | tf_op jit(solution)/shard_map/ppermute | solution.py:62
  5.1 5.7 %collective-permute-start.1 = (bf16[4,8,1056]{2,1,0:T(8,128)(2,1)S(1)}, bf16[4,8,1056]{2,1,0:T(8,128)(2,1)S(1)}, u32[]{:S(2)}, u32[]{:S(2)}) collective-permute-start(bf16[4,8,1056]{2,1,0:T(8,128)(2,1)S(1)} %get-tuple-element.16), channel_id=1, source_target_pairs={{32,0},{64,32},{96,64},{128,96},{160,128},{192,160},{224,192},{33,... | collective-permute-start | bytes 202760 | tf_op jit(solution)/shard_map/ppermute | solution.py:61
  11.5 0.0 copy-done.2
  11.6 0.0 copy-start.1
  11.6 0.1 select_select_fusion.flag_ref
  11.7 0.0 collective-permute-done.before_ref
  11.7 1.1 %collective-permute-done.1.after_ref = bf16[4,8,1056]{2,1,0:T(8,128)(2,1)S(1)} collective-permute-done((bf16[4,8,1056]{2,1,0:T(8,128)(2,1)S(1)}, bf16[4,8,1056]{2,1,0:T(8,128)(2,1)S(1)}, u32[]{:S(2)}, u32[]{:S(2)}) %collective-permute-start.1) | collective-permute-done | bytes 67616 | tf_op jit(solution)/shard_map/ppermute | solution.py:61
  12.8 0.0 copy-done
  12.8 0.0 copy-done.1
  12.8 0.2 mid.1
  13.0 2.1 %collective-permute-start.2 = (bf16[136,512]{1,0:T(8,128)(2,1)S(1)}, bf16[136,512]{1,0:T(8,128)(2,1)S(1)}, u32[]{:S(2)}, u32[]{:S(2)}) collective-permute-start(bf16[136,512]{1,0:T(8,128)(2,1)S(1)} %get-tuple-element.18), channel_id=1, source_target_pairs={{0,1},{1,2},{2,3},{3,4},{4,5},{5,6},{6,7},{7,8},{8,9},{9,10},{10,1... | collective-permute-start | bytes 417800 | tf_op jit(solution)/shard_map/ppermute | solution.py:62
  15.1 1.3 %collective-permute-start.3 = (bf16[136,512]{1,0:T(8,128)(2,1)S(1)}, bf16[136,512]{1,0:T(8,128)(2,1)S(1)}, u32[]{:S(2)}, u32[]{:S(2)}) collective-permute-start(bf16[136,512]{1,0:T(8,128)(2,1)S(1)} %get-tuple-element.19), channel_id=1, source_target_pairs={{1,0},{2,1},{3,2},{4,3},{5,4},{6,5},{7,6},{8,7},{9,8},{10,9},{11,1... | collective-permute-start | bytes 417800 | tf_op jit(solution)/shard_map/ppermute | solution.py:61
  16.4 0.1 select_maximum_fusion.pair_ref
  16.4 0.0 copy-start.3
  16.5 0.1 band.1.w_ref
  16.6 0.5 copy-done.3
  17.1 0.1 maximum_bitcast_fusion.bias_ref
  17.2 0.2 draw.1.t_ref
  17.4 0.2 collective-permute-done.2.before_ref
  17.6 4.4 %collective-permute-done.3.after_ref = bf16[136,512]{1,0:T(8,128)(2,1)S(1)} collective-permute-done((bf16[136,512]{1,0:T(8,128)(2,1)S(1)}, bf16[136,512]{1,0:T(8,128)(2,1)S(1)}, u32[]{:S(2)}, u32[]{:S(2)}) %collective-permute-start.3) | collective-permute-done | bytes 139296 | tf_op jit(solution)/shard_map/ppermute | solution.py:61
  22.0 2.6 %main.1 = (bf16[4,16,16]{2,1,0:T(8,128)(2,1)S(1)}, bf16[8,48,128]{2,1,0:T(8,128)(2,1)S(1)}) custom-call(f32[8,128]{1,0:T(8,128)S(1)} %select_select_fusion.flag_ref, f32[4,40,16]{2,1,0:T(8,128)S(1)} %get-tuple-element.17.column_ref, bf16[136,512]{1,0:T(8,128)(2,1)S(1)} %collective-permute-done.2.before_ref, ...), custom_call_target="tpu_custom_call" | custom-call | tf_op jit(solution)/shard_map/main/pallas_call | solution.py:26
  24.6 11.5 %all_to_all.15.parts_ref = bf16[8,48,128]{2,1,0:T(8,128)(2,1)S(1)} all-to-all(bf16[8,48,128]{2,1,0:T(8,128)(2,1)S(1)} %get-tuple-element.20), channel_id=1, replica_groups=mesh['img'=2,'row_0'=2,'row_1'=4,'col_0'=2,'col_4'=2,'col_1'=2,'col_2'=2..., dimensions={0} | all-to-all | bytes 196608 | tf_op jit(solution)/shard_map/all_to_all | solution.py:428
  36.1 19.4 %all_to_all.16.parts_ref = bf16[8,48,128]{2,1,0:T(8,128)(2,1)S(1)} all-to-all(bf16[8,48,128]{2,1,0:T(8,128)(2,1)S(1)} %spread.2), channel_id=1, replica_groups=mesh['img'=2,'row_0'=2,'row_1'=4,'col_0'=2,'col_4'=2,'col_1'=2,'col_2'=2..., dimensions={0} | all-to-all | bytes 196608 | tf_op jit(solution)/shard_map/all_to_all | solution.py:428
  55.5 13.2 %all_to_all.17.parts_ref = bf16[8,48,128]{2,1,0:T(8,128)(2,1)S(1)} all-to-all(bf16[8,48,128]{2,1,0:T(8,128)(2,1)S(1)} %spread.3), channel_id=1, replica_groups=mesh['img'=2,'row_0'=2,'row_1'=4,'col_0'=2,'col_4'=2,'col_1'=2,'col_2'=2..., dimensions={0} | all-to-all | bytes 196608 | tf_op jit(solution)/shard_map/all_to_all | solution.py:428
  68.7 0.7 %finish.1 = (bf16[4,16,16]{2,1,0:T(8,128)(2,1)}, f32[9,9,64]{2,1,0:T(8,128)}, f32[1,64]{1,0:T(1,128)}, f32[1,1]{1,0:T(1,128)}) custom-call(bf16[8,48,128]{2,1,0:T(8,128)(2,1)S(1)} %all_to_all.17.parts_ref, bf16[4,16,16]{2,1,0:T(8,128)(2,1)S(1)} %get-tuple-element.21.recon_in_ref), custom_call_target="tpu_custom_call" | custom-call | tf_op jit(solution)/shard_map/finish/pallas_call | solution.py:26
  (6 shorter events, 0.1 us)
Async XLA Ops:
  0.6 10.9 %copy-start.2 = (bf16[64,9,9]{0,2,1:T(8,128)(2,1)S(1)}, bf16[64,9,9]{0,2,1:T(8,128)(2,1)}, u32[]{:S(2)}) copy-start(bf16[64,9,9]{0,2,1:T(8,128)(2,1)} %param.6) | copy-start | bytes 31108
  1.6 11.2 %copy-start = (bf16[4,16,1024]{2,1,0:T(8,128)(2,1)S(1)}, bf16[4,16,1024]{2,1,0:T(8,128)(2,1)}, u32[]{:S(2)}) copy-start(bf16[4,16,1024]{2,1,0:T(8,128)(2,1)} %noise_ref.3) | copy-start | bytes 393220
  1.6 10.1 %collective-permute-start = (bf16[4,8,1056]{2,1,0:T(8,128)(2,1)S(1)}, bf16[4,8,1056]{2,1,0:T(8,128)(2,1)S(1)}, u32[]{:S(2)}, u32[]{:S(2)}) collective-permute-start(bf16[4,8,1056]{2,1,0:T(8,128)(2,1)S(1)} %get-tuple-element.15), channel_id=1, source_target_pairs={{0,32},{32,64},{64,96},{96,128},{128,160},{160,192},{192,224},{1,3... | collective-permute-start | bytes 202760 | tf_op jit(solution)/shard_map/ppermute | solution.py:62
  5.1 7.7 %collective-permute-start.1 = (bf16[4,8,1056]{2,1,0:T(8,128)(2,1)S(1)}, bf16[4,8,1056]{2,1,0:T(8,128)(2,1)S(1)}, u32[]{:S(2)}, u32[]{:S(2)}) collective-permute-start(bf16[4,8,1056]{2,1,0:T(8,128)(2,1)S(1)} %get-tuple-element.16), channel_id=1, source_target_pairs={{32,0},{64,32},{96,64},{128,96},{160,128},{192,160},{224,192},{33,... | collective-permute-start | bytes 202760 | tf_op jit(solution)/shard_map/ppermute | solution.py:61
  11.6 1.2 %copy-start.1 = (bf16[4,16,16]{2,1,0:T(8,128)(2,1)S(1)}, bf16[4,16,16]{2,1,0:T(8,128)(2,1)}, u32[]{:S(2)}) copy-start(bf16[4,16,16]{2,1,0:T(8,128)(2,1)} %vis_ref.3) | copy-start | bytes 6148
  13.0 4.7 %collective-permute-start.2 = (bf16[136,512]{1,0:T(8,128)(2,1)S(1)}, bf16[136,512]{1,0:T(8,128)(2,1)S(1)}, u32[]{:S(2)}, u32[]{:S(2)}) collective-permute-start(bf16[136,512]{1,0:T(8,128)(2,1)S(1)} %get-tuple-element.18), channel_id=1, source_target_pairs={{0,1},{1,2},{2,3},{3,4},{4,5},{5,6},{6,7},{7,8},{8,9},{9,10},{10,1... | collective-permute-start | bytes 417800 | tf_op jit(solution)/shard_map/ppermute | solution.py:62
  15.1 6.9 %collective-permute-start.3 = (bf16[136,512]{1,0:T(8,128)(2,1)S(1)}, bf16[136,512]{1,0:T(8,128)(2,1)S(1)}, u32[]{:S(2)}, u32[]{:S(2)}) collective-permute-start(bf16[136,512]{1,0:T(8,128)(2,1)S(1)} %get-tuple-element.19), channel_id=1, source_target_pairs={{1,0},{2,1},{3,2},{4,3},{5,4},{6,5},{7,6},{8,7},{9,8},{10,9},{11,1... | collective-permute-start | bytes 417800 | tf_op jit(solution)/shard_map/ppermute | solution.py:61
  16.4 0.7 copy-start.3
